TPU v7x, 512 devices: a whole 4x8x8 slice. The times are simulated.
512 devices in a mesh: occ: 128 (over z_hi, x, y), aux: 4 (over z_lo, core).
Axes of the slice: x: 4, y: 8, z: 8 (z_hi: 4, z_lo: 2; z = z_hi * 2 + z_lo), core: 2. Of those that a mesh axis runs over, the one named last changes fastest.
Arguments:
- factors: bfloat16 [128, 512, 2048], P('occ', None, 'aux'), may hold values from -0.8984375 to 0.8984375
- offsets: int32 [2], replicated, may hold values from 1 to 127, as said below
- occ_energy: float32 [128], replicated, may hold values from -2 to -0.5
- vir_energy: float32 [512], replicated, may hold values from 0.2 to 3
Outputs:
- gamma: float32 [128, 512, 2048], P('occ', None, 'aux')
- vir_density: float32 [512, 512], P('aux')
Inputs may be any that keep to these rules, and one draw needn't show every extreme that they name: `offsets`: distinct.
All inputs are finite; a program needn't handle non-finite values.
Results may differ from a plain program's by a relative error of at most 0.0027.
Values may be sent and summed in bfloat16 or wider, within the bound.
No kernel may reach another device: no remote copies, remote signals or barrier semaphores. Data moves between devices by JAX's collectives and lax.ppermute only.
A program may use at most 128 MiB of HBM per device.

v0:
```python
import functools

import jax
import jax.numpy as jnp
from jax import lax
from jax.experimental import pallas as pl
from jax.experimental.pallas import tpu as pltpu
from jax.sharding import Mesh
from jax.sharding import PartitionSpec as P

OCC = ("zh", "x", "y")
REST = ("zh", "x", "zl")
SUB = 16
LANES = 128
VMEM = pl.BlockSpec(memory_space=pltpu.VMEM)
SMEM = pl.BlockSpec(memory_space=pltpu.SMEM)
ANY = pl.BlockSpec(memory_space=pl.ANY)
SMALL = pltpu.CompilerParams(vmem_limit_bytes=16 << 20)


def near(value):
    return pltpu.with_memory_space_constraint(value, pltpu.VMEM)


def far(value):
    return pltpu.with_memory_space_constraint(value, pltpu.HBM)


def exchange(value, axis):
    return lax.all_to_all(value, axis, split_axis=0, concat_axis=0, tiled=True)


def swap(value, axis):
    return lax.ppermute(value, axis, [(0, 1), (1, 0)])


def inner(left, right):
    return lax.dot_general(
        left, right, (((1,), (1,)), ((), ())), preferred_element_type=jnp.float32
    )


def to_pieces(block):
    tall, wide = block.shape
    tiles = block.reshape(tall // SUB, SUB, wide // LANES, LANES)
    return tiles.transpose(0, 2, 1, 3).reshape(-1, SUB, LANES)


def roll_kernel(starts_ref, held_ref, out_ref, twice_ref, sems):
    count = held_ref.shape[0]
    twice_ref[:count] = held_ref[...]
    twice_ref[count:] = held_ref[...]
    copies = []
    for k in range(starts_ref.shape[0]):
        copies.append(
            pltpu.make_async_copy(
                twice_ref.at[pl.ds(starts_ref[k], count)],
                out_ref.at[:, pl.ds(k * SUB, SUB), :],
                sems.at[k],
            )
        )
        copies[-1].start()
    for copy in copies:
        copy.wait()


def rolled(starts, held):
    count, sub, lanes = held.shape
    total = starts.shape[0]
    return pl.pallas_call(
        roll_kernel,
        out_shape=pltpu.HBM((count, total * sub, lanes), held.dtype),
        in_specs=[SMEM, VMEM],
        out_specs=ANY,
        compiler_params=SMALL,
        scratch_shapes=[
            pltpu.VMEM((2 * count, sub, lanes), held.dtype),
            pltpu.SemaphoreType.DMA((total,)),
        ],
    )(starts, near(held))


def partial_kernel(
    group, place_ref, own_ref, got_ref, block_ref, kept_ref, sent_ref, held_ref, mine_ref,
    sems,
):
    noff, tall, wide = held_ref.shape
    half = tall // 2
    core = place_ref[1]
    for k in range(noff):
        first = (group * noff + k) * SUB
        for c in range(wide // LANES):
            tile = got_ref[:, c, first : first + SUB, :]
            held_ref[k, :, c * LANES : (c + 1) * LANES] = tile.reshape(tall, LANES)
    copies = [
        pltpu.make_async_copy(held_ref, block_ref, sems.at[0]),
        pltpu.make_async_copy(mine_ref, kept_ref, sems.at[1]),
    ]
    copies[0].start()
    mine = own_ref[pl.ds(pl.multiple_of(core * half, half), half), :]
    other = own_ref[pl.ds(pl.multiple_of((1 - core) * half, half), half), :]
    for k in range(noff):
        mine_ref[k] = inner(mine, held_ref[k])
    copies[1].start()
    for k in range(noff):
        sent_ref[k] = inner(other, held_ref[k])
    for copy in copies:
        copy.wait()


def partials(place, own, got, group):
    tall, wide = own.shape
    noff = got.shape[1] // SUB // 2
    got = got.reshape(tall // SUB, wide // LANES, 2 * noff * SUB, LANES)
    half, whole = (noff, tall // 2, tall), (noff, tall, wide)
    return pl.pallas_call(
        functools.partial(partial_kernel, group),
        out_shape=(
            pltpu.HBM(whole, own.dtype),
            pltpu.HBM(half, jnp.float32),
            jax.ShapeDtypeStruct(half, jnp.float32),
        ),
        in_specs=[SMEM, VMEM, VMEM],
        out_specs=(ANY, ANY, VMEM),
        compiler_params=SMALL,
        scratch_shapes=[
            pltpu.VMEM(whole, own.dtype),
            pltpu.VMEM(half, jnp.float32),
            pltpu.SemaphoreType.DMA((2,)),
        ],
    )(place, own, near(got))


def amplitude(place_ref, shift, occ_ref, row_ref, pair, there, amp_ref):
    me, core = place_ref[0], place_ref[1]
    half, _ = pair.shape
    energy = occ_ref[me] + occ_ref[lax.rem(me + shift, occ_ref.shape[0])]
    row = row_ref[...]
    for value, place in ((pair, core), (there, 1 - core)):
        start = pl.multiple_of(place * half, half)
        mine = row_ref[:, pl.ds(start, half)]
        column = jnp.broadcast_to(mine, (LANES, half)).T[:, :1]
        amp_ref[pl.ds(start, half), :] = value / (energy - column - row)
    return amp_ref[...]


def first_kernel(
    place_ref, shifts_ref, occ_ref, row_ref, pair_ref, there_ref,
    mixed_ref, density_ref, amp_ref, held_ref, sem,
):
    core, chip = place_ref[1], place_ref[2]
    slots, chips, depth, _ = density_ref.shape
    rows = slots * depth
    amp = amplitude(
        place_ref, shifts_ref[chip], occ_ref, row_ref, pair_ref[...], there_ref[...], amp_ref
    )
    held_ref[...] = (2.0 * amp - amp.T).astype(held_ref.dtype)
    out = pltpu.make_async_copy(held_ref, mixed_ref, sem)
    out.start()
    for s in range(chips):
        at = pl.ds(pl.multiple_of((chips * s + core) * rows, rows), rows)
        part = inner(amp_ref[at, :].astype(held_ref.dtype), held_ref[...])
        part = part.astype(density_ref.dtype)
        density_ref[:, s] = part.reshape(slots, depth, part.shape[1])
    out.wait()


def first_pair(place, shifts, occ, row, pair, there, slots):
    _, nvir = pair.shape
    return pl.pallas_call(
        first_kernel,
        out_shape=(
            pltpu.HBM((nvir, nvir), jnp.bfloat16),
            pltpu.HBM((slots, 2, nvir // 4 // slots, nvir), jnp.bfloat16),
        ),
        in_specs=[SMEM, SMEM, SMEM, VMEM, VMEM, VMEM],
        out_specs=(ANY, VMEM),
        compiler_params=SMALL,
        scratch_shapes=[
            pltpu.VMEM((nvir, nvir), jnp.float32),
            pltpu.VMEM((nvir, nvir), jnp.bfloat16),
            pltpu.SemaphoreType.DMA,
        ],
    )(place, shifts, occ, row, near(pair), near(there))


def product_kernel(place_ref, mixed_ref, block_ref, out_ref):
    block = block_ref[place_ref[2]]
    out_ref[...] = jnp.dot(mixed_ref[...], block, preferred_element_type=jnp.float32)


def product(place, mixed, block):
    return pl.pallas_call(
        product_kernel,
        out_shape=pltpu.HBM(block.shape[1:], jnp.float32),
        in_specs=[SMEM, VMEM, VMEM],
        out_specs=VMEM,
        compiler_params=SMALL,
    )(place, far(mixed), far(block))


def rest_kernel(
    place_ref, shifts_ref, occ_ref, row_ref, pair_ref, there_ref, ahead_ref, behind_ref,
    sofar_ref, gamma_ref, amp_ref, block_ref, total_ref, sems,
):
    other = 1 - place_ref[2]
    copies = [
        pltpu.make_async_copy(sofar_ref, total_ref, sems.at[0]),
        pltpu.make_async_copy(ahead_ref.at[other], block_ref.at[0], sems.at[1]),
        pltpu.make_async_copy(behind_ref, block_ref.at[pl.ds(1, 2)], sems.at[2]),
    ]
    for copy in copies:
        copy.start()
    for k in range(pair_ref.shape[0]):
        shift = shifts_ref[other if k == 0 else k + 1]
        amp = amplitude(place_ref, shift, occ_ref, row_ref, pair_ref[k], there_ref[k], amp_ref)
        mixed = (2.0 * amp - amp.T).astype(block_ref.dtype)
        if k == 0:
            copies[0].wait()
            copies[1].wait()
        if k == 1:
            copies[2].wait()
        part = jnp.dot(mixed, block_ref[k], preferred_element_type=jnp.float32)
        gamma_ref[...] = (total_ref[...] if k == 0 else gamma_ref[...]) + part


def add_rest(place, shifts, occ, row, pair, there, ahead, behind, sofar):
    npair = pair.shape[0]
    return pl.pallas_call(
        rest_kernel,
        out_shape=jax.ShapeDtypeStruct(sofar.shape, jnp.float32),
        in_specs=[SMEM, SMEM, SMEM, VMEM, VMEM, VMEM, ANY, ANY, ANY],
        out_specs=VMEM,
        compiler_params=SMALL,
        scratch_shapes=[
            pltpu.VMEM((pair.shape[2],) * 2, jnp.float32),
            pltpu.VMEM((npair, *ahead.shape[1:]), ahead.dtype),
            pltpu.VMEM(sofar.shape, jnp.float32),
            pltpu.SemaphoreType.DMA((3,)),
        ],
    )(place, shifts, occ, row, pair, there, far(ahead), far(behind), far(sofar))


def local(factors, offsets, occ_energy, vir_energy):
    count = lax.axis_size(OCC)
    chip = lax.axis_index("zl").astype(jnp.int32)
    core = lax.axis_index("core").astype(jnp.int32)
    place = jnp.stack([lax.axis_index(OCC).astype(jnp.int32), core, chip])
    own = factors[0]
    nvir = own.shape[0]
    rows = nvir // 4
    row = vir_energy[None, :]
    shifts = jnp.concatenate([offsets, count - offsets])

    held = exchange(to_pieces(own), OCC)
    outgoing = rolled(shifts, held)
    got = exchange(outgoing, OCC)

    ahead, kept, sent = partials(place, own, got, 0)
    came = swap(sent, "core")
    total = kept + came
    mine = lax.dynamic_index_in_dim(total, chip, 0, keepdims=False)
    yours = lax.dynamic_index_in_dim(total, 1 - chip, 0, keepdims=False)
    sent = yours.astype(jnp.bfloat16)
    came = swap(sent, "zl")
    pair = mine + came.astype(jnp.float32)
    there = swap(pair, "core")
    mixed, density = first_pair(
        place, shifts, occ_energy, row, pair, there, lax.axis_size("y")
    )

    behind, kept, sent = partials(place, own, got, 1)
    came = swap(sent, "core")
    back = kept + came
    sent = jnp.concatenate([mine[None], back]).astype(jnp.bfloat16)
    came = swap(sent, "zl")
    pair = jnp.concatenate([yours[None], back]) + came.astype(jnp.float32)
    there = swap(pair, "core")
    sofar = product(place, mixed, ahead)
    gamma = add_rest(place, shifts, occ_energy, row, pair, there, ahead, behind, sofar)

    ny = lax.axis_size("y")
    nrest = lax.axis_size(REST) // 2
    came = exchange(density, "y")
    summed = jnp.sum(came.astype(jnp.float32), axis=0).astype(jnp.bfloat16)
    sent = jnp.broadcast_to(summed, (nrest, *summed.shape)).reshape(
        2 * nrest, rows // ny, nvir
    )
    came = exchange(sent, REST)
    summed = jnp.sum(came.astype(jnp.float32), axis=0).astype(jnp.bfloat16)
    sent = jnp.broadcast_to(summed, (ny, *summed.shape))
    came = exchange(sent, "y")
    return (gamma[None], came.reshape(rows, nvir).astype(jnp.float32))


def solution(mesh):
    split = Mesh(
        mesh.devices.reshape(4, 4, 8, 2, 2), ("zh", "x", "y", "zl", "core")
    )
    aux = ("zl", "core")

    return jax.shard_map(
        local,
        mesh=split,
        in_specs=(P(OCC, None, aux), P(), P(), P()),
        out_specs=(P(OCC, None, aux), P(aux, None)),
        check_vma=False,
    )
```

profile of v0, /device:TPU:4, one launch (start us, length us, event | category | flops | bytes accessed | tf_op | source)
XLA Modules:
  0.0 190.5 jit_solution(12458153442142100276)
XLA Ops:
  2.7 19.9 %all-to-all-start = ((bf16[128,16,128]{2,1,0:T(8,128)(2,1)}), bf16[128,16,128]{2,1,0:T(8,128)(2,1)S(1)}, u32[]{:S(2)}, u32[]{:S(2)}) async-start(bf16[128,16,128]{2,1,0:T(8,128)(2,1)} %bitcast.6), calls=%async_computation | async-start | bytes 1048576 | tf_op jit(solution)/shard_map/all_to_all | solution.py:30
  22.7 20.4 %all-to-all-done.held_ref = bf16[128,16,128]{2,1,0:T(8,128)(2,1)S(1)} async-done(((bf16[128,16,128]{2,1,0:T(8,128)(2,1)}), bf16[128,16,128]{2,1,0:T(8,128)(2,1)S(1)}, u32[]{:S(2)}, u32[]{:S(2)}) %all-to-all-start) | async-done | bytes 524320 | tf_op jit(solution)/shard_map/all_to_all | solution.py:30
  43.1 2.1 %shard_map.59 = bf16[128,64,128]{2,1,0:T(8,128)(2,1)} custom-call(s32[4]{0:T(128)S(1)} %pad_add_fusion.1.starts_ref.shifts_ref, bf16[128,16,128]{2,1,0:T(8,128)(2,1)S(1)} %all-to-all-done.held_ref), custom_call_target="tpu_custom_call" | custom-call | tf_op jit(solution)/shard_map/pallas_call | solution.py:70
  45.2 7.9 %all-to-all-start.1 = ((bf16[128,64,128]{2,1,0:T(8,128)(2,1)}), bf16[128,64,128]{2,1,0:T(8,128)(2,1)S(1)}, u32[]{:S(2)}, u32[]{:S(2)}) async-start(bf16[128,64,128]{2,1,0:T(8,128)(2,1)} %shard_map.59), calls=%async_computation.1 | async-start | bytes 4194304 | tf_op jit(solution)/shard_map/all_to_all | solution.py:30
  53.2 51.0 %all-to-all-done.1 = bf16[128,64,128]{2,1,0:T(8,128)(2,1)S(1)} async-done(((bf16[128,64,128]{2,1,0:T(8,128)(2,1)}), bf16[128,64,128]{2,1,0:T(8,128)(2,1)S(1)}, u32[]{:S(2)}, u32[]{:S(2)}) %all-to-all-start.1) | async-done | bytes 2097184 | tf_op jit(solution)/shard_map/all_to_all | solution.py:30
  104.2 3.2 %shard_map.60 = (bf16[2,512,512]{2,1,0:T(8,128)(2,1)}, f32[2,256,512]{2,1,0:T(8,128)}, f32[2,256,512]{2,1,0:T(8,128)}) custom-call(s32[3]{0:T(128)S(1)} %pad_add_fusion.place_ref, bf16[512,512]{1,0:T(8,128)(2,1)S(1)} %bitcast.20, bf16[32,4,64,128]{3,2,1,0:T(8,128)(2,1)S(1)} %bitcast.18), custom_call_target="tpu_custom_call" | custom-call | tf_op jit(solution)/shard_map/pallas_call | solution.py:116
  107.4 1.9 %collective-permute-start = (f32[2,256,512]{2,1,0:T(8,128)}, f32[2,256,512]{2,1,0:T(8,128)}, u32[]{:S(2)}, u32[]{:S(2)}) collective-permute-start(f32[2,256,512]{2,1,0:T(8,128)} %get-tuple-element.11), channel_id=1, source_target_pairs={{0,1},{1,0},{2,3},{3,2},{4,5},{5,4},{6,7},{7,6},{8,9},{9,8},{10,11... | collective-permute-start | bytes 3145736 | tf_op jit(solution)/shard_map/ppermute | solution.py:34
  109.4 3.2 %shard_map.61 = (bf16[2,512,512]{2,1,0:T(8,128)(2,1)}, f32[2,256,512]{2,1,0:T(8,128)}, f32[2,256,512]{2,1,0:T(8,128)}) custom-call(s32[3]{0:T(128)S(1)} %pad_add_fusion.place_ref, bf16[512,512]{1,0:T(8,128)(2,1)S(1)} %bitcast.21, bf16[32,4,64,128]{3,2,1,0:T(8,128)(2,1)S(1)} %bitcast.19), custom_call_target="tpu_custom_call" | custom-call | tf_op jit(solution)/shard_map/pallas_call | solution.py:116
  112.6 2.4 %collective-permute-start.1 = (f32[2,256,512]{2,1,0:T(8,128)}, f32[2,256,512]{2,1,0:T(8,128)S(1)}, u32[]{:S(2)}, u32[]{:S(2)}) collective-permute-start(f32[2,256,512]{2,1,0:T(8,128)} %get-tuple-element.13), channel_id=1, source_target_pairs={{0,1},{1,0},{2,3},{3,2},{4,5},{5,4},{6,7},{7,6},{8,9},{9,8},{10,11... | collective-permute-start | bytes 3145736 | tf_op jit(solution)/shard_map/ppermute | solution.py:34
  115.0 1.8 add.28
  116.9 3.2 %collective-permute-start.4 = (bf16[256,512]{1,0:T(8,128)(2,1)S(1)}, bf16[256,512]{1,0:T(8,128)(2,1)S(1)}, u32[]{:S(2)}, u32[]{:S(2)}) collective-permute-start(bf16[256,512]{1,0:T(8,128)(2,1)S(1)} %get-tuple-element.18), channel_id=1, source_target_pairs={{0,2},{2,0},{1,3},{3,1},{4,6},{6,4},{5,7},{7,5},{8,10},{10,8},{9,1... | collective-permute-start | bytes 786440 | tf_op jit(solution)/shard_map/ppermute | solution.py:34
  120.6 2.6 %collective-permute-start.2 = (bf16[3,256,512]{2,1,0:T(8,128)(2,1)S(1)}, bf16[3,256,512]{2,1,0:T(8,128)(2,1)S(1)}, u32[]{:S(2)}, u32[]{:S(2)}) collective-permute-start(bf16[3,256,512]{2,1,0:T(8,128)(2,1)S(1)} %pad_maximum_fusion), channel_id=1, source_target_pairs={{0,2},{2,0},{1,3},{3,1},{4,6},{6,4},{5,7},{7,5},{8,10},{10,8},{9,1... | collective-permute-start | bytes 2359304 | tf_op jit(solution)/shard_map/ppermute | solution.py:34
  123.2 4.8 %collective-permute-done.4 = bf16[256,512]{1,0:T(8,128)(2,1)S(1)} collective-permute-done((bf16[256,512]{1,0:T(8,128)(2,1)S(1)}, bf16[256,512]{1,0:T(8,128)(2,1)S(1)}, u32[]{:S(2)}, u32[]{:S(2)}) %collective-permute-start.4) | collective-permute-done | bytes 262176 | tf_op jit(solution)/shard_map/ppermute | solution.py:34
  128.1 1.9 %collective-permute-start.5 = (f32[256,512]{1,0:T(8,128)S(1)}, f32[256,512]{1,0:T(8,128)S(1)}, u32[]{:S(2)}, u32[]{:S(2)}) collective-permute-start(f32[256,512]{1,0:T(8,128)S(1)} %bitcast_add_fusion.pair_ref), channel_id=1, source_target_pairs={{0,1},{1,0},{2,3},{3,2},{4,5},{5,4},{6,7},{7,6},{8,9},{9,8},{10,11... | collective-permute-start | bytes 1572872 | tf_op jit(solution)/shard_map/ppermute | solution.py:34
  130.0 1.9 collective-permute-done.5.there_ref
  131.9 2.7 %shard_map.62 = (bf16[512,512]{1,0:T(8,128)(2,1)}, bf16[8,2,16,512]{3,2,1,0:T(8,128)(2,1)}) custom-call(s32[3]{0:T(128)S(1)} %pad_add_fusion.place_ref, s32[4]{0:T(128)S(1)} %pad_add_fusion.1.starts_ref.shifts_ref, f32[128]{0:T(128)S(1)} %copy-done.2, f32[1,512]{1,0:T(1,128)S(1)} %bitcast.22, f32[256,512]{1,0:T(8,128)S(1)} %bitcast_add_fusion.pair_ref, ...), custom_call_target="tpu_custom_call" | custom-call | tf_op jit(solution)/shard_map/pallas_call | solution.py:170
  134.6 5.0 %all-to-all-start.2 = ((bf16[8,2,16,512]{3,2,1,0:T(8,128)(2,1)}), bf16[8,2,16,512]{3,2,1,0:T(8,128)(2,1)S(1)}, u32[]{:S(2)}, u32[]{:S(2)}) async-start(bf16[8,2,16,512]{3,2,1,0:T(8,128)(2,1)} %get-tuple-element.17), calls=%async_computation.2 | async-start | bytes 524288 | tf_op jit(solution)/shard_map/all_to_all | solution.py:30
  139.7 4.2 %collective-permute-done.2 = bf16[3,256,512]{2,1,0:T(8,128)(2,1)S(1)} collective-permute-done((bf16[3,256,512]{2,1,0:T(8,128)(2,1)S(1)}, bf16[3,256,512]{2,1,0:T(8,128)(2,1)S(1)}, u32[]{:S(2)}, u32[]{:S(2)}) %collective-permute-start.2) | collective-permute-done | bytes 786464 | tf_op jit(solution)/shard_map/ppermute | solution.py:34
  146.2 1.9 %collective-permute-start.3 = (f32[3,256,512]{2,1,0:T(8,128)S(1)}, f32[3,256,512]{2,1,0:T(8,128)S(1)}, u32[]{:S(2)}, u32[]{:S(2)}) collective-permute-start(f32[3,256,512]{2,1,0:T(8,128)S(1)} %maximum_add_fusion.pair_ref), channel_id=1, source_target_pairs={{0,1},{1,0},{2,3},{3,2},{4,5},{5,4},{6,7},{7,6},{8,9},{9,8},{10,11... | collective-permute-start | bytes 4718600 | tf_op jit(solution)/shard_map/ppermute | solution.py:34
  148.1 3.7 %all-to-all-done.2 = bf16[8,2,16,512]{3,2,1,0:T(8,128)(2,1)S(1)} async-done(((bf16[8,2,16,512]{3,2,1,0:T(8,128)(2,1)}), bf16[8,2,16,512]{3,2,1,0:T(8,128)(2,1)S(1)}, u32[]{:S(2)}, u32[]{:S(2)}) %all-to-all-start.2) | async-done | bytes 262176 | tf_op jit(solution)/shard_map/all_to_all | solution.py:30
  152.0 23.7 %all_to_all.25 = bf16[32,16,512]{2,1,0:T(8,128)(2,1)} all-to-all(bf16[32,16,512]{2,1,0:T(8,128)(2,1)S(1)} %bitcast.24), channel_id=1, replica_groups=mesh['zh'=4,'x'=4,'y'=8,'zl'=2,'core'=2] {'zh','x','zl'}, dimensions={0} | all-to-all | bytes 1048576 | tf_op jit(solution)/shard_map/all_to_all | solution.py:30
  177.4 3.4 %all-to-all-start.4 = ((bf16[8,16,512]{2,1,0:T(8,128)(2,1)}), bf16[8,16,512]{2,1,0:T(8,128)(2,1)S(1)}, u32[]{:S(2)}, u32[]{:S(2)}) async-start(bf16[8,16,512]{2,1,0:T(8,128)(2,1)} %broadcast_in_dim.17), calls=%async_computation.4 | async-start | bytes 262144 | tf_op jit(solution)/shard_map/all_to_all | solution.py:30
  180.8 2.8 %shard_map.63.sofar_ref = f32[512,512]{1,0:T(8,128)} custom-call(s32[3]{0:T(128)S(1)} %pad_add_fusion.place_ref, bf16[512,512]{1,0:T(8,128)(2,1)} %get-tuple-element.16.mixed_ref, bf16[2,512,512]{2,1,0:T(8,128)(2,1)} %get-tuple-element.14.block_ref.ahead_ref), custom_call_target="tpu_custom_call" | custom-call | tf_op jit(solution)/shard_map/pallas_call | solution.py:193
  183.6 4.6 %shard_map.64 = f32[512,512]{1,0:T(8,128)} custom-call(s32[3]{0:T(128)S(1)} %pad_add_fusion.place_ref, s32[4]{0:T(128)S(1)} %pad_add_fusion.1.starts_ref.shifts_ref, f32[128]{0:T(128)S(1)} %copy-done.2, f32[1,512]{1,0:T(1,128)S(1)} %bitcast.23, f32[3,256,512]{2,1,0:T(8,128)S(1)} %maximum_add_fusion.pair_ref, ...), custom_call_target="tpu_custom_call" | custom-call | tf_op jit(solution)/shard_map/pallas_call | solution.py:229
  (32 shorter events, 9.3 us)
Async XLA Ops:
  0.6 22.0 %copy-start.5 = (s32[2]{0:T(128)S(1)}, s32[2]{0:T(128)}, u32[]{:S(2)}) copy-start(s32[2]{0:T(128)} %param.5) | copy-start | bytes 28
  2.7 40.4 %all-to-all-start = ((bf16[128,16,128]{2,1,0:T(8,128)(2,1)}), bf16[128,16,128]{2,1,0:T(8,128)(2,1)S(1)}, u32[]{:S(2)}, u32[]{:S(2)}) async-start(bf16[128,16,128]{2,1,0:T(8,128)(2,1)} %bitcast.6), calls=%async_computation | async-start | bytes 1048576 | tf_op jit(solution)/shard_map/all_to_all | solution.py:30
  45.2 59.0 %copy-start = (bf16[1,512,512]{2,1,0:T(8,128)(2,1)S(1)}, bf16[1,512,512]{2,1,0:T(8,128)(2,1)}, u32[]{:S(2)}) copy-start(bf16[1,512,512]{2,1,0:T(8,128)(2,1)} %param.4) | copy-start | bytes 1572868
  45.2 59.0 %all-to-all-start.1 = ((bf16[128,64,128]{2,1,0:T(8,128)(2,1)}), bf16[128,64,128]{2,1,0:T(8,128)(2,1)S(1)}, u32[]{:S(2)}, u32[]{:S(2)}) async-start(bf16[128,64,128]{2,1,0:T(8,128)(2,1)} %shard_map.59), calls=%async_computation.1 | async-start | bytes 4194304 | tf_op jit(solution)/shard_map/all_to_all | solution.py:30
  107.4 7.6 %collective-permute-start = (f32[2,256,512]{2,1,0:T(8,128)}, f32[2,256,512]{2,1,0:T(8,128)}, u32[]{:S(2)}, u32[]{:S(2)}) collective-permute-start(f32[2,256,512]{2,1,0:T(8,128)} %get-tuple-element.11), channel_id=1, source_target_pairs={{0,1},{1,0},{2,3},{3,2},{4,5},{5,4},{6,7},{7,6},{8,9},{9,8},{10,11... | collective-permute-start | bytes 3145736 | tf_op jit(solution)/shard_map/ppermute | solution.py:34
  112.6 7.6 %collective-permute-start.1 = (f32[2,256,512]{2,1,0:T(8,128)}, f32[2,256,512]{2,1,0:T(8,128)S(1)}, u32[]{:S(2)}, u32[]{:S(2)}) collective-permute-start(f32[2,256,512]{2,1,0:T(8,128)} %get-tuple-element.13), channel_id=1, source_target_pairs={{0,1},{1,0},{2,3},{3,2},{4,5},{5,4},{6,7},{7,6},{8,9},{9,8},{10,11... | collective-permute-start | bytes 3145736 | tf_op jit(solution)/shard_map/ppermute | solution.py:34
  115.0 5.2 %copy-start.3 = (f32[2,256,512]{2,1,0:T(8,128)S(1)}, f32[2,256,512]{2,1,0:T(8,128)}, u32[]{:S(2)}) copy-start(f32[2,256,512]{2,1,0:T(8,128)} %get-tuple-element.12) | copy-start | bytes 3145732
  116.9 11.1 %collective-permute-start.4 = (bf16[256,512]{1,0:T(8,128)(2,1)S(1)}, bf16[256,512]{1,0:T(8,128)(2,1)S(1)}, u32[]{:S(2)}, u32[]{:S(2)}) collective-permute-start(bf16[256,512]{1,0:T(8,128)(2,1)S(1)} %get-tuple-element.18), channel_id=1, source_target_pairs={{0,2},{2,0},{1,3},{3,1},{4,6},{6,4},{5,7},{7,5},{8,10},{10,8},{9,1... | collective-permute-start | bytes 786440 | tf_op jit(solution)/shard_map/ppermute | solution.py:34
  120.5 11.4 %copy-start.1 = (f32[512]{0:T(512)S(1)}, f32[512]{0:T(512)}, u32[]{:S(2)}) copy-start(f32[512]{0:T(512)} %param.7) | copy-start | bytes 6148
  120.5 11.4 %copy-start.2 = (f32[128]{0:T(128)S(1)}, f32[128]{0:T(128)}, u32[]{:S(2)}) copy-start(f32[128]{0:T(128)} %occ_ref.3) | copy-start | bytes 1540
  120.6 23.3 %collective-permute-start.2 = (bf16[3,256,512]{2,1,0:T(8,128)(2,1)S(1)}, bf16[3,256,512]{2,1,0:T(8,128)(2,1)S(1)}, u32[]{:S(2)}, u32[]{:S(2)}) collective-permute-start(bf16[3,256,512]{2,1,0:T(8,128)(2,1)S(1)} %pad_maximum_fusion), channel_id=1, source_target_pairs={{0,2},{2,0},{1,3},{3,1},{4,6},{6,4},{5,7},{7,5},{8,10},{10,8},{9,1... | collective-permute-start | bytes 2359304 | tf_op jit(solution)/shard_map/ppermute | solution.py:34
  128.1 3.8 %collective-permute-start.5 = (f32[256,512]{1,0:T(8,128)S(1)}, f32[256,512]{1,0:T(8,128)S(1)}, u32[]{:S(2)}, u32[]{:S(2)}) collective-permute-start(f32[256,512]{1,0:T(8,128)S(1)} %bitcast_add_fusion.pair_ref), channel_id=1, source_target_pairs={{0,1},{1,0},{2,3},{3,2},{4,5},{5,4},{6,7},{7,6},{8,9},{9,8},{10,11... | collective-permute-start | bytes 1572872 | tf_op jit(solution)/shard_map/ppermute | solution.py:34
  134.6 17.2 %all-to-all-start.2 = ((bf16[8,2,16,512]{3,2,1,0:T(8,128)(2,1)}), bf16[8,2,16,512]{3,2,1,0:T(8,128)(2,1)S(1)}, u32[]{:S(2)}, u32[]{:S(2)}) async-start(bf16[8,2,16,512]{3,2,1,0:T(8,128)(2,1)} %get-tuple-element.17), calls=%async_computation.2 | async-start | bytes 524288 | tf_op jit(solution)/shard_map/all_to_all | solution.py:30
  143.9 0.9 copy-start.4
  146.2 37.4 %collective-permute-start.3 = (f32[3,256,512]{2,1,0:T(8,128)S(1)}, f32[3,256,512]{2,1,0:T(8,128)S(1)}, u32[]{:S(2)}, u32[]{:S(2)}) collective-permute-start(f32[3,256,512]{2,1,0:T(8,128)S(1)} %maximum_add_fusion.pair_ref), channel_id=1, source_target_pairs={{0,1},{1,0},{2,3},{3,2},{4,5},{5,4},{6,7},{7,6},{8,9},{9,8},{10,11... | collective-permute-start | bytes 4718600 | tf_op jit(solution)/shard_map/ppermute | solution.py:34
  177.4 12.4 %all-to-all-start.4 = ((bf16[8,16,512]{2,1,0:T(8,128)(2,1)}), bf16[8,16,512]{2,1,0:T(8,128)(2,1)S(1)}, u32[]{:S(2)}, u32[]{:S(2)}) async-start(bf16[8,16,512]{2,1,0:T(8,128)(2,1)} %broadcast_in_dim.17), calls=%async_computation.4 | async-start | bytes 262144 | tf_op jit(solution)/shard_map/all_to_all | solution.py:30
where the time goes:
time: 191 us
  waiting for transfers between devices  87.6 us (46%)
  starting transfers between devices  50.2 us (26%)
  blocking collectives  23.7 us (12%)
  Pallas kernels  18.6 us (10%)
  other arithmetic  5.78 us (3%)
  local copies, waits for them, and re-layouts  3.73 us (2%)
    all_to_all x4, waiting for transfers between devices, exchange(): return lax.all_to_all(value, axis, split_axis=0, concat_axis=0, tiled=True)  76.7 us
    all_to_all x4, starting transfers between devices, exchange(): return lax.all_to_all(value, axis, split_axis=0, concat_axis=0, tiled=True)  36.2 us
    all_to_all x1, blocking collectives, exchange(): return lax.all_to_all(value, axis, split_axis=0, concat_axis=0, tiled=True)  23.7 us
    ppermute x6, starting transfers between devices, swap(): return lax.ppermute(value, axis, [(0, 1), (1, 0)])  14 us
    ppermute x6, waiting for transfers between devices, swap(): return lax.ppermute(value, axis, [(0, 1), (1, 0)])  10.9 us
    pallas_call x2, Pallas kernels, partials(): pl.pallas_call(functools.partial(partial_kernel, group), out_shape=(pltpu...  6.44 us
    pallas_call x1, Pallas kernels, add_rest(): pl.pallas_call(rest_kernel, out_shape=jax.ShapeDtypeStruct(sofar.shape, j...  4.55 us
  transfers between devices with their start and end apart: 10, of which 7 were waited for; matrix products, arithmetic and copies ran while one was open for 3% of the time, Pallas kernels for 7%

commit v1 on v0

v1 whole, which is shorter than its diff:
```python
import jax
import jax.numpy as jnp
from jax import lax
from jax.experimental import pallas as pl
from jax.experimental.pallas import tpu as pltpu
from jax.sharding import Mesh
from jax.sharding import PartitionSpec as P

OCC = ("zh", "x", "y")
ROWS = ("zh", "x")
ROW = 8
SUB = 16
LANES = 128
VMEM = pl.BlockSpec(memory_space=pltpu.VMEM)
SMEM = pl.BlockSpec(memory_space=pltpu.SMEM)
ANY = pl.BlockSpec(memory_space=pl.ANY)
SMALL = pltpu.CompilerParams(vmem_limit_bytes=16 << 20)


def near(value):
    return pltpu.with_memory_space_constraint(value, pltpu.VMEM)


def far(value):
    return pltpu.with_memory_space_constraint(value, pltpu.HBM)


def exchange(value, axis):
    return lax.all_to_all(value, axis, split_axis=0, concat_axis=0, tiled=True)


def swap(value, axis):
    return lax.ppermute(value, axis, [(0, 1), (1, 0)])


def inner(left, right):
    return lax.dot_general(
        left, right, (((1,), (1,)), ((), ())), preferred_element_type=jnp.float32
    )


def busiest_link(shift, sizes):
    count = sizes[0] * sizes[1] * sizes[2]
    load = {}

    def split(i):
        return [i // (sizes[1] * sizes[2]), i // sizes[2] % sizes[1], i % sizes[2]]

    for i in range(count):
        at, goal = split((i + shift) % count), split(i)
        for d, hops in ((1, 1), (2, 1), (0, 2)):
            gap = (goal[d] - at[d]) % sizes[d]
            ways = [(1, gap)] if 2 * gap < sizes[d] else [(-1, sizes[d] - gap)]
            if 2 * gap == sizes[d]:
                ways = [(1, gap), (-1, gap)]
            for sign, steps in ways:
                spot = list(at)
                for _ in range(steps):
                    link = (d, sign, tuple(spot))
                    load[link] = load.get(link, 0) + (2 * hops if d == 0 else 2) // len(ways)
                    spot[d] = (spot[d] + sign) % sizes[d]
            at[d] = goal[d]
    return max(load.values())


def fetch_both_ways(block, amount, count):
    def branch(step):
        ahead = [(i, (i - step) % count) for i in range(count)]
        behind = [(i, (i + step) % count) for i in range(count)]
        return lambda v: (lax.ppermute(v, OCC, ahead), lax.ppermute(v, OCC, behind))

    return lax.switch(amount - 1, [branch(s) for s in range(1, count // 2 + 1)], block)


def to_pieces(block):
    tall, wide = block.shape
    tiles = block.reshape(tall // ROW, ROW, wide // LANES, LANES)
    return tiles.transpose(0, 2, 1, 3).reshape(-1, SUB, LANES)


def roll_kernel(starts_ref, held_ref, out_ref, twice_ref, sems):
    count = held_ref.shape[0]
    twice_ref[:count] = held_ref[...]
    twice_ref[count:] = held_ref[...]
    copies = []
    for k in range(starts_ref.shape[0]):
        copies.append(
            pltpu.make_async_copy(
                twice_ref.at[pl.ds(starts_ref[k], count)],
                out_ref.at[:, pl.ds(k * SUB, SUB), :],
                sems.at[k],
            )
        )
        copies[-1].start()
    for copy in copies:
        copy.wait()


def rolled(starts, held):
    count, sub, lanes = held.shape
    total = starts.shape[0]
    return pl.pallas_call(
        roll_kernel,
        out_shape=pltpu.HBM((count, total * sub, lanes), held.dtype),
        in_specs=[SMEM, VMEM],
        out_specs=ANY,
        compiler_params=SMALL,
        scratch_shapes=[
            pltpu.VMEM((2 * count, sub, lanes), held.dtype),
            pltpu.SemaphoreType.DMA((total,)),
        ],
    )(starts, near(held))


def pair_products(place_ref, own_ref, block_of, mine_ref, kept_ref, sent_ref, sem):
    noff, half, _ = mine_ref.shape
    core = place_ref[1]
    mine = own_ref[pl.ds(pl.multiple_of(core * half, half), half), :]
    other = own_ref[pl.ds(pl.multiple_of((1 - core) * half, half), half), :]
    for k in range(noff):
        mine_ref[k] = inner(mine, block_of(k))
    out = pltpu.make_async_copy(mine_ref, kept_ref, sem)
    out.start()
    for k in range(noff):
        sent_ref[k] = inner(other, block_of(k))
    return out


def direct_kernel(
    place_ref, own_ref, ahead_ref, behind_ref, kept_ref, sent_ref, mine_ref, sem
):
    refs = (ahead_ref, behind_ref)
    pair_products(
        place_ref, own_ref, lambda k: refs[k][...], mine_ref, kept_ref, sent_ref, sem
    ).wait()


def partials_direct(place, own, ahead, behind):
    tall, _ = own.shape
    half = (2, tall // 2, tall)
    return pl.pallas_call(
        direct_kernel,
        out_shape=(pltpu.HBM(half, jnp.float32), jax.ShapeDtypeStruct(half, jnp.float32)),
        in_specs=[SMEM, VMEM, VMEM, VMEM],
        out_specs=(ANY, VMEM),
        compiler_params=SMALL,
        scratch_shapes=[pltpu.VMEM(half, jnp.float32), pltpu.SemaphoreType.DMA],
    )(place, own, far(ahead), far(behind))


def routed_kernel(
    place_ref, own_ref, got_ref, block_ref, kept_ref, sent_ref, held_ref, mine_ref, sems
):
    noff, tall, wide = held_ref.shape
    for k in range(noff):
        for c in range(wide // LANES):
            side, at = c * ROW // SUB, k * SUB + c * ROW % SUB
            tile = got_ref[:, side, at : at + ROW, :]
            held_ref[k, :, c * LANES : (c + 1) * LANES] = tile.reshape(tall, LANES)
    out = pltpu.make_async_copy(held_ref, block_ref, sems.at[0])
    out.start()
    pair_products(
        place_ref, own_ref, lambda k: held_ref[k], mine_ref, kept_ref, sent_ref, sems.at[1]
    ).wait()
    out.wait()


def partials_routed(place, own, got):
    tall, wide = own.shape
    noff = got.shape[1] // SUB
    got = got.reshape(tall // ROW, -1, noff * SUB, LANES)
    half, whole = (noff, tall // 2, tall), (noff, tall, wide)
    return pl.pallas_call(
        routed_kernel,
        out_shape=(
            pltpu.HBM(whole, own.dtype),
            pltpu.HBM(half, jnp.float32),
            jax.ShapeDtypeStruct(half, jnp.float32),
        ),
        in_specs=[SMEM, VMEM, VMEM],
        out_specs=(ANY, ANY, VMEM),
        compiler_params=SMALL,
        scratch_shapes=[
            pltpu.VMEM(whole, own.dtype),
            pltpu.VMEM(half, jnp.float32),
            pltpu.SemaphoreType.DMA((2,)),
        ],
    )(place, own, near(got))


def amplitude(place_ref, shift, occ_ref, row_ref, pair, there, amp_ref):
    me, core = place_ref[0], place_ref[1]
    half, _ = pair.shape
    energy = occ_ref[me] + occ_ref[lax.rem(me + shift, occ_ref.shape[0])]
    row = row_ref[...]
    for value, place in ((pair, core), (there, 1 - core)):
        start = pl.multiple_of(place * half, half)
        mine = row_ref[:, pl.ds(start, half)]
        column = jnp.broadcast_to(mine, (LANES, half)).T[:, :1]
        amp_ref[pl.ds(start, half), :] = value / (energy - column - row)
    return amp_ref[...]


def density_of(place_ref, amp_ref, mixed, rows):
    section = 2 * place_ref[2] + place_ref[1]
    at = pl.ds(pl.multiple_of(section * rows, rows), rows)
    return inner(amp_ref[at, :].astype(mixed.dtype), mixed)


def early_kernel(
    place_ref, shifts_ref, occ_ref, row_ref, pair_ref, there_ref, ahead_ref, behind_ref,
    gamma_ref, density_ref, amp_ref,
):
    rows = density_ref.shape[0]
    refs = (ahead_ref, behind_ref)
    for k in range(2):
        amp = amplitude(
            place_ref, shifts_ref[k], occ_ref, row_ref, pair_ref[k], there_ref[k], amp_ref
        )
        mixed = (2.0 * amp - amp.T).astype(ahead_ref.dtype)
        part = jnp.dot(mixed, refs[k][...], preferred_element_type=jnp.float32)
        gamma_ref[...] = part if k == 0 else gamma_ref[...] + part

        @pl.when(place_ref[3] == k)
        def _():
            density_ref[...] = density_of(place_ref, amp_ref, mixed, rows)


def early_pairs(place, shifts, occ, row, pair, there, ahead, behind):
    nvir, wide = ahead.shape
    return pl.pallas_call(
        early_kernel,
        out_shape=(
            pltpu.HBM((nvir, wide), jnp.float32),
            pltpu.HBM((nvir // 4, nvir), jnp.float32),
        ),
        in_specs=[SMEM, SMEM, SMEM, VMEM, VMEM, VMEM, VMEM, VMEM],
        out_specs=(VMEM, VMEM),
        compiler_params=SMALL,
        scratch_shapes=[pltpu.VMEM((nvir, nvir), jnp.float32)],
    )(place, shifts, occ, row, pair, there, far(ahead), far(behind))


def first_kernel(
    place_ref, shifts_ref, occ_ref, row_ref, pair_ref, there_ref, sofar_ref,
    mixed_ref, density_ref, amp_ref, held_ref, sem,
):
    amp = amplitude(
        place_ref, shifts_ref[2], occ_ref, row_ref, pair_ref[...], there_ref[...], amp_ref
    )
    held_ref[...] = (2.0 * amp - amp.T).astype(held_ref.dtype)
    out = pltpu.make_async_copy(held_ref, mixed_ref, sem)
    out.start()
    part = density_of(place_ref, amp_ref, held_ref[...], density_ref.shape[0])
    density_ref[...] = (sofar_ref[...] + part).astype(density_ref.dtype)
    out.wait()


def first_pair(place, shifts, occ, row, pair, there, sofar):
    _, nvir = pair.shape
    return pl.pallas_call(
        first_kernel,
        out_shape=(
            pltpu.HBM((nvir, nvir), jnp.bfloat16),
            pltpu.HBM(sofar.shape, jnp.bfloat16),
        ),
        in_specs=[SMEM, SMEM, SMEM, VMEM, VMEM, VMEM, VMEM],
        out_specs=(ANY, VMEM),
        compiler_params=SMALL,
        scratch_shapes=[
            pltpu.VMEM((nvir, nvir), jnp.float32),
            pltpu.VMEM((nvir, nvir), jnp.bfloat16),
            pltpu.SemaphoreType.DMA,
        ],
    )(place, shifts, occ, row, near(pair), near(there), sofar)


def rest_kernel(
    place_ref, shifts_ref, occ_ref, row_ref, pair_ref, there_ref, mixed_ref, blocks_ref,
    sofar_ref, gamma_ref, amp_ref, first_ref, block_ref, total_ref, sems,
):
    copies = [
        pltpu.make_async_copy(mixed_ref, first_ref, sems.at[0]),
        pltpu.make_async_copy(blocks_ref, block_ref, sems.at[1]),
        pltpu.make_async_copy(sofar_ref, total_ref, sems.at[2]),
    ]
    for copy in copies:
        copy.start()
    amp = amplitude(
        place_ref, shifts_ref[3], occ_ref, row_ref, pair_ref[...], there_ref[...], amp_ref
    )
    mixed = (2.0 * amp - amp.T).astype(block_ref.dtype)
    for copy in copies:
        copy.wait()
    part = jnp.dot(first_ref[...], block_ref[0], preferred_element_type=jnp.float32)
    part += jnp.dot(mixed, block_ref[1], preferred_element_type=jnp.float32)
    gamma_ref[...] = total_ref[...] + part


def add_rest(place, shifts, occ, row, pair, there, mixed, blocks, sofar):
    return pl.pallas_call(
        rest_kernel,
        out_shape=jax.ShapeDtypeStruct(sofar.shape, jnp.float32),
        in_specs=[SMEM, SMEM, SMEM, VMEM, VMEM, VMEM, ANY, ANY, ANY],
        out_specs=VMEM,
        compiler_params=SMALL,
        scratch_shapes=[
            pltpu.VMEM((pair.shape[1],) * 2, jnp.float32),
            pltpu.VMEM(mixed.shape, mixed.dtype),
            pltpu.VMEM(blocks.shape, blocks.dtype),
            pltpu.VMEM(sofar.shape, jnp.float32),
            pltpu.SemaphoreType.DMA((3,)),
        ],
    )(place, shifts, occ, row, pair, there, far(mixed), far(blocks), far(sofar))


def local(factors, offsets, occ_energy, vir_energy):
    sizes = [lax.axis_size(a) for a in OCC]
    count = lax.axis_size(OCC)
    chip = lax.axis_index("zl").astype(jnp.int32)
    core = lax.axis_index("core").astype(jnp.int32)
    own = factors[0]
    nvir = own.shape[0]
    rows = nvir // 4
    row = vir_energy[None, :]
    costs = [0] + [busiest_link(s, sizes) for s in range(1, count)]
    cost = jnp.array(costs, jnp.int32)[offsets]
    late = cost[1] < cost[0]
    direct = jnp.where(late, offsets[1], offsets[0])
    routed = jnp.where(late, offsets[0], offsets[1])
    step = jnp.minimum(direct, count - direct)
    flip = (direct != step).astype(jnp.int32)
    place = jnp.stack([lax.axis_index(OCC).astype(jnp.int32), core, chip, flip])
    shifts = jnp.stack([step, count - step, routed, count - routed])

    held = exchange(to_pieces(own), OCC)
    ahead, behind = fetch_both_ways(own, step, count)
    outgoing = rolled(shifts[2:], held)
    got = exchange(outgoing, OCC)

    kept, sent = partials_direct(place, own, ahead, behind)
    came = swap(sent, "core")
    total = kept + came
    sent = total.astype(jnp.bfloat16)
    came = swap(sent, "zl")
    pair = total + came.astype(jnp.float32)
    there = swap(pair, "core")
    gamma, density = early_pairs(
        place, shifts, occ_energy, row, pair, there, ahead, behind
    )

    blocks, kept, sent = partials_routed(place, own, got)
    came = swap(sent, "core")
    total = kept + came
    sent = total.astype(jnp.bfloat16)
    came = swap(sent[0], "zl")
    second = swap(sent[1], "zl")
    pair = total[0] + came.astype(jnp.float32)
    there = swap(pair, "core")
    mixed, density = first_pair(place, shifts, occ_energy, row, pair, there, density)
    chip_sum, second, _ = lax.optimization_barrier((total[1], second, density))
    pair = chip_sum + second.astype(jnp.float32)
    there = swap(pair, "core")
    gamma = add_rest(place, shifts, occ_energy, row, pair, there, mixed, blocks, gamma)

    ny = lax.axis_size("y")
    nrow = lax.axis_size(ROWS)
    came = exchange(density.reshape(ny, rows // ny, nvir), "y")
    summed = jnp.sum(came.astype(jnp.float32), axis=0).astype(jnp.bfloat16)
    sent = jnp.broadcast_to(summed, (nrow, *summed.shape))
    came = exchange(sent, ROWS)
    summed = jnp.sum(came.astype(jnp.float32), axis=0).astype(jnp.bfloat16)
    sent = jnp.broadcast_to(summed, (ny, *summed.shape))
    came = exchange(sent, "y")
    return (gamma[None], came.reshape(rows, nvir).astype(jnp.float32))


def solution(mesh):
    split = Mesh(
        mesh.devices.reshape(4, 4, 8, 2, 2), ("zh", "x", "y", "zl", "core")
    )
    aux = ("zl", "core")

    return jax.shard_map(
        local,
        mesh=split,
        in_specs=(P(OCC, None, aux), P(), P(), P()),
        out_specs=(P(OCC, None, aux), P(aux, None)),
        check_vma=False,
    )
```

time: 191 us -> 241 us (1.26)
  the two profiles are of different devices: /device:TPU:4 before, /device:TPU:8 now
where the time goes in v1:
time: 241 us; the launch traced here: 240 us
  starting transfers between devices  113 us (47%)
  waiting for transfers between devices  96 us (40%)
  Pallas kernels  17.4 us (7%)
  local copies, waits for them, and re-layouts  5.7 us (2%)
  between operations  4.81 us (2%)
  other arithmetic  3.12 us (1%)
    all_to_all x5, starting transfers between devices, exchange(): return lax.all_to_all(value, axis, split_axis=0, concat_axis=0, tiled=True)  58.1 us
    ppermute x2, waiting for transfers between devices, branch(): return lambda v: (lax.ppermute(v, OCC, ahead), lax.ppermute(v, OCC, behind))  38.9 us
    all_to_all x5, waiting for transfers between devices, exchange(): return lax.all_to_all(value, axis, split_axis=0, concat_axis=0, tiled=True)  38 us
    ppermute x2, starting transfers between devices, branch(): return lambda v: (lax.ppermute(v, OCC, ahead), lax.ppermute(v, OCC, behind))  31.6 us
    ppermute x8, starting transfers between devices, swap(): return lax.ppermute(value, axis, [(0, 1), (1, 0)])  23.4 us
    ppermute x8, waiting for transfers between devices, swap(): return lax.ppermute(value, axis, [(0, 1), (1, 0)])  19.1 us
  transfers between devices with their start and end apart: 15, of which 8 were waited for; matrix products, arithmetic and copies ran while one was open for 2% of the time, Pallas kernels for 7%

profile of v1, /device:TPU:8, one launch (start us, length us, event | category | flops | bytes accessed | tf_op | source)
XLA Modules:
  0.0 240.3 jit_solution(16358411642385667947)
XLA Ops:
  0.7 19.8 %all-to-all-start = ((bf16[128,16,128]{2,1,0:T(8,128)(2,1)}), bf16[128,16,128]{2,1,0:T(8,128)(2,1)S(1)}, u32[]{:S(2)}, u32[]{:S(2)}) async-start(bf16[128,16,128]{2,1,0:T(8,128)(2,1)} %bitcast.34), calls=%async_computation | async-start | bytes 1048576 | tf_op jit(solution)/shard_map/all_to_all | solution.py:29
  25.0 16.6 %all-to-all-done.held_ref = bf16[128,16,128]{2,1,0:T(8,128)(2,1)S(1)} async-done(((bf16[128,16,128]{2,1,0:T(8,128)(2,1)}), bf16[128,16,128]{2,1,0:T(8,128)(2,1)S(1)}, u32[]{:S(2)}, u32[]{:S(2)}) %all-to-all-start) | async-done | bytes 524320 | tf_op jit(solution)/shard_map/all_to_all | solution.py:29
  43.2 7.3 %all-to-all-start.1 = ((bf16[128,32,128]{2,1,0:T(8,128)(2,1)}), bf16[128,32,128]{2,1,0:T(8,128)(2,1)S(1)}, u32[]{:S(2)}, u32[]{:S(2)}) async-start(bf16[128,32,128]{2,1,0:T(8,128)(2,1)} %shard_map.68), calls=%async_computation.1 | async-start | bytes 2097152 | tf_op jit(solution)/shard_map/all_to_all | solution.py:29
  51.8 70.6 %conditional.1 = (bf16[512,512]{1,0:T(8,128)(2,1)}, bf16[512,512]{1,0:T(8,128)(2,1)}) conditional(s32[]{:T(128)} %clamp.3, bf16[512,512]{1,0:T(8,128)(2,1)S(1)} %bitcast.66, bf16[512,512]{1,0:T(8,128)(2,1)S(1)} %bitcast.98, bf16[512,512]{1,0:T(8,128)(2,1)S(1)} %bitcast.37, bf16[512,512]{1,0:T(8,128)(2,1)S(1)} %bitcast.38, ...), branch_computations={%region_0.1_spmd, %region_1.2_spmd, %region_2.3_spmd, %region_3.4_... | conditional | bytes 4194400 | solution.py:72
  51.9 14.9 %collective-permute-start.92 = (bf16[512,512]{1,0:T(8,128)(2,1)S(1)}, bf16[512,512]{1,0:T(8,128)(2,1)}, u32[]{:S(2)}, u32[]{:S(2)}) collective-permute-start(bf16[512,512]{1,0:T(8,128)(2,1)S(1)} %param.46), channel_id=1, source_target_pairs={{0,324},{4,328},{8,332},{12,336},{16,340},{20,344},{24,348},{28,35... | collective-permute-start | bytes 1572872 | tf_op jit(solution)/shard_map/cond/branch_46_fun/ppermute | solution.py:70
  66.8 16.7 %collective-permute-start.93 = (bf16[512,512]{1,0:T(8,128)(2,1)S(1)}, bf16[512,512]{1,0:T(8,128)(2,1)}, u32[]{:S(2)}, u32[]{:S(2)}) collective-permute-start(bf16[512,512]{1,0:T(8,128)(2,1)S(1)} %param.46), channel_id=1, source_target_pairs={{0,188},{4,192},{8,196},{12,200},{16,204},{20,208},{24,212},{28,21... | collective-permute-start | bytes 1572872 | tf_op jit(solution)/shard_map/cond/branch_46_fun/ppermute | solution.py:70
  83.5 28.6 %collective-permute-done.92 = bf16[512,512]{1,0:T(8,128)(2,1)} collective-permute-done((bf16[512,512]{1,0:T(8,128)(2,1)S(1)}, bf16[512,512]{1,0:T(8,128)(2,1)}, u32[]{:S(2)}, u32[]{:S(2)}) %collective-permute-start.92) | collective-permute-done | bytes 524320 | tf_op jit(solution)/shard_map/cond/branch_46_fun/ppermute | solution.py:70
  112.1 10.3 %collective-permute-done.93 = bf16[512,512]{1,0:T(8,128)(2,1)} collective-permute-done((bf16[512,512]{1,0:T(8,128)(2,1)S(1)}, bf16[512,512]{1,0:T(8,128)(2,1)}, u32[]{:S(2)}, u32[]{:S(2)}) %collective-permute-start.93) | collective-permute-done | bytes 524320 | tf_op jit(solution)/shard_map/cond/branch_46_fun/ppermute | solution.py:70
  122.5 2.6 %shard_map.70 = (f32[2,256,512]{2,1,0:T(8,128)}, f32[2,256,512]{2,1,0:T(8,128)S(1)}) custom-call(s32[4]{0:T(128)S(1)} %pad_add_fusion.place_ref, bf16[512,512]{1,0:T(8,128)(2,1)S(1)} %bitcast.99, bf16[512,512]{1,0:T(8,128)(2,1)} %get-tuple-element.81.ahead_ref, bf16[512,512]{1,0:T(8,128)(2,1)} %get-tuple-element.82.behind_ref), custom_call_target="tpu_custom_call" | custom-call | tf_op jit(solution)/shard_map/pallas_call | solution.py:141
  129.2 2.4 %collective-permute-start.127 = (f32[2,256,512]{2,1,0:T(8,128)S(1)}, f32[2,256,512]{2,1,0:T(8,128)S(1)}, u32[]{:S(2)}, u32[]{:S(2)}) collective-permute-start(f32[2,256,512]{2,1,0:T(8,128)S(1)} %get-tuple-element.80), channel_id=1, source_target_pairs={{0,1},{1,0},{2,3},{3,2},{4,5},{5,4},{6,7},{7,6},{8,9},{9,8},{10,11... | collective-permute-start | bytes 3145736 | tf_op jit(solution)/shard_map/ppermute | solution.py:33
  133.2 5.9 %collective-permute-start.132 = (bf16[2,256,512]{2,1,0:T(8,128)(2,1)S(1)}, bf16[2,256,512]{2,1,0:T(8,128)(2,1)S(1)}, u32[]{:S(2)}, u32[]{:S(2)}) collective-permute-start(bf16[2,256,512]{2,1,0:T(8,128)(2,1)S(1)} %get-tuple-element.92), channel_id=1, source_target_pairs={{0,2},{2,0},{1,3},{3,1},{4,6},{6,4},{5,7},{7,5},{8,10},{10,8},{9,1... | collective-permute-start | bytes 1572872 | tf_op jit(solution)/shard_map/ppermute | solution.py:33
  139.1 12.1 %collective-permute-done.132 = bf16[2,256,512]{2,1,0:T(8,128)(2,1)S(1)} collective-permute-done((bf16[2,256,512]{2,1,0:T(8,128)(2,1)S(1)}, bf16[2,256,512]{2,1,0:T(8,128)(2,1)S(1)}, u32[]{:S(2)}, u32[]{:S(2)}) %collective-permute-start.132) | collective-permute-done | bytes 524320 | tf_op jit(solution)/shard_map/ppermute | solution.py:33
  154.6 3.6 %collective-permute-start.129 = (bf16[256,512]{1,0:T(8,128)(2,1)S(1)}, bf16[256,512]{1,0:T(8,128)(2,1)S(1)}, u32[]{:S(2)}, u32[]{:S(2)}) collective-permute-start(bf16[256,512]{1,0:T(8,128)(2,1)S(1)} %get-tuple-element.96), channel_id=1, source_target_pairs={{0,2},{2,0},{1,3},{3,1},{4,6},{6,4},{5,7},{7,5},{8,10},{10,8},{9,1... | collective-permute-start | bytes 786440 | tf_op jit(solution)/shard_map/ppermute | solution.py:33
  158.2 7.0 %collective-permute-done.129 = bf16[256,512]{1,0:T(8,128)(2,1)S(1)} collective-permute-done((bf16[256,512]{1,0:T(8,128)(2,1)S(1)}, bf16[256,512]{1,0:T(8,128)(2,1)S(1)}, u32[]{:S(2)}, u32[]{:S(2)}) %collective-permute-start.129) | collective-permute-done | bytes 262176 | tf_op jit(solution)/shard_map/ppermute | solution.py:33
  167.2 3.6 %collective-permute-start.128 = (bf16[256,512]{1,0:T(8,128)(2,1)}, bf16[256,512]{1,0:T(8,128)(2,1)S(1)}, u32[]{:S(2)}, u32[]{:S(2)}) collective-permute-start(bf16[256,512]{1,0:T(8,128)(2,1)} %get-tuple-element.97), channel_id=1, source_target_pairs={{0,2},{2,0},{1,3},{3,1},{4,6},{6,4},{5,7},{7,5},{8,10},{10,8},{9,1... | collective-permute-start | bytes 786440 | tf_op jit(solution)/shard_map/ppermute | solution.py:33
  171.6 4.1 %shard_map.71 = (f32[512,512]{1,0:T(8,128)}, f32[128,512]{1,0:T(8,128)}) custom-call(s32[4]{0:T(128)S(1)} %pad_add_fusion.place_ref, s32[4]{0:T(128)S(1)} %pad_add_fusion.1.shifts_ref, f32[128]{0:T(128)S(1)} %copy-done.2, f32[1,512]{1,0:T(1,128)S(1)} %bitcast.31, f32[2,256,512]{2,1,0:T(8,128)S(1)} %convert_add_fusion.pair_ref, ...), custom_call_target="tpu_custom_call" | custom-call | tf_op jit(solution)/shard_map/pallas_call | solution.py:231
  176.7 2.7 %shard_map.72 = (bf16[512,512]{1,0:T(8,128)(2,1)}, bf16[128,512]{1,0:T(8,128)(2,1)}) custom-call(s32[4]{0:T(128)S(1)} %pad_add_fusion.place_ref, s32[4]{0:T(128)S(1)} %pad_add_fusion.1.shifts_ref, f32[128]{0:T(128)S(1)} %copy-done.2, f32[1,512]{1,0:T(1,128)S(1)} %bitcast.32, f32[256,512]{1,0:T(8,128)S(1)} %fusion.pair_ref, ...), custom_call_target="tpu_custom_call" | custom-call | tf_op jit(solution)/shard_map/pallas_call | solution.py:261
  179.3 5.2 %all-to-all-start.2 = ((bf16[8,16,512]{2,1,0:T(8,128)(2,1)}), bf16[8,16,512]{2,1,0:T(8,128)(2,1)S(1)}, u32[]{:S(2)}, u32[]{:S(2)}) async-start(bf16[8,16,512]{2,1,0:T(8,128)(2,1)} %bitcast.102), calls=%async_computation.2 | async-start | bytes 262144 | tf_op jit(solution)/shard_map/all_to_all | solution.py:29
  184.6 7.9 %all-to-all-done.2 = bf16[8,16,512]{2,1,0:T(8,128)(2,1)S(1)} async-done(((bf16[8,16,512]{2,1,0:T(8,128)(2,1)}), bf16[8,16,512]{2,1,0:T(8,128)(2,1)S(1)}, u32[]{:S(2)}, u32[]{:S(2)}) %all-to-all-start.2) | async-done | bytes 131104 | tf_op jit(solution)/shard_map/all_to_all | solution.py:29
  193.3 21.0 %all-to-all-start.3 = ((bf16[16,16,512]{2,1,0:T(8,128)(2,1)}), bf16[16,16,512]{2,1,0:T(8,128)(2,1)S(1)}, u32[]{:S(2)}, u32[]{:S(2)}) async-start(bf16[16,16,512]{2,1,0:T(8,128)(2,1)} %broadcast_in_dim.18), calls=%async_computation.3 | async-start | bytes 524288 | tf_op jit(solution)/shard_map/all_to_all | solution.py:29
  216.3 10.1 %all-to-all-done.3 = bf16[16,16,512]{2,1,0:T(8,128)(2,1)S(1)} async-done(((bf16[16,16,512]{2,1,0:T(8,128)(2,1)}), bf16[16,16,512]{2,1,0:T(8,128)(2,1)S(1)}, u32[]{:S(2)}, u32[]{:S(2)}) %all-to-all-start.3) | async-done | bytes 262176 | tf_op jit(solution)/shard_map/all_to_all | solution.py:29
  227.2 4.7 %all-to-all-start.4 = ((bf16[8,16,512]{2,1,0:T(8,128)(2,1)}), bf16[8,16,512]{2,1,0:T(8,128)(2,1)S(1)}, u32[]{:S(2)}, u32[]{:S(2)}) async-start(bf16[8,16,512]{2,1,0:T(8,128)(2,1)} %broadcast_in_dim.19), calls=%async_computation.4 | async-start | bytes 262144 | tf_op jit(solution)/shard_map/all_to_all | solution.py:29
  231.9 4.3 %shard_map.73 = f32[512,512]{1,0:T(8,128)} custom-call(s32[4]{0:T(128)S(1)} %pad_add_fusion.place_ref, s32[4]{0:T(128)S(1)} %pad_add_fusion.1.shifts_ref, f32[128]{0:T(128)S(1)} %copy-done.2, f32[1,512]{1,0:T(1,128)S(1)} %bitcast.33, f32[256,512]{1,0:T(8,128)S(1)} %convert_add_fusion.1.pair_ref, f32[256,512]{1,0:T(8,128)S(1)} %collective-permute-done.134.there_ref, ...), custom_call_target="tpu_custom_call" | custom-call | tf_op jit(solution)/shard_map/pallas_call | solution.py:301
  236.2 3.4 %all-to-all-done.4 = bf16[8,16,512]{2,1,0:T(8,128)(2,1)S(1)} async-done(((bf16[8,16,512]{2,1,0:T(8,128)(2,1)}), bf16[8,16,512]{2,1,0:T(8,128)(2,1)S(1)}, u32[]{:S(2)}, u32[]{:S(2)}) %all-to-all-start.4) | async-done | bytes 131104 | tf_op jit(solution)/shard_map/all_to_all | solution.py:29
  (53 shorter events, 20.4 us)
Async XLA Ops:
  0.6 19.9 %copy-start.9 = (s32[2]{0:T(128)S(1)}, s32[2]{0:T(128)}, u32[]{:S(2)}) copy-start(s32[2]{0:T(128)} %param.70) | copy-start | bytes 28
  0.6 19.9 %copy-start.3 = (s32[128]{0:T(128)S(1)}, s32[128]{0:T(128)}, u32[]{:S(2)}) copy-start(s32[128]{0:T(128)} %constant.43.clone) | copy-start | bytes 1540
  0.7 40.9 %all-to-all-start = ((bf16[128,16,128]{2,1,0:T(8,128)(2,1)}), bf16[128,16,128]{2,1,0:T(8,128)(2,1)S(1)}, u32[]{:S(2)}, u32[]{:S(2)}) async-start(bf16[128,16,128]{2,1,0:T(8,128)(2,1)} %bitcast.34), calls=%async_computation | async-start | bytes 1048576 | tf_op jit(solution)/shard_map/all_to_all | solution.py:29
  43.2 8.6 %copy-start.4 = (bf16[1,512,512]{2,1,0:T(8,128)(2,1)S(1)}, bf16[1,512,512]{2,1,0:T(8,128)(2,1)}, u32[]{:S(2)}) copy-start(bf16[1,512,512]{2,1,0:T(8,128)(2,1)} %param.69) | copy-start | bytes 1572868
  43.2 83.9 %all-to-all-start.1 = ((bf16[128,32,128]{2,1,0:T(8,128)(2,1)}), bf16[128,32,128]{2,1,0:T(8,128)(2,1)S(1)}, u32[]{:S(2)}, u32[]{:S(2)}) async-start(bf16[128,32,128]{2,1,0:T(8,128)(2,1)} %shard_map.68), calls=%async_computation.1 | async-start | bytes 2097152 | tf_op jit(solution)/shard_map/all_to_all | solution.py:29
  51.9 60.3 %collective-permute-start.92 = (bf16[512,512]{1,0:T(8,128)(2,1)S(1)}, bf16[512,512]{1,0:T(8,128)(2,1)}, u32[]{:S(2)}, u32[]{:S(2)}) collective-permute-start(bf16[512,512]{1,0:T(8,128)(2,1)S(1)} %param.46), channel_id=1, source_target_pairs={{0,324},{4,328},{8,332},{12,336},{16,340},{20,344},{24,348},{28,35... | collective-permute-start | bytes 1572872 | tf_op jit(solution)/shard_map/cond/branch_46_fun/ppermute | solution.py:70
  66.8 55.7 %collective-permute-start.93 = (bf16[512,512]{1,0:T(8,128)(2,1)S(1)}, bf16[512,512]{1,0:T(8,128)(2,1)}, u32[]{:S(2)}, u32[]{:S(2)}) collective-permute-start(bf16[512,512]{1,0:T(8,128)(2,1)S(1)} %param.46), channel_id=1, source_target_pairs={{0,188},{4,192},{8,196},{12,200},{16,204},{20,208},{24,212},{28,21... | collective-permute-start | bytes 1572872 | tf_op jit(solution)/shard_map/cond/branch_46_fun/ppermute | solution.py:70
  125.2 6.5 %collective-permute-start.131 = (f32[2,256,512]{2,1,0:T(8,128)S(1)}, f32[2,256,512]{2,1,0:T(8,128)}, u32[]{:S(2)}, u32[]{:S(2)}) collective-permute-start(f32[2,256,512]{2,1,0:T(8,128)S(1)} %get-tuple-element.84), channel_id=1, source_target_pairs={{0,1},{1,0},{2,3},{3,2},{4,5},{5,4},{6,7},{7,6},{8,9},{9,8},{10,11... | collective-permute-start | bytes 3145736 | tf_op jit(solution)/shard_map/ppermute | solution.py:33
  127.1 4.5 %copy-start.8 = (f32[2,256,512]{2,1,0:T(8,128)S(1)}, f32[2,256,512]{2,1,0:T(8,128)}, u32[]{:S(2)}) copy-start(f32[2,256,512]{2,1,0:T(8,128)} %get-tuple-element.83) | copy-start | bytes 3145732
  129.2 24.2 %collective-permute-start.127 = (f32[2,256,512]{2,1,0:T(8,128)S(1)}, f32[2,256,512]{2,1,0:T(8,128)S(1)}, u32[]{:S(2)}, u32[]{:S(2)}) collective-permute-start(f32[2,256,512]{2,1,0:T(8,128)S(1)} %get-tuple-element.80), channel_id=1, source_target_pairs={{0,1},{1,0},{2,3},{3,2},{4,5},{5,4},{6,7},{7,6},{8,9},{9,8},{10,11... | collective-permute-start | bytes 3145736 | tf_op jit(solution)/shard_map/ppermute | solution.py:33
  133.2 18.1 %collective-permute-start.132 = (bf16[2,256,512]{2,1,0:T(8,128)(2,1)S(1)}, bf16[2,256,512]{2,1,0:T(8,128)(2,1)S(1)}, u32[]{:S(2)}, u32[]{:S(2)}) collective-permute-start(bf16[2,256,512]{2,1,0:T(8,128)(2,1)S(1)} %get-tuple-element.92), channel_id=1, source_target_pairs={{0,2},{2,0},{1,3},{3,1},{4,6},{6,4},{5,7},{7,5},{8,10},{10,8},{9,1... | collective-permute-start | bytes 1572872 | tf_op jit(solution)/shard_map/ppermute | solution.py:33
  151.2 2.3 copy-start.7
  151.4 19.5 %collective-permute-start.133 = (f32[2,256,512]{2,1,0:T(8,128)S(1)}, f32[2,256,512]{2,1,0:T(8,128)S(1)}, u32[]{:S(2)}, u32[]{:S(2)}) collective-permute-start(f32[2,256,512]{2,1,0:T(8,128)S(1)} %convert_add_fusion.pair_ref), channel_id=1, source_target_pairs={{0,1},{1,0},{2,3},{3,2},{4,5},{5,4},{6,7},{7,6},{8,9},{9,8},{10,11... | collective-permute-start | bytes 3145736 | tf_op jit(solution)/shard_map/ppermute | solution.py:33
  153.8 11.5 %copy-start.5 = (f32[2,256,512]{2,1,0:T(8,128)}, f32[2,256,512]{2,1,0:T(8,128)S(1)}, u32[]{:S(2)}) copy-start(f32[2,256,512]{2,1,0:T(8,128)S(1)} %get-tuple-element.95) | copy-start | bytes 3145732
  154.6 10.6 %collective-permute-start.129 = (bf16[256,512]{1,0:T(8,128)(2,1)S(1)}, bf16[256,512]{1,0:T(8,128)(2,1)S(1)}, u32[]{:S(2)}, u32[]{:S(2)}) collective-permute-start(bf16[256,512]{1,0:T(8,128)(2,1)S(1)} %get-tuple-element.96), channel_id=1, source_target_pairs={{0,2},{2,0},{1,3},{3,1},{4,6},{6,4},{5,7},{7,5},{8,10},{10,8},{9,1... | collective-permute-start | bytes 786440 | tf_op jit(solution)/shard_map/ppermute | solution.py:33
  165.3 10.4 %collective-permute-start.130 = (f32[256,512]{1,0:T(8,128)S(1)}, f32[256,512]{1,0:T(8,128)S(1)}, u32[]{:S(2)}, u32[]{:S(2)}) collective-permute-start(f32[256,512]{1,0:T(8,128)S(1)} %fusion.pair_ref), channel_id=1, source_target_pairs={{0,1},{1,0},{2,3},{3,2},{4,5},{5,4},{6,7},{7,6},{8,9},{9,8},{10,11... | collective-permute-start | bytes 1572872 | tf_op jit(solution)/shard_map/ppermute | solution.py:33
  167.2 17.4 %collective-permute-start.128 = (bf16[256,512]{1,0:T(8,128)(2,1)}, bf16[256,512]{1,0:T(8,128)(2,1)S(1)}, u32[]{:S(2)}, u32[]{:S(2)}) collective-permute-start(bf16[256,512]{1,0:T(8,128)(2,1)} %get-tuple-element.97), channel_id=1, source_target_pairs={{0,2},{2,0},{1,3},{3,1},{4,6},{6,4},{5,7},{7,5},{8,10},{10,8},{9,1... | collective-permute-start | bytes 786440 | tf_op jit(solution)/shard_map/ppermute | solution.py:33
  170.8 0.7 copy-start.1
  175.7 1.0 copy-start
  176.7 7.9 %copy-start.6 = (f32[2,256,512]{2,1,0:T(8,128)S(1)}, f32[2,256,512]{2,1,0:T(8,128)}, u32[]{:S(2)}) copy-start(f32[2,256,512]{2,1,0:T(8,128)} %copy-done.5) | copy-start | bytes 3145732
  179.3 13.2 %all-to-all-start.2 = ((bf16[8,16,512]{2,1,0:T(8,128)(2,1)}), bf16[8,16,512]{2,1,0:T(8,128)(2,1)S(1)}, u32[]{:S(2)}, u32[]{:S(2)}) async-start(bf16[8,16,512]{2,1,0:T(8,128)(2,1)} %bitcast.102), calls=%async_computation.2 | async-start | bytes 262144 | tf_op jit(solution)/shard_map/all_to_all | solution.py:29
  193.3 33.2 %all-to-all-start.3 = ((bf16[16,16,512]{2,1,0:T(8,128)(2,1)}), bf16[16,16,512]{2,1,0:T(8,128)(2,1)S(1)}, u32[]{:S(2)}, u32[]{:S(2)}) async-start(bf16[16,16,512]{2,1,0:T(8,128)(2,1)} %broadcast_in_dim.18), calls=%async_computation.3 | async-start | bytes 524288 | tf_op jit(solution)/shard_map/all_to_all | solution.py:29
  214.4 17.5 %collective-permute-start.134 = (f32[256,512]{1,0:T(8,128)S(1)}, f32[256,512]{1,0:T(8,128)S(1)}, u32[]{:S(2)}, u32[]{:S(2)}) collective-permute-start(f32[256,512]{1,0:T(8,128)S(1)} %convert_add_fusion.1.pair_ref), channel_id=1, source_target_pairs={{0,1},{1,0},{2,3},{3,2},{4,5},{5,4},{6,7},{7,6},{8,9},{9,8},{10,11... | collective-permute-start | bytes 1572872 | tf_op jit(solution)/shard_map/ppermute | solution.py:33
  227.2 12.4 %all-to-all-start.4 = ((bf16[8,16,512]{2,1,0:T(8,128)(2,1)}), bf16[8,16,512]{2,1,0:T(8,128)(2,1)S(1)}, u32[]{:S(2)}, u32[]{:S(2)}) async-start(bf16[8,16,512]{2,1,0:T(8,128)(2,1)} %broadcast_in_dim.19), calls=%async_computation.4 | async-start | bytes 262144 | tf_op jit(solution)/shard_map/all_to_all | solution.py:29
  (1 other events, 0.7 us)

commit v2 on v0

--- a/solution.py
+++ b/solution.py
@@ -10,6 +10,7 @@
 
 OCC = ("zh", "x", "y")
 REST = ("zh", "x", "zl")
+ROW = 8
 SUB = 16
 LANES = 128
 VMEM = pl.BlockSpec(memory_space=pltpu.VMEM)
@@ -42,7 +43,7 @@
 
 def to_pieces(block):
     tall, wide = block.shape
-    tiles = block.reshape(tall // SUB, SUB, wide // LANES, LANES)
+    tiles = block.reshape(tall // ROW, ROW, wide // LANES, LANES)
     return tiles.transpose(0, 2, 1, 3).reshape(-1, SUB, LANES)
 
 
@@ -81,53 +82,43 @@
 
 
 def partial_kernel(
-    group, place_ref, own_ref, got_ref, block_ref, kept_ref, sent_ref, held_ref, mine_ref,
-    sems,
+    chip_first, place_ref, own_ref, got_ref, block_ref, kept_ref, sent_ref, held_ref, sem
 ):
     noff, tall, wide = held_ref.shape
     half = tall // 2
-    core = place_ref[1]
+    core, chip = place_ref[1], place_ref[2]
     for k in range(noff):
-        first = (group * noff + k) * SUB
         for c in range(wide // LANES):
-            tile = got_ref[:, c, first : first + SUB, :]
+            side, at = c * ROW // SUB, k * SUB + c * ROW % SUB
+            tile = got_ref[:, side, at : at + ROW, :]
             held_ref[k, :, c * LANES : (c + 1) * LANES] = tile.reshape(tall, LANES)
-    copies = [
-        pltpu.make_async_copy(held_ref, block_ref, sems.at[0]),
-        pltpu.make_async_copy(mine_ref, kept_ref, sems.at[1]),
-    ]
-    copies[0].start()
+    out = pltpu.make_async_copy(held_ref, block_ref, sem)
+    out.start()
     mine = own_ref[pl.ds(pl.multiple_of(core * half, half), half), :]
     other = own_ref[pl.ds(pl.multiple_of((1 - core) * half, half), half), :]
     for k in range(noff):
-        mine_ref[k] = inner(mine, held_ref[k])
-    copies[1].start()
-    for k in range(noff):
-        sent_ref[k] = inner(other, held_ref[k])
-    for copy in copies:
-        copy.wait()
-
-
-def partials(place, own, got, group):
+        block = held_ref[(chip if k == 0 else 1 - chip) if chip_first else k]
+        kept_ref[k] = inner(mine, block)
+        sent_ref[k] = inner(other, block)
+    out.wait()
+
+
+def partials(place, own, got, chip_first):
     tall, wide = own.shape
-    noff = got.shape[1] // SUB // 2
-    got = got.reshape(tall // SUB, wide // LANES, 2 * noff * SUB, LANES)
+    noff = got.shape[1] // SUB
+    got = got.reshape(tall // ROW, -1, noff * SUB, LANES)
     half, whole = (noff, tall // 2, tall), (noff, tall, wide)
     return pl.pallas_call(
-        functools.partial(partial_kernel, group),
+        functools.partial(partial_kernel, chip_first),
         out_shape=(
             pltpu.HBM(whole, own.dtype),
-            pltpu.HBM(half, jnp.float32),
-            jax.ShapeDtypeStruct(half, jnp.float32),
+            pltpu.VMEM(half, jnp.float32),
+            pltpu.VMEM(half, jnp.float32),
         ),
         in_specs=[SMEM, VMEM, VMEM],
-        out_specs=(ANY, ANY, VMEM),
-        compiler_params=SMALL,
-        scratch_shapes=[
-            pltpu.VMEM(whole, own.dtype),
-            pltpu.VMEM(half, jnp.float32),
-            pltpu.SemaphoreType.DMA((2,)),
-        ],
+        out_specs=(ANY, VMEM, VMEM),
+        compiler_params=SMALL,
+        scratch_shapes=[pltpu.VMEM(whole, own.dtype), pltpu.SemaphoreType.DMA],
     )(place, own, near(got))
 
 
@@ -253,28 +244,32 @@
     shifts = jnp.concatenate([offsets, count - offsets])
 
     held = exchange(to_pieces(own), OCC)
-    outgoing = rolled(shifts, held)
-    got = exchange(outgoing, OCC)
-
-    ahead, kept, sent = partials(place, own, got, 0)
+    outgoing = rolled(shifts[:2], held)
+    got_ahead = exchange(outgoing, OCC)
+    outgoing = rolled(shifts[2:], held)
+    got_behind = exchange(outgoing, OCC)
+
+    ahead, kept, sent = partials(place, own, got_ahead, True)
     came = swap(sent, "core")
     total = kept + came
-    mine = lax.dynamic_index_in_dim(total, chip, 0, keepdims=False)
-    yours = lax.dynamic_index_in_dim(total, 1 - chip, 0, keepdims=False)
-    sent = yours.astype(jnp.bfloat16)
-    came = swap(sent, "zl")
-    pair = mine + came.astype(jnp.float32)
+    sent = total.astype(jnp.bfloat16)
+    came = swap(sent[1], "zl")
+    second = swap(sent[0], "zl")
+    pair = total[0] + came.astype(jnp.float32)
     there = swap(pair, "core")
     mixed, density = first_pair(
         place, shifts, occ_energy, row, pair, there, lax.axis_size("y")
     )
 
-    behind, kept, sent = partials(place, own, got, 1)
+    behind, kept, sent = partials(place, own, got_behind, False)
     came = swap(sent, "core")
     back = kept + came
-    sent = jnp.concatenate([mine[None], back]).astype(jnp.bfloat16)
+    sent = back.astype(jnp.bfloat16)
     came = swap(sent, "zl")
-    pair = jnp.concatenate([yours[None], back]) + came.astype(jnp.float32)
+    waiting, second, _ = lax.optimization_barrier((total[1], second, density))
+    pair = jnp.concatenate([waiting[None], back]) + jnp.concatenate(
+        [second[None], came]
+    ).astype(jnp.float32)
     there = swap(pair, "core")
     sofar = product(place, mixed, ahead)
     gamma = add_rest(place, shifts, occ_energy, row, pair, there, ahead, behind, sofar)

time: 191 us -> 204 us (1.068)
  the two profiles are of different devices: /device:TPU:4 before, /device:TPU:2 now
where the time goes in v2:
time: 204 us; the launch traced here: 203 us
  waiting for transfers between devices  71.9 us (35%)
  blocking collectives  63.5 us (31%)
  starting transfers between devices  39.5 us (19%)
  Pallas kernels  18.8 us (9%)
  other arithmetic  5.26 us (3%)
  local copies, waits for them, and re-layouts  3.12 us (2%)
    all_to_all x2, blocking collectives, exchange(): return lax.all_to_all(value, axis, split_axis=0, concat_axis=0, tiled=True)  63.5 us
    all_to_all x4, waiting for transfers between devices, exchange(): return lax.all_to_all(value, axis, split_axis=0, concat_axis=0, tiled=True)  55 us
    all_to_all x4, starting transfers between devices, exchange(): return lax.all_to_all(value, axis, split_axis=0, concat_axis=0, tiled=True)  22.5 us
    ppermute x7, starting transfers between devices, swap(): return lax.ppermute(value, axis, [(0, 1), (1, 0)])  17 us
    ppermute x7, waiting for transfers between devices, swap(): return lax.ppermute(value, axis, [(0, 1), (1, 0)])  16.9 us
    pallas_call x2, Pallas kernels, partials(): pl.pallas_call(functools.partial(partial_kernel, chip_first), out_shape=(...  5.33 us
    pallas_call x1, Pallas kernels, add_rest(): pl.pallas_call(rest_kernel, out_shape=jax.ShapeDtypeStruct(sofar.shape, j...  4.55 us
  transfers between devices with their start and end apart: 11, of which 5 were waited for; matrix products, arithmetic and copies ran while one was open for 3% of the time, Pallas kernels for 8%

profile of v2, /device:TPU:2, one launch (start us, length us, event | category | flops | bytes accessed | tf_op | source)
XLA Modules:
  0.0 203.0 jit_solution(10228170233205322709)
XLA Ops:
  0.6 40.6 %all_to_all.30.held_ref = bf16[128,16,128]{2,1,0:T(8,128)(2,1)S(1)} all-to-all(bf16[128,16,128]{2,1,0:T(8,128)(2,1)} %bitcast.29), channel_id=1, replica_groups=mesh['zh'=4,'x'=4,'y'=8,'zl'=2,'core'=2] {'zh','x','y'}, dimensions={0} | all-to-all | bytes 1048576 | tf_op jit(solution)/shard_map/all_to_all | solution.py:31
  41.9 1.7 shard_map.59
  43.6 7.5 %all-to-all-start.1 = ((bf16[128,32,128]{2,1,0:T(8,128)(2,1)}), bf16[128,32,128]{2,1,0:T(8,128)(2,1)S(1)}, u32[]{:S(2)}, u32[]{:S(2)}) async-start(bf16[128,32,128]{2,1,0:T(8,128)(2,1)} %shard_map.59), calls=%async_computation.1 | async-start | bytes 2097152 | tf_op jit(solution)/shard_map/all_to_all | solution.py:31
  52.8 29.2 %all-to-all-done.1 = bf16[128,32,128]{2,1,0:T(8,128)(2,1)S(1)} async-done(((bf16[128,32,128]{2,1,0:T(8,128)(2,1)}), bf16[128,32,128]{2,1,0:T(8,128)(2,1)S(1)}, u32[]{:S(2)}, u32[]{:S(2)}) %all-to-all-start.1) | async-done | bytes 1048608 | tf_op jit(solution)/shard_map/all_to_all | solution.py:31
  82.1 7.8 %all-to-all-start.2 = ((bf16[128,32,128]{2,1,0:T(8,128)(2,1)}), bf16[128,32,128]{2,1,0:T(8,128)(2,1)S(1)}, u32[]{:S(2)}, u32[]{:S(2)}) async-start(bf16[128,32,128]{2,1,0:T(8,128)(2,1)} %shard_map.62), calls=%async_computation.2 | async-start | bytes 2097152 | tf_op jit(solution)/shard_map/all_to_all | solution.py:31
  90.0 3.2 %shard_map.60 = (bf16[2,512,512]{2,1,0:T(8,128)(2,1)}, f32[2,256,512]{2,1,0:T(8,128)S(1)}, f32[2,256,512]{2,1,0:T(8,128)}) custom-call(s32[3]{0:T(128)S(1)} %pad_add_fusion.place_ref, bf16[512,512]{1,0:T(8,128)(2,1)S(1)} %bitcast.30, bf16[64,2,32,128]{3,2,1,0:T(8,128)(2,1)S(1)} %bitcast.33), custom_call_target="tpu_custom_call" | custom-call | tf_op jit(solution)/shard_map/pallas_call | solution.py:111
  94.1 2.0 %collective-permute-start = (f32[2,256,512]{2,1,0:T(8,128)}, f32[2,256,512]{2,1,0:T(8,128)}, u32[]{:S(2)}, u32[]{:S(2)}) collective-permute-start(f32[2,256,512]{2,1,0:T(8,128)} %get-tuple-element.13), channel_id=1, source_target_pairs={{0,1},{1,0},{2,3},{3,2},{4,5},{5,4},{6,7},{7,6},{8,9},{9,8},{10,11... | collective-permute-start | bytes 3145736 | tf_op jit(solution)/shard_map/ppermute | solution.py:35
  96.2 24.1 %all-to-all-done.2 = bf16[128,32,128]{2,1,0:T(8,128)(2,1)S(1)} async-done(((bf16[128,32,128]{2,1,0:T(8,128)(2,1)}), bf16[128,32,128]{2,1,0:T(8,128)(2,1)S(1)}, u32[]{:S(2)}, u32[]{:S(2)}) %all-to-all-start.2) | async-done | bytes 1048608 | tf_op jit(solution)/shard_map/all_to_all | solution.py:31
  120.3 2.1 %shard_map.63 = (bf16[2,512,512]{2,1,0:T(8,128)(2,1)}, f32[2,256,512]{2,1,0:T(8,128)S(1)}, f32[2,256,512]{2,1,0:T(8,128)S(1)}) custom-call(s32[3]{0:T(128)S(1)} %pad_add_fusion.place_ref, bf16[512,512]{1,0:T(8,128)(2,1)S(1)} %bitcast.31, bf16[64,2,32,128]{3,2,1,0:T(8,128)(2,1)S(1)} %bitcast.32), custom_call_target="tpu_custom_call" | custom-call | tf_op jit(solution)/shard_map/pallas_call | solution.py:111
  122.4 1.9 collective-permute-start.4
  125.9 3.4 %collective-permute-start.2 = (bf16[256,512]{1,0:T(8,128)(2,1)S(1)}, bf16[256,512]{1,0:T(8,128)(2,1)S(1)}, u32[]{:S(2)}, u32[]{:S(2)}) collective-permute-start(bf16[256,512]{1,0:T(8,128)(2,1)S(1)} %get-tuple-element.26), channel_id=1, source_target_pairs={{0,2},{2,0},{1,3},{3,1},{4,6},{6,4},{5,7},{7,5},{8,10},{10,8},{9,1... | collective-permute-start | bytes 786440 | tf_op jit(solution)/shard_map/ppermute | solution.py:35
  129.3 7.2 %collective-permute-done.2 = bf16[256,512]{1,0:T(8,128)(2,1)S(1)} collective-permute-done((bf16[256,512]{1,0:T(8,128)(2,1)S(1)}, bf16[256,512]{1,0:T(8,128)(2,1)S(1)}, u32[]{:S(2)}, u32[]{:S(2)}) %collective-permute-start.2) | collective-permute-done | bytes 262176 | tf_op jit(solution)/shard_map/ppermute | solution.py:35
  136.6 1.9 collective-permute-start.3
  138.8 3.4 %collective-permute-start.5 = (bf16[2,256,512]{2,1,0:T(8,128)(2,1)S(1)}, bf16[2,256,512]{2,1,0:T(8,128)(2,1)}, u32[]{:S(2)}, u32[]{:S(2)}) collective-permute-start(bf16[2,256,512]{2,1,0:T(8,128)(2,1)S(1)} %get-tuple-element.22), channel_id=1, source_target_pairs={{0,2},{2,0},{1,3},{3,1},{4,6},{6,4},{5,7},{7,5},{8,10},{10,8},{9,1... | collective-permute-start | bytes 1572872 | tf_op jit(solution)/shard_map/ppermute | solution.py:35
  142.2 2.5 %collective-permute-start.1 = (bf16[256,512]{1,0:T(8,128)(2,1)S(1)}, bf16[256,512]{1,0:T(8,128)(2,1)S(1)}, u32[]{:S(2)}, u32[]{:S(2)}) collective-permute-start(bf16[256,512]{1,0:T(8,128)(2,1)S(1)} %get-tuple-element.27), channel_id=1, source_target_pairs={{0,2},{2,0},{1,3},{3,1},{4,6},{6,4},{5,7},{7,5},{8,10},{10,8},{9,1... | collective-permute-start | bytes 786440 | tf_op jit(solution)/shard_map/ppermute | solution.py:35
  144.8 2.7 %shard_map.61 = (bf16[512,512]{1,0:T(8,128)(2,1)}, bf16[8,2,16,512]{3,2,1,0:T(8,128)(2,1)}) custom-call(s32[3]{0:T(128)S(1)} %pad_add_fusion.place_ref, s32[4]{0:T(128)S(1)} %pad_add_fusion.1.shifts_ref, f32[128]{0:T(128)S(1)} %copy-done.4, f32[1,512]{1,0:T(1,128)S(1)} %bitcast.34, f32[256,512]{1,0:T(8,128)S(1)} %fusion.pair_ref, ...), custom_call_target="tpu_custom_call" | custom-call | tf_op jit(solution)/shard_map/pallas_call | solution.py:161
  147.6 3.4 %all-to-all-start.3 = ((bf16[8,2,16,512]{3,2,1,0:T(8,128)(2,1)}), bf16[8,2,16,512]{3,2,1,0:T(8,128)(2,1)S(1)}, u32[]{:S(2)}, u32[]{:S(2)}) async-start(bf16[8,2,16,512]{3,2,1,0:T(8,128)(2,1)} %get-tuple-element.14), calls=%async_computation.3 | async-start | bytes 524288 | tf_op jit(solution)/shard_map/all_to_all | solution.py:31
  151.0 9.7 %collective-permute-done.1 = bf16[256,512]{1,0:T(8,128)(2,1)S(1)} collective-permute-done((bf16[256,512]{1,0:T(8,128)(2,1)S(1)}, bf16[256,512]{1,0:T(8,128)(2,1)S(1)}, u32[]{:S(2)}, u32[]{:S(2)}) %collective-permute-start.1) | collective-permute-done | bytes 262176 | tf_op jit(solution)/shard_map/ppermute | solution.py:35
  162.8 1.9 collective-permute-start.6
  164.8 22.9 %all_to_all.31 = bf16[32,16,512]{2,1,0:T(8,128)(2,1)} all-to-all(bf16[32,16,512]{2,1,0:T(8,128)(2,1)S(1)} %bitcast.37), channel_id=1, replica_groups=mesh['zh'=4,'x'=4,'y'=8,'zl'=2,'core'=2] {'zh','x','zl'}, dimensions={0} | all-to-all | bytes 1048576 | tf_op jit(solution)/shard_map/all_to_all | solution.py:31
  189.5 3.8 %all-to-all-start.5 = ((bf16[8,16,512]{2,1,0:T(8,128)(2,1)}), bf16[8,16,512]{2,1,0:T(8,128)(2,1)S(1)}, u32[]{:S(2)}, u32[]{:S(2)}) async-start(bf16[8,16,512]{2,1,0:T(8,128)(2,1)} %broadcast_in_dim.23), calls=%async_computation.5 | async-start | bytes 262144 | tf_op jit(solution)/shard_map/all_to_all | solution.py:31
  193.2 2.8 %shard_map.64.sofar_ref = f32[512,512]{1,0:T(8,128)} custom-call(s32[3]{0:T(128)S(1)} %pad_add_fusion.place_ref, bf16[512,512]{1,0:T(8,128)(2,1)} %get-tuple-element.21.mixed_ref, bf16[2,512,512]{2,1,0:T(8,128)(2,1)} %get-tuple-element.19.block_ref.ahead_ref), custom_call_target="tpu_custom_call" | custom-call | tf_op jit(solution)/shard_map/pallas_call | solution.py:184
  196.1 4.6 %shard_map.65 = f32[512,512]{1,0:T(8,128)} custom-call(s32[3]{0:T(128)S(1)} %pad_add_fusion.place_ref, s32[4]{0:T(128)S(1)} %pad_add_fusion.1.shifts_ref, f32[128]{0:T(128)S(1)} %copy-done.4, f32[1,512]{1,0:T(1,128)S(1)} %bitcast.35, f32[3,256,512]{2,1,0:T(8,128)S(1)} %maximum_add_fusion.pair_ref, f32[3,256,512]{2,1,0:T(8,128)S(1)} %collective-permute-done.6.there_ref, ...), custom_call_target="tpu_custom_call" | custom-call | tf_op jit(solution)/shard_map/pallas_call | solution.py:220
  200.6 1.7 all-to-all-done.5
  (37 shorter events, 10.1 us)
Async XLA Ops:
  41.3 0.7 copy-start.5
  41.9 9.2 %copy-start.6 = (s32[2]{0:T(128)S(1)}, s32[2]{0:T(128)}, u32[]{:S(2)}) copy-start(s32[2]{0:T(128)} %starts_ref.1) | copy-start | bytes 28
  43.6 38.5 %all-to-all-start.1 = ((bf16[128,32,128]{2,1,0:T(8,128)(2,1)}), bf16[128,32,128]{2,1,0:T(8,128)(2,1)S(1)}, u32[]{:S(2)}, u32[]{:S(2)}) async-start(bf16[128,32,128]{2,1,0:T(8,128)(2,1)} %shard_map.59), calls=%async_computation.1 | async-start | bytes 2097152 | tf_op jit(solution)/shard_map/all_to_all | solution.py:31
  51.2 38.8 %copy-start = (bf16[1,512,512]{2,1,0:T(8,128)(2,1)S(1)}, bf16[1,512,512]{2,1,0:T(8,128)(2,1)}, u32[]{:S(2)}) copy-start(bf16[1,512,512]{2,1,0:T(8,128)(2,1)} %param.4) | copy-start | bytes 1572868
  82.1 38.2 %all-to-all-start.2 = ((bf16[128,32,128]{2,1,0:T(8,128)(2,1)}), bf16[128,32,128]{2,1,0:T(8,128)(2,1)S(1)}, u32[]{:S(2)}, u32[]{:S(2)}) async-start(bf16[128,32,128]{2,1,0:T(8,128)(2,1)} %shard_map.62), calls=%async_computation.2 | async-start | bytes 2097152 | tf_op jit(solution)/shard_map/all_to_all | solution.py:31
  93.2 1.0 copy-start.1
  94.1 30.2 %copy-start.2 = (f32[2,256,512]{2,1,0:T(8,128)S(1)}, f32[2,256,512]{2,1,0:T(8,128)}, u32[]{:S(2)}) copy-start(f32[2,256,512]{2,1,0:T(8,128)} %copy-done.1) | copy-start | bytes 3145732
  94.1 30.2 %collective-permute-start = (f32[2,256,512]{2,1,0:T(8,128)}, f32[2,256,512]{2,1,0:T(8,128)}, u32[]{:S(2)}, u32[]{:S(2)}) collective-permute-start(f32[2,256,512]{2,1,0:T(8,128)} %get-tuple-element.13), channel_id=1, source_target_pairs={{0,1},{1,0},{2,3},{3,2},{4,5},{5,4},{6,7},{7,6},{8,9},{9,8},{10,11... | collective-permute-start | bytes 3145736 | tf_op jit(solution)/shard_map/ppermute | solution.py:35
  122.4 16.1 %collective-permute-start.4 = (f32[2,256,512]{2,1,0:T(8,128)S(1)}, f32[2,256,512]{2,1,0:T(8,128)S(1)}, u32[]{:S(2)}, u32[]{:S(2)}) collective-permute-start(f32[2,256,512]{2,1,0:T(8,128)S(1)} %get-tuple-element.17), channel_id=1, source_target_pairs={{0,1},{1,0},{2,3},{3,2},{4,5},{5,4},{6,7},{7,6},{8,9},{9,8},{10,11... | collective-permute-start | bytes 3145736 | tf_op jit(solution)/shard_map/ppermute | solution.py:35
  125.9 10.6 %collective-permute-start.2 = (bf16[256,512]{1,0:T(8,128)(2,1)S(1)}, bf16[256,512]{1,0:T(8,128)(2,1)S(1)}, u32[]{:S(2)}, u32[]{:S(2)}) collective-permute-start(bf16[256,512]{1,0:T(8,128)(2,1)S(1)} %get-tuple-element.26), channel_id=1, source_target_pairs={{0,2},{2,0},{1,3},{3,1},{4,6},{6,4},{5,7},{7,5},{8,10},{10,8},{9,1... | collective-permute-start | bytes 786440 | tf_op jit(solution)/shard_map/ppermute | solution.py:35
  136.6 8.2 %collective-permute-start.3 = (f32[256,512]{1,0:T(8,128)S(1)}, f32[256,512]{1,0:T(8,128)S(1)}, u32[]{:S(2)}, u32[]{:S(2)}) collective-permute-start(f32[256,512]{1,0:T(8,128)S(1)} %fusion.pair_ref), channel_id=1, source_target_pairs={{0,1},{1,0},{2,3},{3,2},{4,5},{5,4},{6,7},{7,6},{8,9},{9,8},{10,11... | collective-permute-start | bytes 1572872 | tf_op jit(solution)/shard_map/ppermute | solution.py:35
  138.5 6.3 %copy-start.3 = (f32[512]{0:T(512)S(1)}, f32[512]{0:T(512)}, u32[]{:S(2)}) copy-start(f32[512]{0:T(512)} %param.7) | copy-start | bytes 6148
  138.5 6.3 %copy-start.4 = (f32[128]{0:T(128)S(1)}, f32[128]{0:T(128)}, u32[]{:S(2)}) copy-start(f32[128]{0:T(128)} %occ_ref.3) | copy-start | bytes 1540
  138.8 21.8 %collective-permute-start.5 = (bf16[2,256,512]{2,1,0:T(8,128)(2,1)S(1)}, bf16[2,256,512]{2,1,0:T(8,128)(2,1)}, u32[]{:S(2)}, u32[]{:S(2)}) collective-permute-start(bf16[2,256,512]{2,1,0:T(8,128)(2,1)S(1)} %get-tuple-element.22), channel_id=1, source_target_pairs={{0,2},{2,0},{1,3},{3,1},{4,6},{6,4},{5,7},{7,5},{8,10},{10,8},{9,1... | collective-permute-start | bytes 1572872 | tf_op jit(solution)/shard_map/ppermute | solution.py:35
  142.2 18.4 %collective-permute-start.1 = (bf16[256,512]{1,0:T(8,128)(2,1)S(1)}, bf16[256,512]{1,0:T(8,128)(2,1)S(1)}, u32[]{:S(2)}, u32[]{:S(2)}) collective-permute-start(bf16[256,512]{1,0:T(8,128)(2,1)S(1)} %get-tuple-element.27), channel_id=1, source_target_pairs={{0,2},{2,0},{1,3},{3,1},{4,6},{6,4},{5,7},{7,5},{8,10},{10,8},{9,1... | collective-permute-start | bytes 786440 | tf_op jit(solution)/shard_map/ppermute | solution.py:35
  147.6 17.1 %all-to-all-start.3 = ((bf16[8,2,16,512]{3,2,1,0:T(8,128)(2,1)}), bf16[8,2,16,512]{3,2,1,0:T(8,128)(2,1)S(1)}, u32[]{:S(2)}, u32[]{:S(2)}) async-start(bf16[8,2,16,512]{3,2,1,0:T(8,128)(2,1)} %get-tuple-element.14), calls=%async_computation.3 | async-start | bytes 524288 | tf_op jit(solution)/shard_map/all_to_all | solution.py:31
  160.7 0.7 copy-start.7
  162.8 33.3 %collective-permute-start.6 = (f32[3,256,512]{2,1,0:T(8,128)S(1)}, f32[3,256,512]{2,1,0:T(8,128)S(1)}, u32[]{:S(2)}, u32[]{:S(2)}) collective-permute-start(f32[3,256,512]{2,1,0:T(8,128)S(1)} %maximum_add_fusion.pair_ref), channel_id=1, source_target_pairs={{0,1},{1,0},{2,3},{3,2},{4,5},{5,4},{6,7},{7,6},{8,9},{9,8},{10,11... | collective-permute-start | bytes 4718600 | tf_op jit(solution)/shard_map/ppermute | solution.py:35
  189.5 12.8 %all-to-all-start.5 = ((bf16[8,16,512]{2,1,0:T(8,128)(2,1)}), bf16[8,16,512]{2,1,0:T(8,128)(2,1)S(1)}, u32[]{:S(2)}, u32[]{:S(2)}) async-start(bf16[8,16,512]{2,1,0:T(8,128)(2,1)} %broadcast_in_dim.23), calls=%async_computation.5 | async-start | bytes 262144 | tf_op jit(solution)/shard_map/all_to_all | solution.py:31

commit v3 on v2

v3 whole, which is shorter than its diff:
```python
import functools

import jax
import jax.numpy as jnp
from jax import lax
from jax.experimental import pallas as pl
from jax.experimental.pallas import tpu as pltpu
from jax.sharding import Mesh
from jax.sharding import PartitionSpec as P

OCC = ("zh", "x", "y")
ROW = 8
SUB = 16
LANES = 128
VMEM = pl.BlockSpec(memory_space=pltpu.VMEM)
SMEM = pl.BlockSpec(memory_space=pltpu.SMEM)
ANY = pl.BlockSpec(memory_space=pl.ANY)
SMALL = pltpu.CompilerParams(vmem_limit_bytes=16 << 20)


def near(value):
    return pltpu.with_memory_space_constraint(value, pltpu.VMEM)


def far(value):
    return pltpu.with_memory_space_constraint(value, pltpu.HBM)


def exchange(value, axis):
    return lax.all_to_all(value, axis, split_axis=0, concat_axis=0, tiled=True)


def swap(value, axis):
    return lax.ppermute(value, axis, [(0, 1), (1, 0)])


def inner(left, right):
    return lax.dot_general(
        left, right, (((1,), (1,)), ((), ())), preferred_element_type=jnp.float32
    )


def to_pieces(block):
    tall, wide = block.shape
    tiles = block.reshape(tall // ROW, ROW, wide // LANES, LANES)
    return tiles.transpose(0, 2, 1, 3).reshape(-1, SUB, LANES)


def roll_kernel(starts_ref, held_ref, out_ref, twice_ref, sems):
    count = held_ref.shape[0]
    twice_ref[:count] = held_ref[...]
    twice_ref[count:] = held_ref[...]
    copies = []
    for k in range(starts_ref.shape[0]):
        copies.append(
            pltpu.make_async_copy(
                twice_ref.at[pl.ds(starts_ref[k], count)],
                out_ref.at[:, pl.ds(k * SUB, SUB), :],
                sems.at[k],
            )
        )
        copies[-1].start()
    for copy in copies:
        copy.wait()


def rolled(starts, held):
    count, sub, lanes = held.shape
    total = starts.shape[0]
    return pl.pallas_call(
        roll_kernel,
        out_shape=pltpu.HBM((count, total * sub, lanes), held.dtype),
        in_specs=[SMEM, VMEM],
        out_specs=ANY,
        compiler_params=SMALL,
        scratch_shapes=[
            pltpu.VMEM((2 * count, sub, lanes), held.dtype),
            pltpu.SemaphoreType.DMA((total,)),
        ],
    )(starts, near(held))


def partial_kernel(
    group, place_ref, own_ref, got_ref, block_ref, kept_ref, sent_ref, held_ref, sem
):
    noff, tall, wide = held_ref.shape
    half = tall // 2
    core = place_ref[1]
    for k in range(noff):
        for c in range(wide // LANES):
            side, at = c * ROW // SUB, (group * noff + k) * SUB + c * ROW % SUB
            tile = got_ref[:, side, at : at + ROW, :]
            held_ref[k, :, c * LANES : (c + 1) * LANES] = tile.reshape(tall, LANES)
    out = pltpu.make_async_copy(held_ref, block_ref, sem)
    out.start()
    mine = own_ref[pl.ds(pl.multiple_of(core * half, half), half), :]
    other = own_ref[pl.ds(pl.multiple_of((1 - core) * half, half), half), :]
    for k in range(noff):
        sent_ref[k] = inner(other, held_ref[k])
        kept_ref[k] = inner(mine, held_ref[k])
    out.wait()


def partials(group, place, own, got):
    tall, wide = own.shape
    noff = got.shape[1] // SUB // 2
    got = got.reshape(tall // ROW, -1, 2 * noff * SUB, LANES)
    half, whole = (noff, tall // 2, tall), (noff, tall, wide)
    return pl.pallas_call(
        functools.partial(partial_kernel, group),
        out_shape=(
            pltpu.HBM(whole, own.dtype),
            jax.ShapeDtypeStruct(half, jnp.float32),
            jax.ShapeDtypeStruct(half, jnp.float32),
        ),
        in_specs=[SMEM, VMEM, VMEM],
        out_specs=(ANY, VMEM, VMEM),
        compiler_params=SMALL,
        scratch_shapes=[pltpu.VMEM(whole, own.dtype), pltpu.SemaphoreType.DMA],
    )(place, own, got)


def amplitude(place_ref, shift, occ_ref, row_ref, pair, there, amp_ref):
    me, core = place_ref[0], place_ref[1]
    half, _ = pair.shape
    energy = occ_ref[me] + occ_ref[lax.rem(me + shift, occ_ref.shape[0])]
    row = row_ref[...]
    for value, place in ((pair, core), (there, 1 - core)):
        start = pl.multiple_of(place * half, half)
        mine = row_ref[:, pl.ds(start, half)]
        column = jnp.broadcast_to(mine, (LANES, half)).T[:, :1]
        amp_ref[pl.ds(start, half), :] = value / (energy - column - row)
    return amp_ref[...]


def ahead_kernel(
    place_ref, shifts_ref, occ_ref, row_ref, pair_ref, there_ref,
    mixed_ref, density_ref, amp_ref, held_ref, sem,
):
    rows = density_ref.shape[0]
    section = 2 * place_ref[2] + place_ref[1]
    at = pl.ds(pl.multiple_of(section * rows, rows), rows)
    total = None
    for k in range(held_ref.shape[0]):
        amp = amplitude(
            place_ref, shifts_ref[k], occ_ref, row_ref, pair_ref[k], there_ref[k], amp_ref
        )
        held_ref[k] = (2.0 * amp - amp.T).astype(held_ref.dtype)
        part = inner(amp_ref[at, :].astype(held_ref.dtype), held_ref[k])
        total = part if total is None else total + part
    out = pltpu.make_async_copy(held_ref, mixed_ref, sem)
    out.start()
    density_ref[...] = total.astype(density_ref.dtype)
    out.wait()


def ahead_pairs(place, shifts, occ, row, pair, there):
    noff, _, nvir = pair.shape
    whole = (noff, nvir, nvir)
    return pl.pallas_call(
        ahead_kernel,
        out_shape=(
            pltpu.HBM(whole, jnp.bfloat16),
            jax.ShapeDtypeStruct((nvir // 4, nvir), jnp.bfloat16),
        ),
        in_specs=[SMEM, SMEM, SMEM, VMEM, VMEM, VMEM],
        out_specs=(ANY, VMEM),
        compiler_params=SMALL,
        scratch_shapes=[
            pltpu.VMEM((nvir, nvir), jnp.float32),
            pltpu.VMEM(whole, jnp.bfloat16),
            pltpu.SemaphoreType.DMA,
        ],
    )(place, shifts, occ, row, near(pair), near(there))


def product_kernel(mixed_ref, block_ref, out_ref):
    total = None
    for k in range(mixed_ref.shape[0]):
        part = jnp.dot(mixed_ref[k], block_ref[k], preferred_element_type=jnp.float32)
        total = part if total is None else total + part
    out_ref[...] = total


def product(mixed, block):
    return pl.pallas_call(
        product_kernel,
        out_shape=pltpu.HBM(block.shape[1:], jnp.float32),
        in_specs=[VMEM, VMEM],
        out_specs=VMEM,
        compiler_params=SMALL,
    )(far(mixed), far(block))


def rest_kernel(
    place_ref, shifts_ref, occ_ref, row_ref, pair_ref, there_ref, blocks_ref, sofar_ref,
    gamma_ref, amp_ref, block_ref, total_ref, sems,
):
    copies = [
        pltpu.make_async_copy(blocks_ref, block_ref, sems.at[0]),
        pltpu.make_async_copy(sofar_ref, total_ref, sems.at[1]),
    ]
    for copy in copies:
        copy.start()
    noff = pair_ref.shape[0]
    for k in range(noff):
        amp = amplitude(
            place_ref, shifts_ref[noff + k], occ_ref, row_ref, pair_ref[k], there_ref[k],
            amp_ref,
        )
        mixed = (2.0 * amp - amp.T).astype(block_ref.dtype)
        if k == 0:
            for copy in copies:
                copy.wait()
        part = jnp.dot(mixed, block_ref[k], preferred_element_type=jnp.float32)
        gamma_ref[...] = (total_ref[...] if k == 0 else gamma_ref[...]) + part


def add_rest(place, shifts, occ, row, pair, there, blocks, sofar):
    nvir = pair.shape[2]
    return pl.pallas_call(
        rest_kernel,
        out_shape=jax.ShapeDtypeStruct(sofar.shape, jnp.float32),
        in_specs=[SMEM, SMEM, SMEM, VMEM, VMEM, VMEM, ANY, ANY],
        out_specs=VMEM,
        compiler_params=SMALL,
        scratch_shapes=[
            pltpu.VMEM((nvir, nvir), jnp.float32),
            pltpu.VMEM(blocks.shape, blocks.dtype),
            pltpu.VMEM(sofar.shape, jnp.float32),
            pltpu.SemaphoreType.DMA((2,)),
        ],
    )(place, shifts, occ, row, pair, there, far(blocks), far(sofar))


def local(factors, offsets, occ_energy, vir_energy):
    count = lax.axis_size(OCC)
    chip = lax.axis_index("zl").astype(jnp.int32)
    core = lax.axis_index("core").astype(jnp.int32)
    place = jnp.stack([lax.axis_index(OCC).astype(jnp.int32), core, chip])
    own = factors[0]
    nvir = own.shape[0]
    rows = nvir // 4
    row = vir_energy[None, :]
    shifts = jnp.concatenate([offsets, count - offsets])

    held = exchange(to_pieces(own), OCC)
    outgoing = rolled(shifts, held)
    got = exchange(outgoing, OCC)

    ahead, kept, sent = partials(0, place, own, got)
    came = swap(sent, "core")
    total = kept + came
    sent = total.astype(jnp.bfloat16)
    came = swap(sent, "zl")
    pair = total + came.astype(jnp.float32)
    there = swap(pair, "core")
    mixed, density = ahead_pairs(place, shifts, occ_energy, row, pair, there)

    behind, kept, sent = partials(1, place, own, got)
    came = swap(sent, "core")
    back = kept + came
    sent = back.astype(jnp.bfloat16)
    came = swap(sent, "zl")
    back, came, _ = lax.optimization_barrier((back, came, density))
    pair = back + came.astype(jnp.float32)
    there = swap(pair, "core")
    sofar = product(mixed, ahead)
    gamma = add_rest(
        place, shifts, occ_energy, row, pair, there, behind, sofar
    )

    came = exchange(density.reshape(count, rows // count, nvir), OCC)
    summed = jnp.sum(came.astype(jnp.float32), axis=0).astype(jnp.bfloat16)
    sent = jnp.broadcast_to(summed, (count, *summed.shape))
    came = exchange(sent, OCC)
    return (gamma[None], came.reshape(rows, nvir).astype(jnp.float32))


def solution(mesh):
    split = Mesh(
        mesh.devices.reshape(4, 4, 8, 2, 2), ("zh", "x", "y", "zl", "core")
    )
    aux = ("zl", "core")

    return jax.shard_map(
        local,
        mesh=split,
        in_specs=(P(OCC, None, aux), P(), P(), P()),
        out_specs=(P(OCC, None, aux), P(aux, None)),
        check_vma=False,
    )
```

time: 204 us -> 202 us (level)
  the two profiles are of different devices: /device:TPU:2 before, /device:TPU:8 now
where the time goes in v3:
time: 202 us
  waiting for transfers between devices  107 us (53%)
  starting transfers between devices  48.6 us (24%)
  blocking collectives  22 us (11%)
  Pallas kernels  16.6 us (8%)
  other arithmetic  4.71 us (2%)
  local copies, waits for them, and re-layouts  2.32 us (1%)
    all_to_all x3, waiting for transfers between devices, exchange(): return lax.all_to_all(value, axis, split_axis=0, concat_axis=0, tiled=True)  84.2 us
    all_to_all x3, starting transfers between devices, exchange(): return lax.all_to_all(value, axis, split_axis=0, concat_axis=0, tiled=True)  33.7 us
    ppermute x6, waiting for transfers between devices, swap(): return lax.ppermute(value, axis, [(0, 1), (1, 0)])  22.4 us
    all_to_all x1, blocking collectives, exchange(): return lax.all_to_all(value, axis, split_axis=0, concat_axis=0, tiled=True)  22 us
    ppermute x6, starting transfers between devices, swap(): return lax.ppermute(value, axis, [(0, 1), (1, 0)])  14.9 us
    pallas_call x2, Pallas kernels, partials(): pl.pallas_call(functools.partial(partial_kernel, group), out_shape=(pltpu...  4.3 us
    pallas_call x1, Pallas kernels, add_rest(): pl.pallas_call(rest_kernel, out_shape=jax.ShapeDtypeStruct(sofar.shape, j...  4.2 us
  transfers between devices with their start and end apart: 9, of which 5 were waited for; matrix products, arithmetic and copies ran while one was open for 3% of the time, Pallas kernels for 4%

profile of v3, /device:TPU:8, one launch (start us, length us, event | category | flops | bytes accessed | tf_op | source)
XLA Modules:
  0.0 201.8 jit_solution(4510486035281439860)
XLA Ops:
  0.6 19.8 %all-to-all-start = ((bf16[128,16,128]{2,1,0:T(8,128)(2,1)}), bf16[128,16,128]{2,1,0:T(8,128)(2,1)S(1)}, u32[]{:S(2)}, u32[]{:S(2)}) async-start(bf16[128,16,128]{2,1,0:T(8,128)(2,1)} %bitcast.18), calls=%async_computation | async-start | bytes 1048576 | tf_op jit(solution)/shard_map/all_to_all | solution.py:30
  21.1 0.7 pad_add_fusion.1.starts_ref.shifts_ref
  21.9 19.7 %all-to-all-done.held_ref = bf16[128,16,128]{2,1,0:T(8,128)(2,1)S(1)} async-done(((bf16[128,16,128]{2,1,0:T(8,128)(2,1)}), bf16[128,16,128]{2,1,0:T(8,128)(2,1)S(1)}, u32[]{:S(2)}, u32[]{:S(2)}) %all-to-all-start) | async-done | bytes 524320 | tf_op jit(solution)/shard_map/all_to_all | solution.py:30
  41.5 2.1 %shard_map.59 = bf16[128,64,128]{2,1,0:T(8,128)(2,1)} custom-call(s32[4]{0:T(128)S(1)} %pad_add_fusion.1.starts_ref.shifts_ref, bf16[128,16,128]{2,1,0:T(8,128)(2,1)S(1)} %all-to-all-done.held_ref), custom_call_target="tpu_custom_call" | custom-call | tf_op jit(solution)/shard_map/pallas_call | solution.py:70
  43.6 7.3 %all-to-all-start.1 = ((bf16[128,64,128]{2,1,0:T(8,128)(2,1)}), bf16[128,64,128]{2,1,0:T(8,128)(2,1)S(1)}, u32[]{:S(2)}, u32[]{:S(2)}) async-start(bf16[128,64,128]{2,1,0:T(8,128)(2,1)} %shard_map.59), calls=%async_computation.1 | async-start | bytes 4194304 | tf_op jit(solution)/shard_map/all_to_all | solution.py:30
  51.0 54.1 %all-to-all-done.1 = bf16[128,64,128]{2,1,0:T(8,128)(2,1)S(1)} async-done(((bf16[128,64,128]{2,1,0:T(8,128)(2,1)}), bf16[128,64,128]{2,1,0:T(8,128)(2,1)S(1)}, u32[]{:S(2)}, u32[]{:S(2)}) %all-to-all-start.1) | async-done | bytes 2097184 | tf_op jit(solution)/shard_map/all_to_all | solution.py:30
  105.1 2.1 %shard_map.61 = (bf16[2,512,512]{2,1,0:T(8,128)(2,1)}, f32[2,256,512]{2,1,0:T(8,128)S(1)}, f32[2,256,512]{2,1,0:T(8,128)S(1)}) custom-call(s32[3]{0:T(128)S(1)} %pad_add_fusion.place_ref, bf16[512,512]{1,0:T(8,128)(2,1)S(1)} %bitcast.19, bf16[64,2,64,128]{3,2,1,0:T(8,128)(2,1)S(1)} %bitcast.16), custom_call_target="tpu_custom_call" | custom-call | tf_op jit(solution)/shard_map/pallas_call | solution.py:109
  107.3 1.9 collective-permute-start.2
  109.2 2.1 %shard_map.60 = (bf16[2,512,512]{2,1,0:T(8,128)(2,1)}, f32[2,256,512]{2,1,0:T(8,128)S(1)}, f32[2,256,512]{2,1,0:T(8,128)S(1)}) custom-call(s32[3]{0:T(128)S(1)} %pad_add_fusion.place_ref, bf16[512,512]{1,0:T(8,128)(2,1)S(1)} %bitcast.20, bf16[64,2,64,128]{3,2,1,0:T(8,128)(2,1)S(1)} %bitcast.17), custom_call_target="tpu_custom_call" | custom-call | tf_op jit(solution)/shard_map/pallas_call | solution.py:109
  111.4 2.4 %collective-permute-start = (f32[2,256,512]{2,1,0:T(8,128)S(1)}, f32[2,256,512]{2,1,0:T(8,128)S(1)}, u32[]{:S(2)}, u32[]{:S(2)}) collective-permute-start(f32[2,256,512]{2,1,0:T(8,128)S(1)} %get-tuple-element.13), channel_id=1, source_target_pairs={{0,1},{1,0},{2,3},{3,2},{4,5},{5,4},{6,7},{7,6},{8,9},{9,8},{10,11... | collective-permute-start | bytes 3145736 | tf_op jit(solution)/shard_map/ppermute | solution.py:34
  114.1 3.4 %collective-permute-start.3 = (bf16[2,256,512]{2,1,0:T(8,128)(2,1)S(1)}, bf16[2,256,512]{2,1,0:T(8,128)(2,1)S(1)}, u32[]{:S(2)}, u32[]{:S(2)}) collective-permute-start(bf16[2,256,512]{2,1,0:T(8,128)(2,1)S(1)} %get-tuple-element.22), channel_id=1, source_target_pairs={{0,2},{2,0},{1,3},{3,1},{4,6},{6,4},{5,7},{7,5},{8,10},{10,8},{9,1... | collective-permute-start | bytes 1572872 | tf_op jit(solution)/shard_map/ppermute | solution.py:34
  117.5 12.3 %collective-permute-done.3 = bf16[2,256,512]{2,1,0:T(8,128)(2,1)S(1)} collective-permute-done((bf16[2,256,512]{2,1,0:T(8,128)(2,1)S(1)}, bf16[2,256,512]{2,1,0:T(8,128)(2,1)S(1)}, u32[]{:S(2)}, u32[]{:S(2)}) %collective-permute-start.3) | collective-permute-done | bytes 524320 | tf_op jit(solution)/shard_map/ppermute | solution.py:34
  130.0 1.9 collective-permute-start.4
  132.2 3.4 %collective-permute-start.1 = (bf16[2,256,512]{2,1,0:T(8,128)(2,1)S(1)}, bf16[2,256,512]{2,1,0:T(8,128)(2,1)S(1)}, u32[]{:S(2)}, u32[]{:S(2)}) collective-permute-start(bf16[2,256,512]{2,1,0:T(8,128)(2,1)S(1)} %get-tuple-element.24), channel_id=1, source_target_pairs={{0,2},{2,0},{1,3},{3,1},{4,6},{6,4},{5,7},{7,5},{8,10},{10,8},{9,1... | collective-permute-start | bytes 1572872 | tf_op jit(solution)/shard_map/ppermute | solution.py:34
  135.7 2.8 %shard_map.62 = (bf16[2,512,512]{2,1,0:T(8,128)(2,1)}, bf16[128,512]{1,0:T(8,128)(2,1)S(1)}) custom-call(s32[3]{0:T(128)S(1)} %pad_add_fusion.place_ref, s32[4]{0:T(128)S(1)} %pad_add_fusion.1.starts_ref.shifts_ref, f32[128]{0:T(128)S(1)} %copy-done.2, f32[1,512]{1,0:T(1,128)S(1)} %bitcast.22, f32[2,256,512]{2,1,0:T(8,128)S(1)} %convert_add_fusion.1.pair_ref, ...), custom_call_target="tpu_custom_call" | custom-call | tf_op jit(solution)/shard_map/pallas_call | solution.py:160
  138.5 10.0 %collective-permute-done.1 = bf16[2,256,512]{2,1,0:T(8,128)(2,1)S(1)} collective-permute-done((bf16[2,256,512]{2,1,0:T(8,128)(2,1)S(1)}, bf16[2,256,512]{2,1,0:T(8,128)(2,1)S(1)}, u32[]{:S(2)}, u32[]{:S(2)}) %collective-permute-start.1) | collective-permute-done | bytes 524320 | tf_op jit(solution)/shard_map/ppermute | solution.py:34
  148.6 1.9 collective-permute-start.5
  151.8 22.0 %all_to_all.20 = bf16[128,2,256]{2,1,0:T(2,128)(2,1)S(1)} all-to-all(bf16[128,2,256]{2,1,0:T(2,128)(2,1)S(1)} %reshape.24), channel_id=1, replica_groups=mesh['zh'=4,'x'=4,'y'=8,'zl'=2,'core'=2] {'zh','x','y'}, dimensions={0} | all-to-all | bytes 262144 | tf_op jit(solution)/shard_map/all_to_all | solution.py:30
  174.3 1.4 reduce.3
  176.4 6.5 %all-to-all-start.3 = ((bf16[128,2,256]{2,1,0:T(2,128)(2,1)}), bf16[128,2,256]{2,1,0:T(2,128)(2,1)S(1)}, u32[]{:S(2)}, u32[]{:S(2)}) async-start(bf16[128,2,256]{2,1,0:T(2,128)(2,1)} %reshape.26), calls=%async_computation.3 | async-start | bytes 262144 | tf_op jit(solution)/shard_map/all_to_all | solution.py:30
  182.9 3.2 %shard_map.63.sofar_ref = f32[512,512]{1,0:T(8,128)} custom-call(bf16[2,512,512]{2,1,0:T(8,128)(2,1)} %get-tuple-element.20.mixed_ref, bf16[2,512,512]{2,1,0:T(8,128)(2,1)} %get-tuple-element.21.block_ref), custom_call_target="tpu_custom_call" | custom-call | tf_op jit(solution)/shard_map/pallas_call | solution.py:186
  186.2 10.4 %all-to-all-done.3 = bf16[128,2,256]{2,1,0:T(2,128)(2,1)S(1)} async-done(((bf16[128,2,256]{2,1,0:T(2,128)(2,1)}), bf16[128,2,256]{2,1,0:T(2,128)(2,1)S(1)}, u32[]{:S(2)}, u32[]{:S(2)}) %all-to-all-start.3) | async-done | bytes 131104 | tf_op jit(solution)/shard_map/all_to_all | solution.py:30
  196.7 0.7 copy.9
  197.4 4.2 %shard_map.64 = f32[512,512]{1,0:T(8,128)} custom-call(s32[3]{0:T(128)S(1)} %pad_add_fusion.place_ref, s32[4]{0:T(128)S(1)} %pad_add_fusion.1.starts_ref.shifts_ref, f32[128]{0:T(128)S(1)} %copy-done.2, f32[1,512]{1,0:T(1,128)S(1)} %bitcast.23, f32[2,256,512]{2,1,0:T(8,128)S(1)} %convert_add_fusion.pair_ref, ...), custom_call_target="tpu_custom_call" | custom-call | tf_op jit(solution)/shard_map/pallas_call | solution.py:221
  (24 shorter events, 4.2 us)
Async XLA Ops:
  0.6 40.9 %all-to-all-start = ((bf16[128,16,128]{2,1,0:T(8,128)(2,1)}), bf16[128,16,128]{2,1,0:T(8,128)(2,1)S(1)}, u32[]{:S(2)}, u32[]{:S(2)}) async-start(bf16[128,16,128]{2,1,0:T(8,128)(2,1)} %bitcast.18), calls=%async_computation | async-start | bytes 1048576 | tf_op jit(solution)/shard_map/all_to_all | solution.py:30
  43.6 61.5 %copy-start = (bf16[1,512,512]{2,1,0:T(8,128)(2,1)S(1)}, bf16[1,512,512]{2,1,0:T(8,128)(2,1)}, u32[]{:S(2)}) copy-start(bf16[1,512,512]{2,1,0:T(8,128)(2,1)} %param.4) | copy-start | bytes 1572868
  43.6 61.5 %all-to-all-start.1 = ((bf16[128,64,128]{2,1,0:T(8,128)(2,1)}), bf16[128,64,128]{2,1,0:T(8,128)(2,1)S(1)}, u32[]{:S(2)}, u32[]{:S(2)}) async-start(bf16[128,64,128]{2,1,0:T(8,128)(2,1)} %shard_map.59), calls=%async_computation.1 | async-start | bytes 4194304 | tf_op jit(solution)/shard_map/all_to_all | solution.py:30
  107.3 6.5 %collective-permute-start.2 = (f32[2,256,512]{2,1,0:T(8,128)S(1)}, f32[2,256,512]{2,1,0:T(8,128)S(1)}, u32[]{:S(2)}, u32[]{:S(2)}) collective-permute-start(f32[2,256,512]{2,1,0:T(8,128)S(1)} %get-tuple-element.15), channel_id=1, source_target_pairs={{0,1},{1,0},{2,3},{3,2},{4,5},{5,4},{6,7},{7,6},{8,9},{9,8},{10,11... | collective-permute-start | bytes 3145736 | tf_op jit(solution)/shard_map/ppermute | solution.py:34
  111.4 20.6 %collective-permute-start = (f32[2,256,512]{2,1,0:T(8,128)S(1)}, f32[2,256,512]{2,1,0:T(8,128)S(1)}, u32[]{:S(2)}, u32[]{:S(2)}) collective-permute-start(f32[2,256,512]{2,1,0:T(8,128)S(1)} %get-tuple-element.13), channel_id=1, source_target_pairs={{0,1},{1,0},{2,3},{3,2},{4,5},{5,4},{6,7},{7,6},{8,9},{9,8},{10,11... | collective-permute-start | bytes 3145736 | tf_op jit(solution)/shard_map/ppermute | solution.py:34
  114.1 15.7 %collective-permute-start.3 = (bf16[2,256,512]{2,1,0:T(8,128)(2,1)S(1)}, bf16[2,256,512]{2,1,0:T(8,128)(2,1)S(1)}, u32[]{:S(2)}, u32[]{:S(2)}) collective-permute-start(bf16[2,256,512]{2,1,0:T(8,128)(2,1)S(1)} %get-tuple-element.22), channel_id=1, source_target_pairs={{0,2},{2,0},{1,3},{3,1},{4,6},{6,4},{5,7},{7,5},{8,10},{10,8},{9,1... | collective-permute-start | bytes 1572872 | tf_op jit(solution)/shard_map/ppermute | solution.py:34
  130.0 5.6 %copy-start.1 = (f32[512]{0:T(512)S(1)}, f32[512]{0:T(512)}, u32[]{:S(2)}) copy-start(f32[512]{0:T(512)} %param.7) | copy-start | bytes 6148
  130.0 5.6 %copy-start.2 = (f32[128]{0:T(128)S(1)}, f32[128]{0:T(128)}, u32[]{:S(2)}) copy-start(f32[128]{0:T(128)} %occ_ref.3) | copy-start | bytes 1540
  130.0 5.6 %collective-permute-start.4 = (f32[2,256,512]{2,1,0:T(8,128)S(1)}, f32[2,256,512]{2,1,0:T(8,128)S(1)}, u32[]{:S(2)}, u32[]{:S(2)}) collective-permute-start(f32[2,256,512]{2,1,0:T(8,128)S(1)} %convert_add_fusion.1.pair_ref), channel_id=1, source_target_pairs={{0,1},{1,0},{2,3},{3,2},{4,5},{5,4},{6,7},{7,6},{8,9},{9,8},{10,11... | collective-permute-start | bytes 3145736 | tf_op jit(solution)/shard_map/ppermute | solution.py:34
  132.2 16.2 %collective-permute-start.1 = (bf16[2,256,512]{2,1,0:T(8,128)(2,1)S(1)}, bf16[2,256,512]{2,1,0:T(8,128)(2,1)S(1)}, u32[]{:S(2)}, u32[]{:S(2)}) collective-permute-start(bf16[2,256,512]{2,1,0:T(8,128)(2,1)S(1)} %get-tuple-element.24), channel_id=1, source_target_pairs={{0,2},{2,0},{1,3},{3,1},{4,6},{6,4},{5,7},{7,5},{8,10},{10,8},{9,1... | collective-permute-start | bytes 1572872 | tf_op jit(solution)/shard_map/ppermute | solution.py:34
  148.6 48.8 %collective-permute-start.5 = (f32[2,256,512]{2,1,0:T(8,128)S(1)}, f32[2,256,512]{2,1,0:T(8,128)S(1)}, u32[]{:S(2)}, u32[]{:S(2)}) collective-permute-start(f32[2,256,512]{2,1,0:T(8,128)S(1)} %convert_add_fusion.pair_ref), channel_id=1, source_target_pairs={{0,1},{1,0},{2,3},{3,2},{4,5},{5,4},{6,7},{7,6},{8,9},{9,8},{10,11... | collective-permute-start | bytes 3145736 | tf_op jit(solution)/shard_map/ppermute | solution.py:34
  176.4 20.2 %all-to-all-start.3 = ((bf16[128,2,256]{2,1,0:T(2,128)(2,1)}), bf16[128,2,256]{2,1,0:T(2,128)(2,1)S(1)}, u32[]{:S(2)}, u32[]{:S(2)}) async-start(bf16[128,2,256]{2,1,0:T(2,128)(2,1)} %reshape.26), calls=%async_computation.3 | async-start | bytes 262144 | tf_op jit(solution)/shard_map/all_to_all | solution.py:30

commit v4 on v3

--- a/solution.py
+++ b/solution.py
@@ -137,7 +137,8 @@
     place_ref, shifts_ref, occ_ref, row_ref, pair_ref, there_ref,
     mixed_ref, density_ref, amp_ref, held_ref, sem,
 ):
-    rows = density_ref.shape[0]
+    groups, cols, deep, lanes = density_ref.shape
+    rows = groups * deep
     section = 2 * place_ref[2] + place_ref[1]
     at = pl.ds(pl.multiple_of(section * rows, rows), rows)
     total = None
@@ -150,7 +151,9 @@
         total = part if total is None else total + part
     out = pltpu.make_async_copy(held_ref, mixed_ref, sem)
     out.start()
-    density_ref[...] = total.astype(density_ref.dtype)
+    for c in range(cols):
+        tile = total[:, c * lanes : (c + 1) * lanes].reshape(groups, deep, lanes)
+        density_ref[:, c] = tile.astype(density_ref.dtype)
     out.wait()
 
 
@@ -161,7 +164,7 @@
         ahead_kernel,
         out_shape=(
             pltpu.HBM(whole, jnp.bfloat16),
-            jax.ShapeDtypeStruct((nvir // 4, nvir), jnp.bfloat16),
+            jax.ShapeDtypeStruct((nvir // 16, nvir // LANES, 4, LANES), jnp.bfloat16),
         ),
         in_specs=[SMEM, SMEM, SMEM, VMEM, VMEM, VMEM],
         out_specs=(ANY, VMEM),
@@ -174,35 +177,18 @@
     )(place, shifts, occ, row, near(pair), near(there))
 
 
-def product_kernel(mixed_ref, block_ref, out_ref):
-    total = None
-    for k in range(mixed_ref.shape[0]):
-        part = jnp.dot(mixed_ref[k], block_ref[k], preferred_element_type=jnp.float32)
-        total = part if total is None else total + part
-    out_ref[...] = total
-
-
-def product(mixed, block):
-    return pl.pallas_call(
-        product_kernel,
-        out_shape=pltpu.HBM(block.shape[1:], jnp.float32),
-        in_specs=[VMEM, VMEM],
-        out_specs=VMEM,
-        compiler_params=SMALL,
-    )(far(mixed), far(block))
-
-
-def rest_kernel(
-    place_ref, shifts_ref, occ_ref, row_ref, pair_ref, there_ref, blocks_ref, sofar_ref,
-    gamma_ref, amp_ref, block_ref, total_ref, sems,
+def gamma_kernel(
+    place_ref, shifts_ref, occ_ref, row_ref, pair_ref, there_ref, mixed_ref, ahead_ref,
+    behind_ref, gamma_ref, amp_ref, first_ref, block_ref, sems,
 ):
+    noff = pair_ref.shape[0]
     copies = [
-        pltpu.make_async_copy(blocks_ref, block_ref, sems.at[0]),
-        pltpu.make_async_copy(sofar_ref, total_ref, sems.at[1]),
+        pltpu.make_async_copy(mixed_ref, first_ref, sems.at[0]),
+        pltpu.make_async_copy(ahead_ref, block_ref.at[pl.ds(0, noff)], sems.at[1]),
+        pltpu.make_async_copy(behind_ref, block_ref.at[pl.ds(noff, noff)], sems.at[2]),
     ]
     for copy in copies:
         copy.start()
-    noff = pair_ref.shape[0]
     for k in range(noff):
         amp = amplitude(
             place_ref, shifts_ref[noff + k], occ_ref, row_ref, pair_ref[k], there_ref[k],
@@ -212,25 +198,44 @@
         if k == 0:
             for copy in copies:
                 copy.wait()
-        part = jnp.dot(mixed, block_ref[k], preferred_element_type=jnp.float32)
-        gamma_ref[...] = (total_ref[...] if k == 0 else gamma_ref[...]) + part
-
-
-def add_rest(place, shifts, occ, row, pair, there, blocks, sofar):
-    nvir = pair.shape[2]
-    return pl.pallas_call(
-        rest_kernel,
-        out_shape=jax.ShapeDtypeStruct(sofar.shape, jnp.float32),
-        in_specs=[SMEM, SMEM, SMEM, VMEM, VMEM, VMEM, ANY, ANY],
+        part = jnp.dot(mixed, block_ref[noff + k], preferred_element_type=jnp.float32)
+        part += jnp.dot(first_ref[k], block_ref[k], preferred_element_type=jnp.float32)
+        gamma_ref[...] = part if k == 0 else gamma_ref[...] + part
+
+
+def gamma_of(place, shifts, occ, row, pair, there, mixed, ahead, behind):
+    noff, nvir, wide = ahead.shape
+    return pl.pallas_call(
+        gamma_kernel,
+        out_shape=jax.ShapeDtypeStruct((nvir, wide), jnp.float32),
+        in_specs=[SMEM, SMEM, SMEM, VMEM, VMEM, VMEM, ANY, ANY, ANY],
         out_specs=VMEM,
         compiler_params=SMALL,
         scratch_shapes=[
             pltpu.VMEM((nvir, nvir), jnp.float32),
-            pltpu.VMEM(blocks.shape, blocks.dtype),
-            pltpu.VMEM(sofar.shape, jnp.float32),
-            pltpu.SemaphoreType.DMA((2,)),
+            pltpu.VMEM(mixed.shape, mixed.dtype),
+            pltpu.VMEM((2 * noff, nvir, wide), ahead.dtype),
+            pltpu.SemaphoreType.DMA((3,)),
         ],
-    )(place, shifts, occ, row, pair, there, far(blocks), far(sofar))
+    )(place, shifts, occ, row, pair, there, far(mixed), far(ahead), far(behind))
+
+
+def lines_kernel(tiles_ref, out_ref):
+    groups, cols, deep, lanes = tiles_ref.shape
+    for c in range(cols):
+        tile = tiles_ref[:, c].astype(out_ref.dtype)
+        out_ref[:, c * lanes : (c + 1) * lanes] = tile.reshape(groups * deep, lanes)
+
+
+def to_lines(tiles):
+    groups, cols, deep, lanes = tiles.shape
+    return pl.pallas_call(
+        lines_kernel,
+        out_shape=jax.ShapeDtypeStruct((groups * deep, cols * lanes), jnp.float32),
+        in_specs=[VMEM],
+        out_specs=VMEM,
+        compiler_params=SMALL,
+    )(near(tiles))
 
 
 def local(factors, offsets, occ_energy, vir_energy):
@@ -239,8 +244,6 @@
     core = lax.axis_index("core").astype(jnp.int32)
     place = jnp.stack([lax.axis_index(OCC).astype(jnp.int32), core, chip])
     own = factors[0]
-    nvir = own.shape[0]
-    rows = nvir // 4
     row = vir_energy[None, :]
     shifts = jnp.concatenate([offsets, count - offsets])
 
@@ -262,19 +265,15 @@
     back = kept + came
     sent = back.astype(jnp.bfloat16)
     came = swap(sent, "zl")
-    back, came, _ = lax.optimization_barrier((back, came, density))
     pair = back + came.astype(jnp.float32)
     there = swap(pair, "core")
-    sofar = product(mixed, ahead)
-    gamma = add_rest(
-        place, shifts, occ_energy, row, pair, there, behind, sofar
-    )
-
-    came = exchange(density.reshape(count, rows // count, nvir), OCC)
+    gamma = gamma_of(place, shifts, occ_energy, row, pair, there, mixed, ahead, behind)
+
+    came = exchange(density.reshape(count, -1, LANES), OCC)
     summed = jnp.sum(came.astype(jnp.float32), axis=0).astype(jnp.bfloat16)
     sent = jnp.broadcast_to(summed, (count, *summed.shape))
     came = exchange(sent, OCC)
-    return (gamma[None], came.reshape(rows, nvir).astype(jnp.float32))
+    return (gamma[None], to_lines(came.reshape(density.shape)))
 
 
 def solution(mesh):

time: 202 us -> 190 us (0.941)
  waiting for transfers between devices: 107 us -> 101 us
  other arithmetic: 4.71 us -> 2.47 us
    ppermute x6, waiting for transfers between devices: 22.4 us -> 18.7 us  [swap(): return lax.ppermute(value, axis, [(0, 1), (1, 0)])]
  transfers between devices with their start and end apart: 9 -> 9, of which waited for: 5 -> 5; matrix products, arithmetic and copies ran while one was open for 3% -> 2% of each run, Pallas kernels for 4% -> 5%
where the time goes in v4:
time: 190 us
  waiting for transfers between devices  101 us (53%)
  starting transfers between devices  47.5 us (25%)
  blocking collectives  22 us (12%)
  Pallas kernels  14.9 us (8%)
  other arithmetic  2.47 us (1%)
    all_to_all x3, waiting for transfers between devices, exchange(): return lax.all_to_all(value, axis, split_axis=0, concat_axis=0, tiled=True)  82.5 us
    all_to_all x3, starting transfers between devices, exchange(): return lax.all_to_all(value, axis, split_axis=0, concat_axis=0, tiled=True)  33.5 us
    all_to_all x1, blocking collectives, exchange(): return lax.all_to_all(value, axis, split_axis=0, concat_axis=0, tiled=True)  22 us
    ppermute x6, waiting for transfers between devices, swap(): return lax.ppermute(value, axis, [(0, 1), (1, 0)])  18.7 us
    ppermute x6, starting transfers between devices, swap(): return lax.ppermute(value, axis, [(0, 1), (1, 0)])  14 us
    pallas_call x1, Pallas kernels, gamma_of(): pl.pallas_call(gamma_kernel, out_shape=jax.ShapeDtypeStruct((nvir, wide),...  4.95 us
    pallas_call x2, Pallas kernels, partials(): pl.pallas_call(functools.partial(partial_kernel, group), out_shape=(pltpu...  4.33 us
  transfers between devices with their start and end apart: 9, of which 5 were waited for; matrix products, arithmetic and copies ran while one was open for 2% of the time, Pallas kernels for 5%

profile of v4, /device:TPU:8, one launch (start us, length us, event | category | flops | bytes accessed | tf_op | source)
XLA Modules:
  0.0 189.6 jit_solution(12567507980737159884)
XLA Ops:
  0.6 19.8 %all-to-all-start = ((bf16[128,16,128]{2,1,0:T(8,128)(2,1)}), bf16[128,16,128]{2,1,0:T(8,128)(2,1)S(1)}, u32[]{:S(2)}, u32[]{:S(2)}) async-start(bf16[128,16,128]{2,1,0:T(8,128)(2,1)} %bitcast.16), calls=%async_computation | async-start | bytes 1048576 | tf_op jit(solution)/shard_map/all_to_all | solution.py:30
  20.5 0.7 broadcast_subtract_fusion
  21.1 0.7 pad_add_fusion.1.starts_ref.shifts_ref
  21.9 19.7 %all-to-all-done.held_ref = bf16[128,16,128]{2,1,0:T(8,128)(2,1)S(1)} async-done(((bf16[128,16,128]{2,1,0:T(8,128)(2,1)}), bf16[128,16,128]{2,1,0:T(8,128)(2,1)S(1)}, u32[]{:S(2)}, u32[]{:S(2)}) %all-to-all-start) | async-done | bytes 524320 | tf_op jit(solution)/shard_map/all_to_all | solution.py:30
  41.5 2.1 %shard_map.59 = bf16[128,64,128]{2,1,0:T(8,128)(2,1)} custom-call(s32[4]{0:T(128)S(1)} %pad_add_fusion.1.starts_ref.shifts_ref, bf16[128,16,128]{2,1,0:T(8,128)(2,1)S(1)} %all-to-all-done.held_ref), custom_call_target="tpu_custom_call" | custom-call | tf_op jit(solution)/shard_map/pallas_call | solution.py:70
  43.6 7.3 %all-to-all-start.1 = ((bf16[128,64,128]{2,1,0:T(8,128)(2,1)}), bf16[128,64,128]{2,1,0:T(8,128)(2,1)S(1)}, u32[]{:S(2)}, u32[]{:S(2)}) async-start(bf16[128,64,128]{2,1,0:T(8,128)(2,1)} %shard_map.59), calls=%async_computation.1 | async-start | bytes 4194304 | tf_op jit(solution)/shard_map/all_to_all | solution.py:30
  51.0 54.1 %all-to-all-done.1 = bf16[128,64,128]{2,1,0:T(8,128)(2,1)S(1)} async-done(((bf16[128,64,128]{2,1,0:T(8,128)(2,1)}), bf16[128,64,128]{2,1,0:T(8,128)(2,1)S(1)}, u32[]{:S(2)}, u32[]{:S(2)}) %all-to-all-start.1) | async-done | bytes 2097184 | tf_op jit(solution)/shard_map/all_to_all | solution.py:30
  105.2 2.2 %shard_map.61 = (bf16[2,512,512]{2,1,0:T(8,128)(2,1)}, f32[2,256,512]{2,1,0:T(8,128)S(1)}, f32[2,256,512]{2,1,0:T(8,128)S(1)}) custom-call(s32[3]{0:T(128)S(1)} %pad_add_fusion.place_ref, bf16[512,512]{1,0:T(8,128)(2,1)S(1)} %bitcast.17, bf16[64,2,64,128]{3,2,1,0:T(8,128)(2,1)S(1)} %bitcast.14), custom_call_target="tpu_custom_call" | custom-call | tf_op jit(solution)/shard_map/pallas_call | solution.py:109
  107.3 1.9 %collective-permute-start.3 = (f32[2,256,512]{2,1,0:T(8,128)S(1)}, f32[2,256,512]{2,1,0:T(8,128)S(1)}, u32[]{:S(2)}, u32[]{:S(2)}) collective-permute-start(f32[2,256,512]{2,1,0:T(8,128)S(1)} %get-tuple-element.13), channel_id=1, source_target_pairs={{0,1},{1,0},{2,3},{3,2},{4,5},{5,4},{6,7},{7,6},{8,9},{9,8},{10,11... | collective-permute-start | bytes 3145736 | tf_op jit(solution)/shard_map/ppermute | solution.py:34
  109.3 2.2 %shard_map.60 = (bf16[2,512,512]{2,1,0:T(8,128)(2,1)}, f32[2,256,512]{2,1,0:T(8,128)S(1)}, f32[2,256,512]{2,1,0:T(8,128)S(1)}) custom-call(s32[3]{0:T(128)S(1)} %pad_add_fusion.place_ref, bf16[512,512]{1,0:T(8,128)(2,1)S(1)} %bitcast.18, bf16[64,2,64,128]{3,2,1,0:T(8,128)(2,1)S(1)} %bitcast.15), custom_call_target="tpu_custom_call" | custom-call | tf_op jit(solution)/shard_map/pallas_call | solution.py:109
  111.4 2.4 %collective-permute-start = (f32[2,256,512]{2,1,0:T(8,128)S(1)}, f32[2,256,512]{2,1,0:T(8,128)S(1)}, u32[]{:S(2)}, u32[]{:S(2)}) collective-permute-start(f32[2,256,512]{2,1,0:T(8,128)S(1)} %get-tuple-element.11), channel_id=1, source_target_pairs={{0,1},{1,0},{2,3},{3,2},{4,5},{5,4},{6,7},{7,6},{8,9},{9,8},{10,11... | collective-permute-start | bytes 3145736 | tf_op jit(solution)/shard_map/ppermute | solution.py:34
  114.1 3.4 %collective-permute-start.4 = (bf16[2,256,512]{2,1,0:T(8,128)(2,1)S(1)}, bf16[2,256,512]{2,1,0:T(8,128)(2,1)S(1)}, u32[]{:S(2)}, u32[]{:S(2)}) collective-permute-start(bf16[2,256,512]{2,1,0:T(8,128)(2,1)S(1)} %get-tuple-element.18), channel_id=1, source_target_pairs={{0,2},{2,0},{1,3},{3,1},{4,6},{6,4},{5,7},{7,5},{8,10},{10,8},{9,1... | collective-permute-start | bytes 1572872 | tf_op jit(solution)/shard_map/ppermute | solution.py:34
  117.8 2.5 %collective-permute-start.1 = (bf16[2,256,512]{2,1,0:T(8,128)(2,1)S(1)}, bf16[2,256,512]{2,1,0:T(8,128)(2,1)S(1)}, u32[]{:S(2)}, u32[]{:S(2)}) collective-permute-start(bf16[2,256,512]{2,1,0:T(8,128)(2,1)S(1)} %get-tuple-element.20), channel_id=1, source_target_pairs={{0,2},{2,0},{1,3},{3,1},{4,6},{6,4},{5,7},{7,5},{8,10},{10,8},{9,1... | collective-permute-start | bytes 1572872 | tf_op jit(solution)/shard_map/ppermute | solution.py:34
  120.3 10.6 %collective-permute-done.4 = bf16[2,256,512]{2,1,0:T(8,128)(2,1)S(1)} collective-permute-done((bf16[2,256,512]{2,1,0:T(8,128)(2,1)S(1)}, bf16[2,256,512]{2,1,0:T(8,128)(2,1)S(1)}, u32[]{:S(2)}, u32[]{:S(2)}) %collective-permute-start.4) | collective-permute-done | bytes 524320 | tf_op jit(solution)/shard_map/ppermute | solution.py:34
  131.0 1.9 %collective-permute-start.5 = (f32[2,256,512]{2,1,0:T(8,128)S(1)}, f32[2,256,512]{2,1,0:T(8,128)S(1)}, u32[]{:S(2)}, u32[]{:S(2)}) collective-permute-start(f32[2,256,512]{2,1,0:T(8,128)S(1)} %convert_add_fusion.pair_ref), channel_id=1, source_target_pairs={{0,1},{1,0},{2,3},{3,2},{4,5},{5,4},{6,7},{7,6},{8,9},{9,8},{10,11... | collective-permute-start | bytes 3145736 | tf_op jit(solution)/shard_map/ppermute | solution.py:34
  132.9 8.2 %collective-permute-done.1 = bf16[2,256,512]{2,1,0:T(8,128)(2,1)S(1)} collective-permute-done((bf16[2,256,512]{2,1,0:T(8,128)(2,1)S(1)}, bf16[2,256,512]{2,1,0:T(8,128)(2,1)S(1)}, u32[]{:S(2)}, u32[]{:S(2)}) %collective-permute-start.1) | collective-permute-done | bytes 524320 | tf_op jit(solution)/shard_map/ppermute | solution.py:34
  141.3 1.9 %collective-permute-start.2 = (f32[2,256,512]{2,1,0:T(8,128)S(1)}, f32[2,256,512]{2,1,0:T(8,128)S(1)}, u32[]{:S(2)}, u32[]{:S(2)}) collective-permute-start(f32[2,256,512]{2,1,0:T(8,128)S(1)} %convert_add_fusion.1.pair_ref), channel_id=1, source_target_pairs={{0,1},{1,0},{2,3},{3,2},{4,5},{5,4},{6,7},{7,6},{8,9},{9,8},{10,11... | collective-permute-start | bytes 3145736 | tf_op jit(solution)/shard_map/ppermute | solution.py:34
  143.2 2.8 %shard_map.62 = (bf16[2,512,512]{2,1,0:T(8,128)(2,1)}, bf16[32,4,4,128]{3,2,1,0:T(4,128)(2,1)S(1)}) custom-call(s32[3]{0:T(128)S(1)} %pad_add_fusion.place_ref, s32[4]{0:T(128)S(1)} %pad_add_fusion.1.starts_ref.shifts_ref, f32[128]{0:T(128)S(1)} %copy-done.2, f32[1,512]{1,0:T(1,128)S(1)} %bitcast.21, f32[2,256,512]{2,1,0:T(8,128)S(1)} %convert_add_fusion.pair_ref, ...), custom_call_target="tpu_custom_call" | custom-call | tf_op jit(solution)/shard_map/pallas_call | solution.py:163
  146.0 22.0 %all_to_all.20 = bf16[128,4,128]{2,1,0:T(4,128)(2,1)S(1)} all-to-all(bf16[128,4,128]{2,1,0:T(4,128)(2,1)S(1)} %bitcast.20), channel_id=1, replica_groups=mesh['zh'=4,'x'=4,'y'=8,'zl'=2,'core'=2] {'zh','x','y'}, dimensions={0} | all-to-all | bytes 262144 | tf_op jit(solution)/shard_map/all_to_all | solution.py:30
  168.1 0.7 broadcast_in_dim.11
  168.8 6.3 %all-to-all-start.3 = ((bf16[128,4,128]{2,1,0:T(4,128)(2,1)}), bf16[128,4,128]{2,1,0:T(4,128)(2,1)S(1)}, u32[]{:S(2)}, u32[]{:S(2)}) async-start(bf16[128,4,128]{2,1,0:T(4,128)(2,1)} %broadcast_in_dim.11), calls=%async_computation.3 | async-start | bytes 262144 | tf_op jit(solution)/shard_map/all_to_all | solution.py:30
  175.2 4.9 %shard_map.63 = f32[512,512]{1,0:T(8,128)} custom-call(s32[3]{0:T(128)S(1)} %pad_add_fusion.place_ref, s32[4]{0:T(128)S(1)} %pad_add_fusion.1.starts_ref.shifts_ref, f32[128]{0:T(128)S(1)} %copy-done.2, f32[1,512]{1,0:T(1,128)S(1)} %bitcast.22, f32[2,256,512]{2,1,0:T(8,128)S(1)} %convert_add_fusion.1.pair_ref, ...), custom_call_target="tpu_custom_call" | custom-call | tf_op jit(solution)/shard_map/pallas_call | solution.py:208
  180.1 8.7 %all-to-all-done.3 = bf16[128,4,128]{2,1,0:T(4,128)(2,1)S(1)} async-done(((bf16[128,4,128]{2,1,0:T(4,128)(2,1)}), bf16[128,4,128]{2,1,0:T(4,128)(2,1)S(1)}, u32[]{:S(2)}, u32[]{:S(2)}) %all-to-all-start.3) | async-done | bytes 131104 | tf_op jit(solution)/shard_map/all_to_all | solution.py:30
  188.8 0.7 shard_map.64
  (16 shorter events, 1.1 us)
Async XLA Ops:
  0.6 40.9 %all-to-all-start = ((bf16[128,16,128]{2,1,0:T(8,128)(2,1)}), bf16[128,16,128]{2,1,0:T(8,128)(2,1)S(1)}, u32[]{:S(2)}, u32[]{:S(2)}) async-start(bf16[128,16,128]{2,1,0:T(8,128)(2,1)} %bitcast.16), calls=%async_computation | async-start | bytes 1048576 | tf_op jit(solution)/shard_map/all_to_all | solution.py:30
  43.6 61.5 %copy-start = (bf16[1,512,512]{2,1,0:T(8,128)(2,1)S(1)}, bf16[1,512,512]{2,1,0:T(8,128)(2,1)}, u32[]{:S(2)}) copy-start(bf16[1,512,512]{2,1,0:T(8,128)(2,1)} %param.4) | copy-start | bytes 1572868
  43.6 61.5 %all-to-all-start.1 = ((bf16[128,64,128]{2,1,0:T(8,128)(2,1)}), bf16[128,64,128]{2,1,0:T(8,128)(2,1)S(1)}, u32[]{:S(2)}, u32[]{:S(2)}) async-start(bf16[128,64,128]{2,1,0:T(8,128)(2,1)} %shard_map.59), calls=%async_computation.1 | async-start | bytes 4194304 | tf_op jit(solution)/shard_map/all_to_all | solution.py:30
  107.3 6.5 %collective-permute-start.3 = (f32[2,256,512]{2,1,0:T(8,128)S(1)}, f32[2,256,512]{2,1,0:T(8,128)S(1)}, u32[]{:S(2)}, u32[]{:S(2)}) collective-permute-start(f32[2,256,512]{2,1,0:T(8,128)S(1)} %get-tuple-element.13), channel_id=1, source_target_pairs={{0,1},{1,0},{2,3},{3,2},{4,5},{5,4},{6,7},{7,6},{8,9},{9,8},{10,11... | collective-permute-start | bytes 3145736 | tf_op jit(solution)/shard_map/ppermute | solution.py:34
  111.4 6.1 %collective-permute-start = (f32[2,256,512]{2,1,0:T(8,128)S(1)}, f32[2,256,512]{2,1,0:T(8,128)S(1)}, u32[]{:S(2)}, u32[]{:S(2)}) collective-permute-start(f32[2,256,512]{2,1,0:T(8,128)S(1)} %get-tuple-element.11), channel_id=1, source_target_pairs={{0,1},{1,0},{2,3},{3,2},{4,5},{5,4},{6,7},{7,6},{8,9},{9,8},{10,11... | collective-permute-start | bytes 3145736 | tf_op jit(solution)/shard_map/ppermute | solution.py:34
  114.1 16.7 %collective-permute-start.4 = (bf16[2,256,512]{2,1,0:T(8,128)(2,1)S(1)}, bf16[2,256,512]{2,1,0:T(8,128)(2,1)S(1)}, u32[]{:S(2)}, u32[]{:S(2)}) collective-permute-start(bf16[2,256,512]{2,1,0:T(8,128)(2,1)S(1)} %get-tuple-element.18), channel_id=1, source_target_pairs={{0,2},{2,0},{1,3},{3,1},{4,6},{6,4},{5,7},{7,5},{8,10},{10,8},{9,1... | collective-permute-start | bytes 1572872 | tf_op jit(solution)/shard_map/ppermute | solution.py:34
  117.8 23.3 %collective-permute-start.1 = (bf16[2,256,512]{2,1,0:T(8,128)(2,1)S(1)}, bf16[2,256,512]{2,1,0:T(8,128)(2,1)S(1)}, u32[]{:S(2)}, u32[]{:S(2)}) collective-permute-start(bf16[2,256,512]{2,1,0:T(8,128)(2,1)S(1)} %get-tuple-element.20), channel_id=1, source_target_pairs={{0,2},{2,0},{1,3},{3,1},{4,6},{6,4},{5,7},{7,5},{8,10},{10,8},{9,1... | collective-permute-start | bytes 1572872 | tf_op jit(solution)/shard_map/ppermute | solution.py:34
  130.8 12.4 %copy-start.1 = (f32[512]{0:T(512)S(1)}, f32[512]{0:T(512)}, u32[]{:S(2)}) copy-start(f32[512]{0:T(512)} %param.7) | copy-start | bytes 6148
  130.8 12.4 %copy-start.2 = (f32[128]{0:T(128)S(1)}, f32[128]{0:T(128)}, u32[]{:S(2)}) copy-start(f32[128]{0:T(128)} %occ_ref.3) | copy-start | bytes 1540
  131.0 12.2 %collective-permute-start.5 = (f32[2,256,512]{2,1,0:T(8,128)S(1)}, f32[2,256,512]{2,1,0:T(8,128)S(1)}, u32[]{:S(2)}, u32[]{:S(2)}) collective-permute-start(f32[2,256,512]{2,1,0:T(8,128)S(1)} %convert_add_fusion.pair_ref), channel_id=1, source_target_pairs={{0,1},{1,0},{2,3},{3,2},{4,5},{5,4},{6,7},{7,6},{8,9},{9,8},{10,11... | collective-permute-start | bytes 3145736 | tf_op jit(solution)/shard_map/ppermute | solution.py:34
  141.3 33.9 %collective-permute-start.2 = (f32[2,256,512]{2,1,0:T(8,128)S(1)}, f32[2,256,512]{2,1,0:T(8,128)S(1)}, u32[]{:S(2)}, u32[]{:S(2)}) collective-permute-start(f32[2,256,512]{2,1,0:T(8,128)S(1)} %convert_add_fusion.1.pair_ref), channel_id=1, source_target_pairs={{0,1},{1,0},{2,3},{3,2},{4,5},{5,4},{6,7},{7,6},{8,9},{9,8},{10,11... | collective-permute-start | bytes 3145736 | tf_op jit(solution)/shard_map/ppermute | solution.py:34
  168.8 20.0 %all-to-all-start.3 = ((bf16[128,4,128]{2,1,0:T(4,128)(2,1)}), bf16[128,4,128]{2,1,0:T(4,128)(2,1)S(1)}, u32[]{:S(2)}, u32[]{:S(2)}) async-start(bf16[128,4,128]{2,1,0:T(4,128)(2,1)} %broadcast_in_dim.11), calls=%async_computation.3 | async-start | bytes 262144 | tf_op jit(solution)/shard_map/all_to_all | solution.py:30

commit v5 on v4

--- a/solution.py
+++ b/solution.py
@@ -120,104 +120,138 @@
     )(place, own, got)
 
 
-def amplitude(place_ref, shift, occ_ref, row_ref, pair, there, amp_ref):
+def half_kernel(
+    first, place_ref, shifts_ref, occ_ref, row_ref, total_ref, came_ref, amp_ref
+):
+    pairs, half, _ = amp_ref.shape
     me, core = place_ref[0], place_ref[1]
-    half, _ = pair.shape
-    energy = occ_ref[me] + occ_ref[lax.rem(me + shift, occ_ref.shape[0])]
     row = row_ref[...]
-    for value, place in ((pair, core), (there, 1 - core)):
-        start = pl.multiple_of(place * half, half)
-        mine = row_ref[:, pl.ds(start, half)]
-        column = jnp.broadcast_to(mine, (LANES, half)).T[:, :1]
-        amp_ref[pl.ds(start, half), :] = value / (energy - column - row)
+    mine = row_ref[:, pl.ds(pl.multiple_of(core * half, half), half)]
+    column = jnp.broadcast_to(mine, (LANES, half)).T[:, :1]
+    for k in range(pairs):
+        shift = shifts_ref[first + k]
+        energy = occ_ref[me] + occ_ref[lax.rem(me + shift, occ_ref.shape[0])]
+        at = (first + k) % total_ref.shape[0]
+        pair = total_ref[at] + came_ref[k].astype(jnp.float32)
+        amp_ref[k] = pair / (energy - column - row)
+
+
+def half_amplitudes(first, place, shifts, occ, row, total, came):
+    return pl.pallas_call(
+        functools.partial(half_kernel, first),
+        out_shape=jax.ShapeDtypeStruct(came.shape, jnp.float32),
+        in_specs=[SMEM, SMEM, SMEM, VMEM, VMEM, VMEM],
+        out_specs=VMEM,
+        compiler_params=SMALL,
+    )(place, shifts, occ, row, near(total), near(came))
+
+
+def whole_of(place_ref, mine, there, amp_ref):
+    half = mine.shape[0]
+    core = place_ref[1]
+    amp_ref[pl.ds(pl.multiple_of(core * half, half), half), :] = mine
+    amp_ref[pl.ds(pl.multiple_of((1 - core) * half, half), half), :] = there
     return amp_ref[...]
 
 
-def ahead_kernel(
-    place_ref, shifts_ref, occ_ref, row_ref, pair_ref, there_ref,
-    mixed_ref, density_ref, amp_ref, held_ref, sem,
-):
-    groups, cols, deep, lanes = density_ref.shape
-    rows = groups * deep
+def mixed_of(amp):
+    return (2.0 * amp - amp.T).astype(jnp.bfloat16)
+
+
+def density_of(place_ref, amp_ref, mixed, rows):
     section = 2 * place_ref[2] + place_ref[1]
     at = pl.ds(pl.multiple_of(section * rows, rows), rows)
-    total = None
-    for k in range(held_ref.shape[0]):
-        amp = amplitude(
-            place_ref, shifts_ref[k], occ_ref, row_ref, pair_ref[k], there_ref[k], amp_ref
-        )
-        held_ref[k] = (2.0 * amp - amp.T).astype(held_ref.dtype)
-        part = inner(amp_ref[at, :].astype(held_ref.dtype), held_ref[k])
-        total = part if total is None else total + part
+    return inner(amp_ref[at, :].astype(mixed.dtype), mixed)
+
+
+def first_kernel(
+    place_ref, mine_ref, there_ref, mixed_ref, density_ref, amp_ref, held_ref, sem
+):
+    held_ref[...] = mixed_of(whole_of(place_ref, mine_ref[0], there_ref[0], amp_ref))
     out = pltpu.make_async_copy(held_ref, mixed_ref, sem)
     out.start()
+    density_ref[...] = density_of(
+        place_ref, amp_ref, held_ref[...], density_ref.shape[0]
+    )
+    out.wait()
+
+
+def second_kernel(
+    place_ref, mine_ref, there_ref, sofar_ref, mixed_ref, density_ref, amp_ref, held_ref,
+    sem,
+):
+    groups, cols, deep, lanes = density_ref.shape
+    held_ref[...] = mixed_of(whole_of(place_ref, mine_ref[0], there_ref[0], amp_ref))
+    out = pltpu.make_async_copy(held_ref, mixed_ref, sem)
+    out.start()
+    total = sofar_ref[...] + density_of(
+        place_ref, amp_ref, held_ref[...], sofar_ref.shape[0]
+    )
     for c in range(cols):
         tile = total[:, c * lanes : (c + 1) * lanes].reshape(groups, deep, lanes)
         density_ref[:, c] = tile.astype(density_ref.dtype)
     out.wait()
 
 
-def ahead_pairs(place, shifts, occ, row, pair, there):
-    noff, _, nvir = pair.shape
-    whole = (noff, nvir, nvir)
-    return pl.pallas_call(
-        ahead_kernel,
+def mix(place, mine, there, *sofar):
+    nvir = mine.shape[2]
+    lines = jax.ShapeDtypeStruct((nvir // 4, nvir), jnp.float32)
+    tiles = jax.ShapeDtypeStruct((nvir // 16, nvir // LANES, 4, LANES), jnp.bfloat16)
+    return pl.pallas_call(
+        second_kernel if sofar else first_kernel,
         out_shape=(
-            pltpu.HBM(whole, jnp.bfloat16),
-            jax.ShapeDtypeStruct((nvir // 16, nvir // LANES, 4, LANES), jnp.bfloat16),
+            pltpu.HBM((nvir, nvir), jnp.bfloat16),
+            tiles if sofar else lines,
         ),
-        in_specs=[SMEM, SMEM, SMEM, VMEM, VMEM, VMEM],
+        in_specs=[SMEM] + [VMEM] * (2 + len(sofar)),
         out_specs=(ANY, VMEM),
         compiler_params=SMALL,
         scratch_shapes=[
             pltpu.VMEM((nvir, nvir), jnp.float32),
-            pltpu.VMEM(whole, jnp.bfloat16),
+            pltpu.VMEM((nvir, nvir), jnp.bfloat16),
             pltpu.SemaphoreType.DMA,
         ],
-    )(place, shifts, occ, row, near(pair), near(there))
+    )(place, near(mine), near(there), *sofar)
 
 
 def gamma_kernel(
-    place_ref, shifts_ref, occ_ref, row_ref, pair_ref, there_ref, mixed_ref, ahead_ref,
-    behind_ref, gamma_ref, amp_ref, first_ref, block_ref, sems,
-):
-    noff = pair_ref.shape[0]
+    place_ref, mine_ref, there_ref, first_ref, second_ref, ahead_ref, behind_ref, gamma_ref,
+    amp_ref, held_ref, block_ref, sems,
+):
+    noff = mine_ref.shape[0]
     copies = [
-        pltpu.make_async_copy(mixed_ref, first_ref, sems.at[0]),
-        pltpu.make_async_copy(ahead_ref, block_ref.at[pl.ds(0, noff)], sems.at[1]),
-        pltpu.make_async_copy(behind_ref, block_ref.at[pl.ds(noff, noff)], sems.at[2]),
+        pltpu.make_async_copy(first_ref, held_ref.at[0], sems.at[0]),
+        pltpu.make_async_copy(second_ref, held_ref.at[1], sems.at[1]),
+        pltpu.make_async_copy(ahead_ref, block_ref.at[pl.ds(0, noff)], sems.at[2]),
+        pltpu.make_async_copy(behind_ref, block_ref.at[pl.ds(noff, noff)], sems.at[3]),
     ]
     for copy in copies:
         copy.start()
     for k in range(noff):
-        amp = amplitude(
-            place_ref, shifts_ref[noff + k], occ_ref, row_ref, pair_ref[k], there_ref[k],
-            amp_ref,
-        )
-        mixed = (2.0 * amp - amp.T).astype(block_ref.dtype)
+        mixed = mixed_of(whole_of(place_ref, mine_ref[k], there_ref[k], amp_ref))
         if k == 0:
             for copy in copies:
                 copy.wait()
         part = jnp.dot(mixed, block_ref[noff + k], preferred_element_type=jnp.float32)
-        part += jnp.dot(first_ref[k], block_ref[k], preferred_element_type=jnp.float32)
+        part += jnp.dot(held_ref[k], block_ref[k], preferred_element_type=jnp.float32)
         gamma_ref[...] = part if k == 0 else gamma_ref[...] + part
 
 
-def gamma_of(place, shifts, occ, row, pair, there, mixed, ahead, behind):
+def gamma_of(place, mine, there, first, second, ahead, behind):
     noff, nvir, wide = ahead.shape
     return pl.pallas_call(
         gamma_kernel,
         out_shape=jax.ShapeDtypeStruct((nvir, wide), jnp.float32),
-        in_specs=[SMEM, SMEM, SMEM, VMEM, VMEM, VMEM, ANY, ANY, ANY],
+        in_specs=[SMEM, VMEM, VMEM, ANY, ANY, ANY, ANY],
         out_specs=VMEM,
         compiler_params=SMALL,
         scratch_shapes=[
             pltpu.VMEM((nvir, nvir), jnp.float32),
-            pltpu.VMEM(mixed.shape, mixed.dtype),
+            pltpu.VMEM((noff, nvir, nvir), first.dtype),
             pltpu.VMEM((2 * noff, nvir, wide), ahead.dtype),
-            pltpu.SemaphoreType.DMA((3,)),
+            pltpu.SemaphoreType.DMA((4,)),
         ],
-    )(place, shifts, occ, row, pair, there, far(mixed), far(ahead), far(behind))
+    )(place, mine, there, far(first), far(second), far(ahead), far(behind))
 
 
 def lines_kernel(tiles_ref, out_ref):
@@ -255,19 +289,23 @@
     came = swap(sent, "core")
     total = kept + came
     sent = total.astype(jnp.bfloat16)
-    came = swap(sent, "zl")
-    pair = total + came.astype(jnp.float32)
-    there = swap(pair, "core")
-    mixed, density = ahead_pairs(place, shifts, occ_energy, row, pair, there)
+    came = swap(sent[:1], "zl")
+    later = swap(sent[1:], "zl")
+    amp = half_amplitudes(0, place, shifts, occ_energy, row, total, came)
+    there = swap(amp, "core")
+    first, density = mix(place, amp, there)
+    amp = half_amplitudes(1, place, shifts, occ_energy, row, total, later)
+    there = swap(amp, "core")
+    second, density = mix(place, amp, there, density)
 
     behind, kept, sent = partials(1, place, own, got)
     came = swap(sent, "core")
     back = kept + came
     sent = back.astype(jnp.bfloat16)
     came = swap(sent, "zl")
-    pair = back + came.astype(jnp.float32)
-    there = swap(pair, "core")
-    gamma = gamma_of(place, shifts, occ_energy, row, pair, there, mixed, ahead, behind)
+    amp = half_amplitudes(2, place, shifts, occ_energy, row, back, came)
+    there = swap(amp, "core")
+    gamma = gamma_of(place, amp, there, first, second, ahead, behind)
 
     came = exchange(density.reshape(count, -1, LANES), OCC)
     summed = jnp.sum(came.astype(jnp.float32), axis=0).astype(jnp.bfloat16)

time: 190 us -> 196 us (1.032)
  the two profiles are of different devices: /device:TPU:8 before, /device:TPU:1 now
where the time goes in v5:
time: 196 us; the launch traced here: 195 us
  waiting for transfers between devices  78.9 us (40%)
  starting transfers between devices  55.5 us (28%)
  blocking collectives  39.4 us (20%)
  Pallas kernels  17.8 us (9%)
  other arithmetic  2.12 us (1%)
    all_to_all x2, waiting for transfers between devices, exchange(): return lax.all_to_all(value, axis, split_axis=0, concat_axis=0, tiled=True)  71.6 us
    all_to_all x2, blocking collectives, exchange(): return lax.all_to_all(value, axis, split_axis=0, concat_axis=0, tiled=True)  39.4 us
    all_to_all x2, starting transfers between devices, exchange(): return lax.all_to_all(value, axis, split_axis=0, concat_axis=0, tiled=True)  28.5 us
    ppermute x8, starting transfers between devices, swap(): return lax.ppermute(value, axis, [(0, 1), (1, 0)])  27.1 us
    ppermute x8, waiting for transfers between devices, swap(): return lax.ppermute(value, axis, [(0, 1), (1, 0)])  7.28 us
    pallas_call x1, Pallas kernels, gamma_of(): pl.pallas_call(gamma_kernel, out_shape=jax.ShapeDtypeStruct((nvir, wide),...  4.73 us
    pallas_call x2, Pallas kernels, partials(): pl.pallas_call(functools.partial(partial_kernel, group), out_shape=(pltpu...  4.31 us
  transfers between devices with their start and end apart: 10, of which 5 were waited for; matrix products, arithmetic and copies ran while one was open for 1% of the time, Pallas kernels for 5%

profile of v5, /device:TPU:1, one launch (start us, length us, event | category | flops | bytes accessed | tf_op | source)
XLA Modules:
  0.0 194.9 jit_solution(3912189567997655028)
XLA Ops:
  0.6 20.8 %all-to-all-start = ((bf16[128,16,128]{2,1,0:T(8,128)(2,1)}), bf16[128,16,128]{2,1,0:T(8,128)(2,1)S(1)}, u32[]{:S(2)}, u32[]{:S(2)}) async-start(bf16[128,16,128]{2,1,0:T(8,128)(2,1)} %bitcast.16), calls=%async_computation | async-start | bytes 1048576 | tf_op jit(solution)/shard_map/all_to_all | solution.py:30
  22.8 18.6 %all-to-all-done.held_ref = bf16[128,16,128]{2,1,0:T(8,128)(2,1)S(1)} async-done(((bf16[128,16,128]{2,1,0:T(8,128)(2,1)}), bf16[128,16,128]{2,1,0:T(8,128)(2,1)S(1)}, u32[]{:S(2)}, u32[]{:S(2)}) %all-to-all-start) | async-done | bytes 524320 | tf_op jit(solution)/shard_map/all_to_all | solution.py:30
  41.5 2.1 %shard_map.59 = bf16[128,64,128]{2,1,0:T(8,128)(2,1)} custom-call(s32[4]{0:T(128)S(1)} %pad_add_fusion.1.starts_ref.shifts_ref, bf16[128,16,128]{2,1,0:T(8,128)(2,1)S(1)} %all-to-all-done.held_ref), custom_call_target="tpu_custom_call" | custom-call | tf_op jit(solution)/shard_map/pallas_call | solution.py:70
  43.6 7.6 %all-to-all-start.1 = ((bf16[128,64,128]{2,1,0:T(8,128)(2,1)}), bf16[128,64,128]{2,1,0:T(8,128)(2,1)S(1)}, u32[]{:S(2)}, u32[]{:S(2)}) async-start(bf16[128,64,128]{2,1,0:T(8,128)(2,1)} %shard_map.59), calls=%async_computation.1 | async-start | bytes 4194304 | tf_op jit(solution)/shard_map/all_to_all | solution.py:30
  51.3 53.0 %all-to-all-done.1 = bf16[128,64,128]{2,1,0:T(8,128)(2,1)S(1)} async-done(((bf16[128,64,128]{2,1,0:T(8,128)(2,1)}), bf16[128,64,128]{2,1,0:T(8,128)(2,1)S(1)}, u32[]{:S(2)}, u32[]{:S(2)}) %all-to-all-start.1) | async-done | bytes 2097184 | tf_op jit(solution)/shard_map/all_to_all | solution.py:30
  104.3 2.1 %shard_map.60 = (bf16[2,512,512]{2,1,0:T(8,128)(2,1)}, f32[2,256,512]{2,1,0:T(8,128)S(1)}, f32[2,256,512]{2,1,0:T(8,128)S(1)}) custom-call(s32[3]{0:T(128)S(1)} %pad_add_fusion.place_ref, bf16[512,512]{1,0:T(8,128)(2,1)S(1)} %bitcast.17, bf16[64,2,64,128]{3,2,1,0:T(8,128)(2,1)S(1)} %bitcast.14), custom_call_target="tpu_custom_call" | custom-call | tf_op jit(solution)/shard_map/pallas_call | solution.py:109
  106.5 5.1 %collective-permute-start = (f32[2,256,512]{2,1,0:T(8,128)S(1)}, f32[2,256,512]{2,1,0:T(8,128)S(1)}, u32[]{:S(2)}, u32[]{:S(2)}) collective-permute-start(f32[2,256,512]{2,1,0:T(8,128)S(1)} %get-tuple-element.13), channel_id=1, source_target_pairs={{0,1},{1,0},{2,3},{3,2},{4,5},{5,4},{6,7},{7,6},{8,9},{9,8},{10,11... | collective-permute-start | bytes 3145736 | tf_op jit(solution)/shard_map/ppermute | solution.py:34
  111.6 2.2 %shard_map.62 = (bf16[2,512,512]{2,1,0:T(8,128)(2,1)}, f32[2,256,512]{2,1,0:T(8,128)S(1)}, f32[2,256,512]{2,1,0:T(8,128)S(1)}) custom-call(s32[3]{0:T(128)S(1)} %pad_add_fusion.place_ref, bf16[512,512]{1,0:T(8,128)(2,1)S(1)} %bitcast.18, bf16[64,2,64,128]{3,2,1,0:T(8,128)(2,1)S(1)} %bitcast.15), custom_call_target="tpu_custom_call" | custom-call | tf_op jit(solution)/shard_map/pallas_call | solution.py:109
  113.7 1.9 collective-permute-start.3
  115.9 3.1 %collective-permute-start.1 = (bf16[2,256,512]{2,1,0:T(8,128)(2,1)S(1)}, bf16[2,256,512]{2,1,0:T(8,128)(2,1)S(1)}, u32[]{:S(2)}, u32[]{:S(2)}) collective-permute-start(bf16[2,256,512]{2,1,0:T(8,128)(2,1)S(1)} %get-tuple-element.24), channel_id=1, source_target_pairs={{0,2},{2,0},{1,3},{3,1},{4,6},{6,4},{5,7},{7,5},{8,10},{10,8},{9,1... | collective-permute-start | bytes 1572872 | tf_op jit(solution)/shard_map/ppermute | solution.py:34
  119.4 2.3 %collective-permute-start.4 = (bf16[1,256,512]{2,1,0:T(8,128)(2,1)S(1)}, bf16[1,256,512]{2,1,0:T(8,128)(2,1)S(1)}, u32[]{:S(2)}, u32[]{:S(2)}) collective-permute-start(bf16[1,256,512]{2,1,0:T(8,128)(2,1)S(1)} %get-tuple-element.27), channel_id=1, source_target_pairs={{0,2},{2,0},{1,3},{3,1},{4,6},{6,4},{5,7},{7,5},{8,10},{10,8},{9,1... | collective-permute-start | bytes 786440 | tf_op jit(solution)/shard_map/ppermute | solution.py:34
  121.7 3.0 %collective-permute-start.6 = (bf16[1,256,512]{2,1,0:T(8,128)(2,1)S(1)}, bf16[1,256,512]{2,1,0:T(8,128)(2,1)S(1)}, u32[]{:S(2)}, u32[]{:S(2)}) collective-permute-start(bf16[1,256,512]{2,1,0:T(8,128)(2,1)S(1)} %get-tuple-element.26), channel_id=1, source_target_pairs={{0,2},{2,0},{1,3},{3,1},{4,6},{6,4},{5,7},{7,5},{8,10},{10,8},{9,1... | collective-permute-start | bytes 786440 | tf_op jit(solution)/shard_map/ppermute | solution.py:34
  124.7 6.1 %collective-permute-done.1.came_ref = bf16[2,256,512]{2,1,0:T(8,128)(2,1)S(1)} collective-permute-done((bf16[2,256,512]{2,1,0:T(8,128)(2,1)S(1)}, bf16[2,256,512]{2,1,0:T(8,128)(2,1)S(1)}, u32[]{:S(2)}, u32[]{:S(2)}) %collective-permute-start.1) | collective-permute-done | bytes 524320 | tf_op jit(solution)/shard_map/ppermute | solution.py:34
  130.8 0.9 shard_map.61.mine_ref
  131.7 4.2 %collective-permute-start.2 = (f32[2,256,512]{2,1,0:T(8,128)S(1)}, f32[2,256,512]{2,1,0:T(8,128)S(1)}, u32[]{:S(2)}, u32[]{:S(2)}) collective-permute-start(f32[2,256,512]{2,1,0:T(8,128)S(1)} %shard_map.61.mine_ref), channel_id=1, source_target_pairs={{0,1},{1,0},{2,3},{3,2},{4,5},{5,4},{6,7},{7,6},{8,9},{9,8},{10,11... | collective-permute-start | bytes 3145736 | tf_op jit(solution)/shard_map/ppermute | solution.py:34
  136.4 0.8 shard_map.63.mine_ref
  137.2 4.2 %collective-permute-start.5 = (f32[1,256,512]{2,1,0:T(8,128)S(1)}, f32[1,256,512]{2,1,0:T(8,128)S(1)}, u32[]{:S(2)}, u32[]{:S(2)}) collective-permute-start(f32[1,256,512]{2,1,0:T(8,128)S(1)} %shard_map.63.mine_ref), channel_id=1, source_target_pairs={{0,1},{1,0},{2,3},{3,2},{4,5},{5,4},{6,7},{7,6},{8,9},{9,8},{10,11... | collective-permute-start | bytes 1572872 | tf_op jit(solution)/shard_map/ppermute | solution.py:34
  142.0 0.8 shard_map.65.mine_ref
  142.8 3.3 %collective-permute-start.7 = (f32[1,256,512]{2,1,0:T(8,128)S(1)}, f32[1,256,512]{2,1,0:T(8,128)S(1)}, u32[]{:S(2)}, u32[]{:S(2)}) collective-permute-start(f32[1,256,512]{2,1,0:T(8,128)S(1)} %shard_map.65.mine_ref), channel_id=1, source_target_pairs={{0,1},{1,0},{2,3},{3,2},{4,5},{5,4},{6,7},{7,6},{8,9},{9,8},{10,11... | collective-permute-start | bytes 1572872 | tf_op jit(solution)/shard_map/ppermute | solution.py:34
  146.1 1.8 shard_map.64
  147.9 1.8 shard_map.66
  149.7 19.9 %all_to_all.20 = bf16[128,4,128]{2,1,0:T(4,128)(2,1)S(1)} all-to-all(bf16[128,4,128]{2,1,0:T(4,128)(2,1)S(1)} %bitcast.20), channel_id=1, replica_groups=mesh['zh'=4,'x'=4,'y'=8,'zl'=2,'core'=2] {'zh','x','y'}, dimensions={0} | all-to-all | bytes 262144 | tf_op jit(solution)/shard_map/all_to_all | solution.py:30
  169.8 19.5 %all_to_all.21 = bf16[128,4,128]{2,1,0:T(4,128)(2,1)S(1)} all-to-all(bf16[128,4,128]{2,1,0:T(4,128)(2,1)S(1)} %broadcast_in_dim.11), channel_id=1, replica_groups=mesh['zh'=4,'x'=4,'y'=8,'zl'=2,'core'=2] {'zh','x','y'}, dimensions={0} | all-to-all | bytes 262144 | tf_op jit(solution)/shard_map/all_to_all | solution.py:30
  190.0 4.7 %shard_map.67 = f32[512,512]{1,0:T(8,128)} custom-call(s32[3]{0:T(128)S(1)} %pad_add_fusion.place_ref, f32[2,256,512]{2,1,0:T(8,128)S(1)} %shard_map.61.mine_ref, f32[2,256,512]{2,1,0:T(8,128)S(1)} %collective-permute-done.2.there_ref, bf16[512,512]{1,0:T(8,128)(2,1)} %get-tuple-element.16.first_ref, bf16[512,512]{1,0:T(8,128)(2,1)} %get-tuple-element.18.second_ref, ...), custom_call_target="tpu_custom_call" | custom-call | tf_op jit(solution)/shard_map/pallas_call | solution.py:242
  (22 shorter events, 4.1 us)
Async XLA Ops:
  0.6 40.8 %all-to-all-start = ((bf16[128,16,128]{2,1,0:T(8,128)(2,1)}), bf16[128,16,128]{2,1,0:T(8,128)(2,1)S(1)}, u32[]{:S(2)}, u32[]{:S(2)}) async-start(bf16[128,16,128]{2,1,0:T(8,128)(2,1)} %bitcast.16), calls=%async_computation | async-start | bytes 1048576 | tf_op jit(solution)/shard_map/all_to_all | solution.py:30
  43.6 60.8 %copy-start = (bf16[1,512,512]{2,1,0:T(8,128)(2,1)S(1)}, bf16[1,512,512]{2,1,0:T(8,128)(2,1)}, u32[]{:S(2)}) copy-start(bf16[1,512,512]{2,1,0:T(8,128)(2,1)} %param.4) | copy-start | bytes 1572868
  43.6 60.8 %all-to-all-start.1 = ((bf16[128,64,128]{2,1,0:T(8,128)(2,1)}), bf16[128,64,128]{2,1,0:T(8,128)(2,1)S(1)}, u32[]{:S(2)}, u32[]{:S(2)}) async-start(bf16[128,64,128]{2,1,0:T(8,128)(2,1)} %shard_map.59), calls=%async_computation.1 | async-start | bytes 4194304 | tf_op jit(solution)/shard_map/all_to_all | solution.py:30
  106.5 9.2 %collective-permute-start = (f32[2,256,512]{2,1,0:T(8,128)S(1)}, f32[2,256,512]{2,1,0:T(8,128)S(1)}, u32[]{:S(2)}, u32[]{:S(2)}) collective-permute-start(f32[2,256,512]{2,1,0:T(8,128)S(1)} %get-tuple-element.13), channel_id=1, source_target_pairs={{0,1},{1,0},{2,3},{3,2},{4,5},{5,4},{6,7},{7,6},{8,9},{9,8},{10,11... | collective-permute-start | bytes 3145736 | tf_op jit(solution)/shard_map/ppermute | solution.py:34
  113.7 5.3 %collective-permute-start.3 = (f32[2,256,512]{2,1,0:T(8,128)S(1)}, f32[2,256,512]{2,1,0:T(8,128)S(1)}, u32[]{:S(2)}, u32[]{:S(2)}) collective-permute-start(f32[2,256,512]{2,1,0:T(8,128)S(1)} %get-tuple-element.15), channel_id=1, source_target_pairs={{0,1},{1,0},{2,3},{3,2},{4,5},{5,4},{6,7},{7,6},{8,9},{9,8},{10,11... | collective-permute-start | bytes 3145736 | tf_op jit(solution)/shard_map/ppermute | solution.py:34
  115.9 14.9 %collective-permute-start.1 = (bf16[2,256,512]{2,1,0:T(8,128)(2,1)S(1)}, bf16[2,256,512]{2,1,0:T(8,128)(2,1)S(1)}, u32[]{:S(2)}, u32[]{:S(2)}) collective-permute-start(bf16[2,256,512]{2,1,0:T(8,128)(2,1)S(1)} %get-tuple-element.24), channel_id=1, source_target_pairs={{0,2},{2,0},{1,3},{3,1},{4,6},{6,4},{5,7},{7,5},{8,10},{10,8},{9,1... | collective-permute-start | bytes 1572872 | tf_op jit(solution)/shard_map/ppermute | solution.py:34
  119.1 11.8 %copy-start.1 = (f32[512]{0:T(512)S(1)}, f32[512]{0:T(512)}, u32[]{:S(2)}) copy-start(f32[512]{0:T(512)} %param.7) | copy-start | bytes 6148
  119.1 11.7 %copy-start.2 = (f32[128]{0:T(128)S(1)}, f32[128]{0:T(128)}, u32[]{:S(2)}) copy-start(f32[128]{0:T(128)} %occ_ref.5) | copy-start | bytes 1540
  119.4 17.0 %collective-permute-start.4 = (bf16[1,256,512]{2,1,0:T(8,128)(2,1)S(1)}, bf16[1,256,512]{2,1,0:T(8,128)(2,1)S(1)}, u32[]{:S(2)}, u32[]{:S(2)}) collective-permute-start(bf16[1,256,512]{2,1,0:T(8,128)(2,1)S(1)} %get-tuple-element.27), channel_id=1, source_target_pairs={{0,2},{2,0},{1,3},{3,1},{4,6},{6,4},{5,7},{7,5},{8,10},{10,8},{9,1... | collective-permute-start | bytes 786440 | tf_op jit(solution)/shard_map/ppermute | solution.py:34
  121.7 20.3 %collective-permute-start.6 = (bf16[1,256,512]{2,1,0:T(8,128)(2,1)S(1)}, bf16[1,256,512]{2,1,0:T(8,128)(2,1)S(1)}, u32[]{:S(2)}, u32[]{:S(2)}) collective-permute-start(bf16[1,256,512]{2,1,0:T(8,128)(2,1)S(1)} %get-tuple-element.26), channel_id=1, source_target_pairs={{0,2},{2,0},{1,3},{3,1},{4,6},{6,4},{5,7},{7,5},{8,10},{10,8},{9,1... | collective-permute-start | bytes 786440 | tf_op jit(solution)/shard_map/ppermute | solution.py:34
  131.7 58.3 %collective-permute-start.2 = (f32[2,256,512]{2,1,0:T(8,128)S(1)}, f32[2,256,512]{2,1,0:T(8,128)S(1)}, u32[]{:S(2)}, u32[]{:S(2)}) collective-permute-start(f32[2,256,512]{2,1,0:T(8,128)S(1)} %shard_map.61.mine_ref), channel_id=1, source_target_pairs={{0,1},{1,0},{2,3},{3,2},{4,5},{5,4},{6,7},{7,6},{8,9},{9,8},{10,11... | collective-permute-start | bytes 3145736 | tf_op jit(solution)/shard_map/ppermute | solution.py:34
  137.2 8.9 %collective-permute-start.5 = (f32[1,256,512]{2,1,0:T(8,128)S(1)}, f32[1,256,512]{2,1,0:T(8,128)S(1)}, u32[]{:S(2)}, u32[]{:S(2)}) collective-permute-start(f32[1,256,512]{2,1,0:T(8,128)S(1)} %shard_map.63.mine_ref), channel_id=1, source_target_pairs={{0,1},{1,0},{2,3},{3,2},{4,5},{5,4},{6,7},{7,6},{8,9},{9,8},{10,11... | collective-permute-start | bytes 1572872 | tf_op jit(solution)/shard_map/ppermute | solution.py:34
  142.8 5.1 %collective-permute-start.7 = (f32[1,256,512]{2,1,0:T(8,128)S(1)}, f32[1,256,512]{2,1,0:T(8,128)S(1)}, u32[]{:S(2)}, u32[]{:S(2)}) collective-permute-start(f32[1,256,512]{2,1,0:T(8,128)S(1)} %shard_map.65.mine_ref), channel_id=1, source_target_pairs={{0,1},{1,0},{2,3},{3,2},{4,5},{5,4},{6,7},{7,6},{8,9},{9,8},{10,11... | collective-permute-start | bytes 1572872 | tf_op jit(solution)/shard_map/ppermute | solution.py:34

commit v6 on v4

--- a/solution.py
+++ b/solution.py
@@ -9,6 +9,7 @@
 from jax.sharding import PartitionSpec as P
 
 OCC = ("zh", "x", "y")
+PLANE = ("x", "y")
 ROW = 8
 SUB = 16
 LANES = 128
@@ -221,14 +222,16 @@
 
 
 def lines_kernel(tiles_ref, out_ref):
-    groups, cols, deep, lanes = tiles_ref.shape
+    parts, groups, cols, deep, lanes = tiles_ref.shape
     for c in range(cols):
-        tile = tiles_ref[:, c].astype(out_ref.dtype)
-        out_ref[:, c * lanes : (c + 1) * lanes] = tile.reshape(groups * deep, lanes)
+        total = tiles_ref[0, :, c].astype(out_ref.dtype)
+        for p in range(1, parts):
+            total += tiles_ref[p, :, c].astype(out_ref.dtype)
+        out_ref[:, c * lanes : (c + 1) * lanes] = total.reshape(groups * deep, lanes)
 
 
 def to_lines(tiles):
-    groups, cols, deep, lanes = tiles.shape
+    _, groups, cols, deep, lanes = tiles.shape
     return pl.pallas_call(
         lines_kernel,
         out_shape=jax.ShapeDtypeStruct((groups * deep, cols * lanes), jnp.float32),
@@ -269,11 +272,11 @@
     there = swap(pair, "core")
     gamma = gamma_of(place, shifts, occ_energy, row, pair, there, mixed, ahead, behind)
 
-    came = exchange(density.reshape(count, -1, LANES), OCC)
+    came = exchange(density, PLANE)
     summed = jnp.sum(came.astype(jnp.float32), axis=0).astype(jnp.bfloat16)
     sent = jnp.broadcast_to(summed, (count, *summed.shape))
     came = exchange(sent, OCC)
-    return (gamma[None], to_lines(came.reshape(density.shape)))
+    return (gamma[None], to_lines(came.reshape(-1, *density.shape)))
 
 
 def solution(mesh):

time: 190 us -> 185 us (0.974)
  blocking collectives: 22 us -> 0 us
  waiting for transfers between devices: 101 us -> 110 us
  starting transfers between devices: 47.5 us -> 54.2 us
    all_to_all x1 -> x0, blocking collectives: 22 us -> none  [exchange(): return lax.all_to_all(value, axis, split_axis=0, concat_axis=0, tiled=True)]
    all_to_all x3 -> x4, waiting for transfers between devices: 82.5 us -> 93.3 us  [exchange(): return lax.all_to_all(value, axis, split_axis=0, concat_axis=0, tiled=True)]
    all_to_all x3 -> x4, starting transfers between devices: 33.5 us -> 39.2 us  [exchange(): return lax.all_to_all(value, axis, split_axis=0, concat_axis=0, tiled=True)]
    ppermute x6, waiting for transfers between devices: 18.7 us -> 16.7 us  [swap(): return lax.ppermute(value, axis, [(0, 1), (1, 0)])]
  transfers between devices with their start and end apart: 9 -> 10, of which waited for: 5 -> 6; matrix products, arithmetic and copies ran while one was open for 2% -> 2% of each run, Pallas kernels for 5% -> 6%
where the time goes in v6:
time: 185 us; the launch traced here: 184 us
  waiting for transfers between devices  110 us (59%)
  starting transfers between devices  54.2 us (29%)
  Pallas kernels  15.6 us (8%)
  other arithmetic  2.43 us (1%)
    all_to_all x4, waiting for transfers between devices, exchange(): return lax.all_to_all(value, axis, split_axis=0, concat_axis=0, tiled=True)  93.3 us
    all_to_all x4, starting transfers between devices, exchange(): return lax.all_to_all(value, axis, split_axis=0, concat_axis=0, tiled=True)  39.2 us
    ppermute x6, waiting for transfers between devices, swap(): return lax.ppermute(value, axis, [(0, 1), (1, 0)])  16.7 us
    ppermute x6, starting transfers between devices, swap(): return lax.ppermute(value, axis, [(0, 1), (1, 0)])  14.9 us
    pallas_call x1, Pallas kernels, gamma_of(): pl.pallas_call(gamma_kernel, out_shape=jax.ShapeDtypeStruct((nvir, wide),...  4.95 us
    pallas_call x2, Pallas kernels, partials(): pl.pallas_call(functools.partial(partial_kernel, group), out_shape=(pltpu...  4.32 us
  transfers between devices with their start and end apart: 10, of which 6 were waited for; matrix products, arithmetic and copies ran while one was open for 2% of the time, Pallas kernels for 6%

profile of v6, /device:TPU:8, one launch (start us, length us, event | category | flops | bytes accessed | tf_op | source)
XLA Modules:
  0.0 184.1 jit_solution(4656373371949885579)
XLA Ops:
  0.6 19.8 %all-to-all-start = ((bf16[128,16,128]{2,1,0:T(8,128)(2,1)}), bf16[128,16,128]{2,1,0:T(8,128)(2,1)S(1)}, u32[]{:S(2)}, u32[]{:S(2)}) async-start(bf16[128,16,128]{2,1,0:T(8,128)(2,1)} %bitcast.15), calls=%async_computation | async-start | bytes 1048576 | tf_op jit(solution)/shard_map/all_to_all | solution.py:31
  21.1 0.7 pad_add_fusion.1.starts_ref.shifts_ref
  21.9 19.7 %all-to-all-done.held_ref = bf16[128,16,128]{2,1,0:T(8,128)(2,1)S(1)} async-done(((bf16[128,16,128]{2,1,0:T(8,128)(2,1)}), bf16[128,16,128]{2,1,0:T(8,128)(2,1)S(1)}, u32[]{:S(2)}, u32[]{:S(2)}) %all-to-all-start) | async-done | bytes 524320 | tf_op jit(solution)/shard_map/all_to_all | solution.py:31
  41.5 2.1 %shard_map.59 = bf16[128,64,128]{2,1,0:T(8,128)(2,1)} custom-call(s32[4]{0:T(128)S(1)} %pad_add_fusion.1.starts_ref.shifts_ref, bf16[128,16,128]{2,1,0:T(8,128)(2,1)S(1)} %all-to-all-done.held_ref), custom_call_target="tpu_custom_call" | custom-call | tf_op jit(solution)/shard_map/pallas_call | solution.py:71
  43.6 7.3 %all-to-all-start.1 = ((bf16[128,64,128]{2,1,0:T(8,128)(2,1)}), bf16[128,64,128]{2,1,0:T(8,128)(2,1)S(1)}, u32[]{:S(2)}, u32[]{:S(2)}) async-start(bf16[128,64,128]{2,1,0:T(8,128)(2,1)} %shard_map.59), calls=%async_computation.1 | async-start | bytes 4194304 | tf_op jit(solution)/shard_map/all_to_all | solution.py:31
  51.0 54.1 %all-to-all-done.1 = bf16[128,64,128]{2,1,0:T(8,128)(2,1)S(1)} async-done(((bf16[128,64,128]{2,1,0:T(8,128)(2,1)}), bf16[128,64,128]{2,1,0:T(8,128)(2,1)S(1)}, u32[]{:S(2)}, u32[]{:S(2)}) %all-to-all-start.1) | async-done | bytes 2097184 | tf_op jit(solution)/shard_map/all_to_all | solution.py:31
  105.2 2.2 %shard_map.61 = (bf16[2,512,512]{2,1,0:T(8,128)(2,1)}, f32[2,256,512]{2,1,0:T(8,128)S(1)}, f32[2,256,512]{2,1,0:T(8,128)S(1)}) custom-call(s32[3]{0:T(128)S(1)} %pad_add_fusion.place_ref, bf16[512,512]{1,0:T(8,128)(2,1)S(1)} %bitcast.16, bf16[64,2,64,128]{3,2,1,0:T(8,128)(2,1)S(1)} %bitcast.13), custom_call_target="tpu_custom_call" | custom-call | tf_op jit(solution)/shard_map/pallas_call | solution.py:110
  107.3 1.9 %collective-permute-start.3 = (f32[2,256,512]{2,1,0:T(8,128)S(1)}, f32[2,256,512]{2,1,0:T(8,128)S(1)}, u32[]{:S(2)}, u32[]{:S(2)}) collective-permute-start(f32[2,256,512]{2,1,0:T(8,128)S(1)} %get-tuple-element.13), channel_id=1, source_target_pairs={{0,1},{1,0},{2,3},{3,2},{4,5},{5,4},{6,7},{7,6},{8,9},{9,8},{10,11... | collective-permute-start | bytes 3145736 | tf_op jit(solution)/shard_map/ppermute | solution.py:35
  109.3 2.2 %shard_map.60 = (bf16[2,512,512]{2,1,0:T(8,128)(2,1)}, f32[2,256,512]{2,1,0:T(8,128)S(1)}, f32[2,256,512]{2,1,0:T(8,128)S(1)}) custom-call(s32[3]{0:T(128)S(1)} %pad_add_fusion.place_ref, bf16[512,512]{1,0:T(8,128)(2,1)S(1)} %bitcast.17, bf16[64,2,64,128]{3,2,1,0:T(8,128)(2,1)S(1)} %bitcast.14), custom_call_target="tpu_custom_call" | custom-call | tf_op jit(solution)/shard_map/pallas_call | solution.py:110
  111.4 2.4 %collective-permute-start = (f32[2,256,512]{2,1,0:T(8,128)S(1)}, f32[2,256,512]{2,1,0:T(8,128)S(1)}, u32[]{:S(2)}, u32[]{:S(2)}) collective-permute-start(f32[2,256,512]{2,1,0:T(8,128)S(1)} %get-tuple-element.11), channel_id=1, source_target_pairs={{0,1},{1,0},{2,3},{3,2},{4,5},{5,4},{6,7},{7,6},{8,9},{9,8},{10,11... | collective-permute-start | bytes 3145736 | tf_op jit(solution)/shard_map/ppermute | solution.py:35
  114.1 3.4 %collective-permute-start.4 = (bf16[2,256,512]{2,1,0:T(8,128)(2,1)S(1)}, bf16[2,256,512]{2,1,0:T(8,128)(2,1)S(1)}, u32[]{:S(2)}, u32[]{:S(2)}) collective-permute-start(bf16[2,256,512]{2,1,0:T(8,128)(2,1)S(1)} %get-tuple-element.18), channel_id=1, source_target_pairs={{0,2},{2,0},{1,3},{3,1},{4,6},{6,4},{5,7},{7,5},{8,10},{10,8},{9,1... | collective-permute-start | bytes 1572872 | tf_op jit(solution)/shard_map/ppermute | solution.py:35
  117.5 12.3 %collective-permute-done.4 = bf16[2,256,512]{2,1,0:T(8,128)(2,1)S(1)} collective-permute-done((bf16[2,256,512]{2,1,0:T(8,128)(2,1)S(1)}, bf16[2,256,512]{2,1,0:T(8,128)(2,1)S(1)}, u32[]{:S(2)}, u32[]{:S(2)}) %collective-permute-start.4) | collective-permute-done | bytes 524320 | tf_op jit(solution)/shard_map/ppermute | solution.py:35
  130.1 1.9 %collective-permute-start.5 = (f32[2,256,512]{2,1,0:T(8,128)S(1)}, f32[2,256,512]{2,1,0:T(8,128)S(1)}, u32[]{:S(2)}, u32[]{:S(2)}) collective-permute-start(f32[2,256,512]{2,1,0:T(8,128)S(1)} %convert_add_fusion.pair_ref), channel_id=1, source_target_pairs={{0,1},{1,0},{2,3},{3,2},{4,5},{5,4},{6,7},{7,6},{8,9},{9,8},{10,11... | collective-permute-start | bytes 3145736 | tf_op jit(solution)/shard_map/ppermute | solution.py:35
  132.3 3.4 %collective-permute-start.1 = (bf16[2,256,512]{2,1,0:T(8,128)(2,1)S(1)}, bf16[2,256,512]{2,1,0:T(8,128)(2,1)S(1)}, u32[]{:S(2)}, u32[]{:S(2)}) collective-permute-start(bf16[2,256,512]{2,1,0:T(8,128)(2,1)S(1)} %get-tuple-element.20), channel_id=1, source_target_pairs={{0,2},{2,0},{1,3},{3,1},{4,6},{6,4},{5,7},{7,5},{8,10},{10,8},{9,1... | collective-permute-start | bytes 1572872 | tf_op jit(solution)/shard_map/ppermute | solution.py:35
  135.7 3.4 %shard_map.62 = (bf16[2,512,512]{2,1,0:T(8,128)(2,1)}, bf16[32,4,4,128]{3,2,1,0:T(4,128)(2,1)}) custom-call(s32[3]{0:T(128)S(1)} %pad_add_fusion.place_ref, s32[4]{0:T(128)S(1)} %pad_add_fusion.1.starts_ref.shifts_ref, f32[128]{0:T(128)S(1)} %copy-done.2, f32[1,512]{1,0:T(1,128)S(1)} %bitcast.19, f32[2,256,512]{2,1,0:T(8,128)S(1)} %convert_add_fusion.pair_ref, ...), custom_call_target="tpu_custom_call" | custom-call | tf_op jit(solution)/shard_map/pallas_call | solution.py:164
  139.1 5.0 %all-to-all-start.2 = ((bf16[32,4,4,128]{3,2,1,0:T(4,128)(2,1)}), bf16[32,4,4,128]{3,2,1,0:T(4,128)(2,1)S(1)}, u32[]{:S(2)}, u32[]{:S(2)}) async-start(bf16[32,4,4,128]{3,2,1,0:T(4,128)(2,1)} %get-tuple-element.17), calls=%async_computation.2 | async-start | bytes 262144 | tf_op jit(solution)/shard_map/all_to_all | solution.py:31
  144.1 4.4 %collective-permute-done.1 = bf16[2,256,512]{2,1,0:T(8,128)(2,1)S(1)} collective-permute-done((bf16[2,256,512]{2,1,0:T(8,128)(2,1)S(1)}, bf16[2,256,512]{2,1,0:T(8,128)(2,1)S(1)}, u32[]{:S(2)}, u32[]{:S(2)}) %collective-permute-start.1) | collective-permute-done | bytes 524320 | tf_op jit(solution)/shard_map/ppermute | solution.py:35
  148.7 1.9 %collective-permute-start.2 = (f32[2,256,512]{2,1,0:T(8,128)S(1)}, f32[2,256,512]{2,1,0:T(8,128)S(1)}, u32[]{:S(2)}, u32[]{:S(2)}) collective-permute-start(f32[2,256,512]{2,1,0:T(8,128)S(1)} %convert_add_fusion.1.pair_ref), channel_id=1, source_target_pairs={{0,1},{1,0},{2,3},{3,2},{4,5},{5,4},{6,7},{7,6},{8,9},{9,8},{10,11... | collective-permute-start | bytes 3145736 | tf_op jit(solution)/shard_map/ppermute | solution.py:35
  150.6 3.8 %all-to-all-done.2 = bf16[32,4,4,128]{3,2,1,0:T(4,128)(2,1)S(1)} async-done(((bf16[32,4,4,128]{3,2,1,0:T(4,128)(2,1)}), bf16[32,4,4,128]{3,2,1,0:T(4,128)(2,1)S(1)}, u32[]{:S(2)}, u32[]{:S(2)}) %all-to-all-start.2) | async-done | bytes 131104 | tf_op jit(solution)/shard_map/all_to_all | solution.py:31
  154.5 0.9 broadcast_in_dim.11
  155.5 7.1 %all-to-all-start.3 = ((bf16[128,4,4,128]{3,2,1,0:T(4,128)(2,1)}), bf16[128,4,4,128]{3,2,1,0:T(4,128)(2,1)S(1)}, u32[]{:S(2)}, u32[]{:S(2)}) async-start(bf16[128,4,4,128]{3,2,1,0:T(4,128)(2,1)} %broadcast_in_dim.11), calls=%async_computation.3 | async-start | bytes 1048576 | tf_op jit(solution)/shard_map/all_to_all | solution.py:31
  162.6 4.9 %shard_map.63 = f32[512,512]{1,0:T(8,128)} custom-call(s32[3]{0:T(128)S(1)} %pad_add_fusion.place_ref, s32[4]{0:T(128)S(1)} %pad_add_fusion.1.starts_ref.shifts_ref, f32[128]{0:T(128)S(1)} %copy-done.2, f32[1,512]{1,0:T(1,128)S(1)} %bitcast.20, f32[2,256,512]{2,1,0:T(8,128)S(1)} %convert_add_fusion.1.pair_ref, ...), custom_call_target="tpu_custom_call" | custom-call | tf_op jit(solution)/shard_map/pallas_call | solution.py:209
  167.5 15.7 %all-to-all-done.3 = bf16[128,4,4,128]{3,2,1,0:T(4,128)(2,1)S(1)} async-done(((bf16[128,4,4,128]{3,2,1,0:T(4,128)(2,1)}), bf16[128,4,4,128]{3,2,1,0:T(4,128)(2,1)S(1)}, u32[]{:S(2)}, u32[]{:S(2)}) %all-to-all-start.3) | async-done | bytes 524320 | tf_op jit(solution)/shard_map/all_to_all | solution.py:31
  183.2 0.8 shard_map.64
  (17 shorter events, 1.7 us)
Async XLA Ops:
  0.6 40.9 %all-to-all-start = ((bf16[128,16,128]{2,1,0:T(8,128)(2,1)}), bf16[128,16,128]{2,1,0:T(8,128)(2,1)S(1)}, u32[]{:S(2)}, u32[]{:S(2)}) async-start(bf16[128,16,128]{2,1,0:T(8,128)(2,1)} %bitcast.15), calls=%async_computation | async-start | bytes 1048576 | tf_op jit(solution)/shard_map/all_to_all | solution.py:31
  43.6 61.5 %copy-start = (bf16[1,512,512]{2,1,0:T(8,128)(2,1)S(1)}, bf16[1,512,512]{2,1,0:T(8,128)(2,1)}, u32[]{:S(2)}) copy-start(bf16[1,512,512]{2,1,0:T(8,128)(2,1)} %param.4) | copy-start | bytes 1572868
  43.6 61.5 %all-to-all-start.1 = ((bf16[128,64,128]{2,1,0:T(8,128)(2,1)}), bf16[128,64,128]{2,1,0:T(8,128)(2,1)S(1)}, u32[]{:S(2)}, u32[]{:S(2)}) async-start(bf16[128,64,128]{2,1,0:T(8,128)(2,1)} %shard_map.59), calls=%async_computation.1 | async-start | bytes 4194304 | tf_op jit(solution)/shard_map/all_to_all | solution.py:31
  107.3 6.5 %collective-permute-start.3 = (f32[2,256,512]{2,1,0:T(8,128)S(1)}, f32[2,256,512]{2,1,0:T(8,128)S(1)}, u32[]{:S(2)}, u32[]{:S(2)}) collective-permute-start(f32[2,256,512]{2,1,0:T(8,128)S(1)} %get-tuple-element.13), channel_id=1, source_target_pairs={{0,1},{1,0},{2,3},{3,2},{4,5},{5,4},{6,7},{7,6},{8,9},{9,8},{10,11... | collective-permute-start | bytes 3145736 | tf_op jit(solution)/shard_map/ppermute | solution.py:35
  111.4 20.6 %collective-permute-start = (f32[2,256,512]{2,1,0:T(8,128)S(1)}, f32[2,256,512]{2,1,0:T(8,128)S(1)}, u32[]{:S(2)}, u32[]{:S(2)}) collective-permute-start(f32[2,256,512]{2,1,0:T(8,128)S(1)} %get-tuple-element.11), channel_id=1, source_target_pairs={{0,1},{1,0},{2,3},{3,2},{4,5},{5,4},{6,7},{7,6},{8,9},{9,8},{10,11... | collective-permute-start | bytes 3145736 | tf_op jit(solution)/shard_map/ppermute | solution.py:35
  114.1 15.7 %collective-permute-start.4 = (bf16[2,256,512]{2,1,0:T(8,128)(2,1)S(1)}, bf16[2,256,512]{2,1,0:T(8,128)(2,1)S(1)}, u32[]{:S(2)}, u32[]{:S(2)}) collective-permute-start(bf16[2,256,512]{2,1,0:T(8,128)(2,1)S(1)} %get-tuple-element.18), channel_id=1, source_target_pairs={{0,2},{2,0},{1,3},{3,1},{4,6},{6,4},{5,7},{7,5},{8,10},{10,8},{9,1... | collective-permute-start | bytes 1572872 | tf_op jit(solution)/shard_map/ppermute | solution.py:35
  130.0 5.6 %copy-start.1 = (f32[512]{0:T(512)S(1)}, f32[512]{0:T(512)}, u32[]{:S(2)}) copy-start(f32[512]{0:T(512)} %param.7) | copy-start | bytes 6148
  130.0 5.6 %copy-start.2 = (f32[128]{0:T(128)S(1)}, f32[128]{0:T(128)}, u32[]{:S(2)}) copy-start(f32[128]{0:T(128)} %occ_ref.3) | copy-start | bytes 1540
  130.1 5.6 %collective-permute-start.5 = (f32[2,256,512]{2,1,0:T(8,128)S(1)}, f32[2,256,512]{2,1,0:T(8,128)S(1)}, u32[]{:S(2)}, u32[]{:S(2)}) collective-permute-start(f32[2,256,512]{2,1,0:T(8,128)S(1)} %convert_add_fusion.pair_ref), channel_id=1, source_target_pairs={{0,1},{1,0},{2,3},{3,2},{4,5},{5,4},{6,7},{7,6},{8,9},{9,8},{10,11... | collective-permute-start | bytes 3145736 | tf_op jit(solution)/shard_map/ppermute | solution.py:35
  132.3 16.2 %collective-permute-start.1 = (bf16[2,256,512]{2,1,0:T(8,128)(2,1)S(1)}, bf16[2,256,512]{2,1,0:T(8,128)(2,1)S(1)}, u32[]{:S(2)}, u32[]{:S(2)}) collective-permute-start(bf16[2,256,512]{2,1,0:T(8,128)(2,1)S(1)} %get-tuple-element.20), channel_id=1, source_target_pairs={{0,2},{2,0},{1,3},{3,1},{4,6},{6,4},{5,7},{7,5},{8,10},{10,8},{9,1... | collective-permute-start | bytes 1572872 | tf_op jit(solution)/shard_map/ppermute | solution.py:35
  139.1 15.3 %all-to-all-start.2 = ((bf16[32,4,4,128]{3,2,1,0:T(4,128)(2,1)}), bf16[32,4,4,128]{3,2,1,0:T(4,128)(2,1)S(1)}, u32[]{:S(2)}, u32[]{:S(2)}) async-start(bf16[32,4,4,128]{3,2,1,0:T(4,128)(2,1)} %get-tuple-element.17), calls=%async_computation.2 | async-start | bytes 262144 | tf_op jit(solution)/shard_map/all_to_all | solution.py:31
  148.7 13.9 %collective-permute-start.2 = (f32[2,256,512]{2,1,0:T(8,128)S(1)}, f32[2,256,512]{2,1,0:T(8,128)S(1)}, u32[]{:S(2)}, u32[]{:S(2)}) collective-permute-start(f32[2,256,512]{2,1,0:T(8,128)S(1)} %convert_add_fusion.1.pair_ref), channel_id=1, source_target_pairs={{0,1},{1,0},{2,3},{3,2},{4,5},{5,4},{6,7},{7,6},{8,9},{9,8},{10,11... | collective-permute-start | bytes 3145736 | tf_op jit(solution)/shard_map/ppermute | solution.py:35
  155.5 27.8 %all-to-all-start.3 = ((bf16[128,4,4,128]{3,2,1,0:T(4,128)(2,1)}), bf16[128,4,4,128]{3,2,1,0:T(4,128)(2,1)S(1)}, u32[]{:S(2)}, u32[]{:S(2)}) async-start(bf16[128,4,4,128]{3,2,1,0:T(4,128)(2,1)} %broadcast_in_dim.11), calls=%async_computation.3 | async-start | bytes 1048576 | tf_op jit(solution)/shard_map/all_to_all | solution.py:31
